TPU v7x, 32 devices: a whole 2x2x4 slice. The times are simulated.
32 devices in a mesh: seq: 4 (over z), ctx: 8 (over y, x, core).
Axes of the slice: x: 2, y: 2, z: 4, core: 2. Of those that a mesh axis runs over, the one named last changes fastest.
Arguments:
- hidden_states: bfloat16 [4, 1024, 1024], P('seq', 'ctx'), may hold values from -6 to 6
- positions: int32 [4, 1024], P('seq'), may hold values from 0 to 1023, as said below
- gain_first: bfloat16 [1024], P(('seq', 'ctx')), may hold values from 0.25 to 1.75
- weight_query: bfloat16 [1024, 2048], P(('seq', 'ctx')), may hold values from -0.1875 to 0.1875
- key_weight_matrix: bfloat16 [1024, 1024], P(('seq', 'ctx')), may hold values from -0.1875 to 0.1875
- value_weight_matrix: bfloat16 [1024, 1024], P(('seq', 'ctx')), may hold values from -0.1875 to 0.1875
- gain_query: bfloat16 [128], P(('seq', 'ctx')), may hold values from 0.25 to 1.75
- gain_key: bfloat16 [128], P(('seq', 'ctx')), may hold values from 0.25 to 1.75
- weight_output: bfloat16 [2048, 1024], P(('seq', 'ctx')), may hold values from -2 to 2
- gain_second: bfloat16 [1024], P(('seq', 'ctx')), may hold values from 0.25 to 1.75
- weight_gate: bfloat16 [1024, 3072], P(('seq', 'ctx')), may hold values from -0.1875 to 0.1875
- weight_up: bfloat16 [1024, 3072], P(('seq', 'ctx')), may hold values from -0.1875 to 0.1875
- weight_down: bfloat16 [3072, 1024], P(('seq', 'ctx')), may hold values from -0.109375 to 0.109375
- output_cotangent: bfloat16 [4, 1024, 1024], P('seq', 'ctx'), may hold values from -6 to 6
Outputs:
- layer_output: bfloat16 [4, 1024, 1024], P('seq', 'ctx')
- hidden_gradient: float32 [4, 1024, 1024], P('seq', 'ctx')
- change_first: float32 [1024], P(('seq', 'ctx'))
- delta_query: float32 [1024, 2048], P(('seq', 'ctx'))
- delta_key: float32 [1024, 1024], P(('seq', 'ctx'))
- delta_value: float32 [1024, 1024], P(('seq', 'ctx'))
- change_query: float32 [128], P(('seq', 'ctx'))
- change_key: float32 [128], P(('seq', 'ctx'))
- delta_output: float32 [2048, 1024], P(('seq', 'ctx'))
- change_second: float32 [1024], P(('seq', 'ctx'))
- delta_gate: float32 [1024, 3072], P(('seq', 'ctx'))
- delta_up: float32 [1024, 3072], P(('seq', 'ctx'))
- delta_down: float32 [3072, 1024], P(('seq', 'ctx'))
Inputs may be any that keep to these rules, and one draw needn't show every extreme that they name: In every sequence each position 0 to 1023 occurs once; the 128 stored tokens of one device of ctx are two runs of 64 consecutive ascending positions, each run starting at a multiple of 64, and their two run numbers sum to 15.
All inputs are finite; a program needn't handle non-finite values.
Results may differ from a plain program's by a relative error of at most 0.023.
Values may be sent and summed in bfloat16 or wider, within the bound.
A program may use at most 104 MiB of HBM per device.

v0:
```python
import jax
import jax.numpy as jnp
from jax import lax
from jax.sharding import PartitionSpec as P

QUERY_HEAD_COUNT = 16
KEY_VALUE_HEADS = 8
HEAD_DIMENSION = 128


EPS = 1e-06
THETA = 1000000.0
NEGATIVE = -1e30


def inverse_root(values):
    return lax.rsqrt(jnp.mean(values * values, axis=-1, keepdims=True) + EPS)


def angles(places, head_size):
    half_size = head_size // 2
    frequency = jnp.power(THETA, -jnp.arange(half_size, dtype=jnp.float32) * (2.0 / head_size))
    phases = places.astype(jnp.float32)[:, None] * frequency[None, :]
    phases = jnp.concatenate([phases, phases], axis=-1)
    return (jnp.cos(phases), jnp.sin(phases))


def rotate(values, cosines, sines):
    half_size = values.shape[-1] // 2
    turned = jnp.concatenate([-values[..., half_size:], values[..., :half_size]], axis=-1)
    return values * cosines + turned * sines


def rotate_back(upstream, cosines, sines):
    half_size = upstream.shape[-1] // 2
    scaled = upstream * sines
    turned = jnp.concatenate([scaled[..., half_size:], -scaled[..., :half_size]], axis=-1)
    return upstream * cosines + turned


def norm_backward(normed_grad, normed, inverse):
    return inverse * (normed_grad - normed * jnp.mean(normed_grad * normed, axis=-1, keepdims=True))


def local(
    hidden_states,
    positions,
    gain_first,
    weight_query,
    key_weight_matrix,
    value_weight_matrix,
    gain_query,
    gain_key,
    weight_output,
    gain_second,
    weight_gate,
    weight_up,
    weight_down,
    output_cotangent,
):
    tokens = hidden_states.shape[1]
    sequence_length = positions.shape[1]
    head_size = HEAD_DIMENSION
    query_heads = QUERY_HEAD_COUNT
    key_head_rows = KEY_VALUE_HEADS
    group_width = query_heads // key_head_rows
    scale_factor = head_size ** (-0.5)
    key_places = positions[0]
    own_places = lax.dynamic_slice_in_dim(key_places, lax.axis_index("ctx") * tokens, tokens)
    causal_mask = key_places[None, :] <= own_places[:, None]
    cosines, sines = angles(own_places, head_size)
    cosine_heads = cosines[:, None, :]
    sine_heads = sines[:, None, :]
    residual = hidden_states[0].astype(jnp.float32)
    first_gains, query_full, key_full, value_full, query_gains, key_gains, output_full = (
        lax.all_gather(gain_first, ("seq", "ctx"), axis=0, tiled=True),
        lax.all_gather(weight_query, ("seq", "ctx"), axis=0, tiled=True),
        lax.all_gather(key_weight_matrix, ("seq", "ctx"), axis=0, tiled=True),
        lax.all_gather(value_weight_matrix, ("seq", "ctx"), axis=0, tiled=True),
        lax.all_gather(gain_query, ("seq", "ctx"), axis=0, tiled=True),
        lax.all_gather(gain_key, ("seq", "ctx"), axis=0, tiled=True),
        lax.all_gather(weight_output, ("seq", "ctx"), axis=0, tiled=True),
    )
    first_scale = first_gains.astype(jnp.float32)
    query_scale = query_gains.astype(jnp.float32)
    key_scale = key_gains.astype(jnp.float32)
    first_inverse = inverse_root(residual)
    first_normed = residual * first_inverse
    leading_input = (first_normed * first_scale).astype(jnp.bfloat16)
    query_linear = jnp.dot(leading_input, query_full, preferred_element_type=jnp.float32).reshape(
        tokens, query_heads, head_size
    )
    key_projected = jnp.dot(leading_input, key_full, preferred_element_type=jnp.float32).reshape(
        tokens, key_head_rows, head_size
    )
    value_local = jnp.dot(leading_input, value_full, preferred_element_type=jnp.float32).astype(
        jnp.bfloat16
    )
    query_inverse = inverse_root(query_linear)
    query_normed = query_linear * query_inverse
    key_inverse = inverse_root(key_projected)
    key_normed = key_projected * key_inverse
    rotary_query = rotate(query_normed * query_scale, cosine_heads, sine_heads).astype(jnp.bfloat16)
    key_rotated = rotate(key_normed * key_scale, cosine_heads, sine_heads).astype(jnp.bfloat16)
    keys_all, values_all = (
        lax.all_gather(
            key_rotated.reshape(tokens, key_head_rows * head_size), "ctx", axis=0, tiled=True
        ),
        lax.all_gather(value_local, "ctx", axis=0, tiled=True),
    )
    query_blocks = rotary_query.reshape(tokens, key_head_rows, group_width, head_size)
    key_blocks = keys_all.reshape(sequence_length, key_head_rows, head_size)
    value_blocks = values_all.reshape(sequence_length, key_head_rows, head_size)

    def head_scores(head_index):
        query_head = lax.dynamic_index_in_dim(query_blocks, head_index, 1, keepdims=False)
        key_head = lax.dynamic_index_in_dim(key_blocks, head_index, 1, keepdims=False)
        value_head = lax.dynamic_index_in_dim(value_blocks, head_index, 1, keepdims=False)
        raw_scores = (
            jnp.einsum("qgd,kd->gqk", query_head, key_head, preferred_element_type=jnp.float32)
            * scale_factor
        )
        return (
            query_head,
            key_head,
            value_head,
            jnp.where(causal_mask[None], raw_scores, NEGATIVE),
        )

    def forward_head(head_index, carry):
        outputs, log_sums = carry
        query_head, key_head, value_head, scores = head_scores(head_index)
        row_max = jnp.max(scores, axis=-1, keepdims=True)
        exponent = jnp.exp(scores - row_max)
        row_total = jnp.sum(exponent, axis=-1, keepdims=True)
        weights_low = (exponent / row_total).astype(jnp.bfloat16)
        head_output = jnp.einsum(
            "gqk,kd->qgd", weights_low, value_head, preferred_element_type=jnp.float32
        )
        log_total = row_max[..., 0] + jnp.log(row_total[..., 0])
        return (
            lax.dynamic_update_index_in_dim(outputs, head_output, head_index, 1),
            lax.dynamic_update_index_in_dim(log_sums, log_total, head_index, 0),
        )

    start_carry = (
        jnp.zeros((tokens, key_head_rows, group_width, head_size), jnp.float32),
        jnp.zeros((key_head_rows, group_width, tokens), jnp.float32),
    )
    attention, log_totals = lax.fori_loop(0, key_head_rows, forward_head, start_carry)
    attention_low = attention.reshape(tokens, query_heads * head_size).astype(jnp.bfloat16)
    middle = residual + jnp.dot(attention_low, output_full, preferred_element_type=jnp.float32)
    second_gains, gate_full, up_full, down_full = (
        lax.all_gather(gain_second, ("seq", "ctx"), axis=0, tiled=True),
        lax.all_gather(weight_gate, ("seq", "ctx"), axis=0, tiled=True),
        lax.all_gather(weight_up, ("seq", "ctx"), axis=0, tiled=True),
        lax.all_gather(weight_down, ("seq", "ctx"), axis=0, tiled=True),
    )
    second_scale = second_gains.astype(jnp.float32)
    second_inverse = inverse_root(middle)
    second_normed = middle * second_inverse
    second_input = (second_normed * second_scale).astype(jnp.bfloat16)
    gate_linear = jnp.dot(second_input, gate_full, preferred_element_type=jnp.float32)
    up_linear = jnp.dot(second_input, up_full, preferred_element_type=jnp.float32)
    sigmoid_gate = jax.nn.sigmoid(gate_linear)
    silu_gate = gate_linear * sigmoid_gate
    activation = (silu_gate * up_linear).astype(jnp.bfloat16)
    layer_output = (
        middle + jnp.dot(activation, down_full, preferred_element_type=jnp.float32)
    ).astype(jnp.bfloat16)
    gate_back, up_back, down_back = (
        lax.all_gather(weight_gate, ("seq", "ctx"), axis=0, tiled=True),
        lax.all_gather(weight_up, ("seq", "ctx"), axis=0, tiled=True),
        lax.all_gather(weight_down, ("seq", "ctx"), axis=0, tiled=True),
    )
    upstream = output_cotangent[0].astype(jnp.float32)
    upstream_low = upstream.astype(jnp.bfloat16)
    delta_down = lax.psum_scatter(
        jnp.dot(activation.T, upstream_low, preferred_element_type=jnp.float32),
        ("seq", "ctx"),
        scatter_dimension=0,
        tiled=True,
    )
    act_grad = jnp.dot(upstream_low, down_back.T, preferred_element_type=jnp.float32)
    gate_low = (
        act_grad * up_linear * sigmoid_gate * (1.0 + gate_linear * (1.0 - sigmoid_gate))
    ).astype(jnp.bfloat16)
    up_low = (act_grad * silu_gate).astype(jnp.bfloat16)
    second_input_grad = jnp.dot(
        gate_low, gate_back.T, preferred_element_type=jnp.float32
    ) + jnp.dot(up_low, up_back.T, preferred_element_type=jnp.float32)
    second_gain_term = jnp.sum(second_input_grad * second_normed, axis=0)
    middle_grad = upstream + norm_backward(
        second_input_grad * second_scale, second_normed, second_inverse
    )
    hidden_units = gate_low.shape[1]
    both_low = jnp.concatenate([gate_low, up_low], axis=1)
    both_delta = lax.psum_scatter(
        jnp.dot(second_input.T, both_low, preferred_element_type=jnp.float32),
        ("seq", "ctx"),
        scatter_dimension=0,
        tiled=True,
    )
    delta_gate = both_delta[:, :hidden_units]
    delta_up = both_delta[:, hidden_units:]
    query_back, key_back, value_back, output_back = (
        lax.all_gather(weight_query, ("seq", "ctx"), axis=0, tiled=True),
        lax.all_gather(key_weight_matrix, ("seq", "ctx"), axis=0, tiled=True),
        lax.all_gather(value_weight_matrix, ("seq", "ctx"), axis=0, tiled=True),
        lax.all_gather(weight_output, ("seq", "ctx"), axis=0, tiled=True),
    )
    middle_low = middle_grad.astype(jnp.bfloat16)
    delta_output = lax.psum_scatter(
        jnp.dot(attention_low.T, middle_low, preferred_element_type=jnp.float32),
        ("seq", "ctx"),
        scatter_dimension=0,
        tiled=True,
    )
    attention_grad = jnp.dot(middle_low, output_back.T, preferred_element_type=jnp.float32).astype(
        jnp.bfloat16
    )
    attention_grad = attention_grad.reshape(tokens, key_head_rows, group_width, head_size)

    def backward_head(head_index, carry):
        query_sums, key_sums, value_sums = carry
        query_head, key_head, value_head, scores = head_scores(head_index)
        upstream_head = lax.dynamic_index_in_dim(attention_grad, head_index, 1, keepdims=False)
        log_head = lax.dynamic_index_in_dim(log_totals, head_index, 0, keepdims=False)
        probabilities = jnp.exp(scores - log_head[..., None])
        probabilities_low = probabilities.astype(jnp.bfloat16)
        prob_grad = jnp.einsum(
            "qgd,kd->gqk", upstream_head, value_head, preferred_element_type=jnp.float32
        )
        row_inner = jnp.sum(probabilities * prob_grad, axis=-1, keepdims=True)
        score_grad = (probabilities * (prob_grad - row_inner) * scale_factor).astype(jnp.bfloat16)
        query_part = jnp.einsum(
            "gqk,kd->qgd", score_grad, key_head, preferred_element_type=jnp.float32
        )
        key_part = jnp.einsum(
            "gqk,qgd->kd", score_grad, query_head, preferred_element_type=jnp.float32
        )
        value_part = jnp.einsum(
            "gqk,qgd->kd", probabilities_low, upstream_head, preferred_element_type=jnp.float32
        )
        return (
            lax.dynamic_update_index_in_dim(query_sums, query_part, head_index, 1),
            lax.dynamic_update_index_in_dim(key_sums, key_part, head_index, 1),
            lax.dynamic_update_index_in_dim(value_sums, value_part, head_index, 1),
        )

    back_carry = (
        jnp.zeros((tokens, key_head_rows, group_width, head_size), jnp.float32),
        jnp.zeros((sequence_length, key_head_rows, head_size), jnp.float32),
        jnp.zeros((sequence_length, key_head_rows, head_size), jnp.float32),
    )
    query_sums, key_sums, value_sums = lax.fori_loop(0, key_head_rows, backward_head, back_carry)
    key_total, value_total = (
        lax.psum_scatter(
            key_sums.reshape(sequence_length, key_head_rows * head_size).astype(jnp.bfloat16),
            "ctx",
            scatter_dimension=0,
            tiled=True,
        ).astype(jnp.float32),
        lax.psum_scatter(
            value_sums.reshape(sequence_length, key_head_rows * head_size).astype(jnp.bfloat16),
            "ctx",
            scatter_dimension=0,
            tiled=True,
        ).astype(jnp.float32),
    )
    value_grad_low = value_total.astype(jnp.bfloat16)
    key_pre = rotate_back(
        key_total.reshape(tokens, key_head_rows, head_size), cosine_heads, sine_heads
    )
    key_gain_term = jnp.sum(key_pre * key_normed, axis=(0, 1))
    key_low = norm_backward(key_pre * key_scale, key_normed, key_inverse).astype(jnp.bfloat16)
    key_low = key_low.reshape(tokens, key_head_rows * head_size)
    query_pre = rotate_back(
        query_sums.reshape(tokens, query_heads, head_size), cosine_heads, sine_heads
    )
    query_gain_term = jnp.sum(query_pre * query_normed, axis=(0, 1))
    query_low = norm_backward(query_pre * query_scale, query_normed, query_inverse).astype(
        jnp.bfloat16
    )
    query_low = query_low.reshape(tokens, query_heads * head_size)
    first_input_grad = (
        jnp.dot(query_low, query_back.T, preferred_element_type=jnp.float32)
        + jnp.dot(key_low, key_back.T, preferred_element_type=jnp.float32)
        + jnp.dot(value_grad_low, value_back.T, preferred_element_type=jnp.float32)
    )
    first_gain_term = jnp.sum(first_input_grad * first_normed, axis=0)
    hidden_gradient = middle_grad + norm_backward(
        first_input_grad * first_scale, first_normed, first_inverse
    )
    query_term = jnp.dot(leading_input.T, query_low, preferred_element_type=jnp.float32)
    key_term = jnp.dot(leading_input.T, key_low, preferred_element_type=jnp.float32)
    value_term = jnp.dot(leading_input.T, value_grad_low, preferred_element_type=jnp.float32)
    change_first, delta_query, delta_key, delta_value, change_query, change_key, change_second = (
        lax.psum_scatter(first_gain_term, ("seq", "ctx"), scatter_dimension=0, tiled=True),
        lax.psum_scatter(query_term, ("seq", "ctx"), scatter_dimension=0, tiled=True),
        lax.psum_scatter(key_term, ("seq", "ctx"), scatter_dimension=0, tiled=True),
        lax.psum_scatter(value_term, ("seq", "ctx"), scatter_dimension=0, tiled=True),
        lax.psum_scatter(query_gain_term, ("seq", "ctx"), scatter_dimension=0, tiled=True),
        lax.psum_scatter(key_gain_term, ("seq", "ctx"), scatter_dimension=0, tiled=True),
        lax.psum_scatter(second_gain_term, ("seq", "ctx"), scatter_dimension=0, tiled=True),
    )
    return (
        layer_output[None],
        hidden_gradient[None],
        change_first,
        delta_query,
        delta_key,
        delta_value,
        change_query,
        change_key,
        delta_output,
        change_second,
        delta_gate,
        delta_up,
        delta_down,
    )


def solution(mesh):
    return jax.shard_map(
        local,
        mesh=mesh,
        in_specs=(
            P("seq", "ctx", None),
            P("seq", None),
            P(("seq", "ctx")),
            P(("seq", "ctx"), None),
            P(("seq", "ctx"), None),
            P(("seq", "ctx"), None),
            P(("seq", "ctx")),
            P(("seq", "ctx")),
            P(("seq", "ctx"), None),
            P(("seq", "ctx")),
            P(("seq", "ctx"), None),
            P(("seq", "ctx"), None),
            P(("seq", "ctx"), None),
            P("seq", "ctx", None),
        ),
        out_specs=(
            P("seq", "ctx", None),
            P("seq", "ctx", None),
            P(("seq", "ctx")),
            P(("seq", "ctx"), None),
            P(("seq", "ctx"), None),
            P(("seq", "ctx"), None),
            P(("seq", "ctx")),
            P(("seq", "ctx")),
            P(("seq", "ctx"), None),
            P(("seq", "ctx")),
            P(("seq", "ctx"), None),
            P(("seq", "ctx"), None),
            P(("seq", "ctx"), None),
        ),
        check_vma=False,
    )
```

profile of v0, /device:TPU:9, one launch (start us, length us, event | category | flops | bytes accessed | tf_op | source)
XLA Modules:
  0.0 1709.3 jit_solution(6148967494213294258)
XLA Ops:
  12.1 39.8 %all-reduce.9 = (bf16[1024]{0:T(1024)(128)(2,1)S(1)}, bf16[128]{0:T(256)(128)(2,1)S(1)}, bf16[128]{0:T(256)(128)(2,1)S(1)}, bf16[1024]{0:T(1024)(128)(2,1)S(1)}) all-reduce(bf16[1024]{0:T(1024)(128)(2,1)S(1)} %dynamic-update-slice, bf16[128]{0:T(256)(128)(2,1)S(1)} %dynamic-update-slice.1, ...), channel_id=1, replica_groups=mesh['seq'=4,'ctx'=8] {'seq','ctx'}, use_global_device_ids=true, to_apply=%add | all-reduce | flops 2304 | bytes 9216
  53.1 14.7 all-gather.10.cloned.1.call-done
  71.6 54.1 %all-gather.14.cloned.1.call-done = bf16[1024,1024]{1,0:T(8,128)(2,1)} async-done(((bf16[32,1024]{1,0:T(8,128)(2,1)}), bf16[1024,1024]{1,0:T(8,128)(2,1)}) %all-gather.14.cloned.1.call-update) | async-done | bytes 2097168 | tf_op jit(solution)/shard_map/all_gather | solution.py:78
  135.3 20.5 %all-gather.12.cloned.1.call-done = bf16[1024,1024]{1,0:T(8,128)(2,1)} async-done(((bf16[128,1024]{1,0:T(8,128)(2,1)}), bf16[1024,1024]{1,0:T(8,128)(2,1)}) %all-gather.12.cloned.1.call-update) | async-done | bytes 2097168 | tf_op jit(solution)/shard_map/all_gather | solution.py:109
  162.9 23.4 %all-gather.16.cloned.1.call-done = bf16[1024,1024]{0,1:T(8,128)(2,1)} async-done(((bf16[128,1024]{0,1:T(8,128)(2,1)}), bf16[1024,1024]{0,1:T(8,128)(2,1)}) %all-gather.16.cloned.1.call-update) | async-done | bytes 2097168 | tf_op jit(solution)/shard_map/all_gather | solution.py:106
  190.2 60.5 %all-gather.18.cloned.1.call-done = bf16[1024,2048]{1,0:T(8,128)(2,1)} async-done(((bf16[32,2048]{1,0:T(8,128)(2,1)}), bf16[1024,2048]{1,0:T(8,128)(2,1)}) %all-gather.18.cloned.1.call-update) | async-done | bytes 4194320 | tf_op jit(solution)/shard_map/all_gather | solution.py:77
  250.7 6.4 copy.55
  262.8 33.7 %while.36 = (s32[]{:T(128)}, bf16[128,8,2,128]{0,3,2,1:T(8,128)(2,1)S(1)}, f32[8,2,128]{2,1,0:T(2,128)}, bf16[1024,8,128]{0,2,1:T(8,128)(2,1)}, bf16[1024,8,128]...) while((s32[]{:T(128)}, ...), condition=%wide.region_6.7_spmd.clone.clone, body=%wide.region_3.6_spmd.clone.sunk.clone | while | flops 136445696 | bytes 4143713 | solution.py:150
  296.6 17.4 %all-gather.20.cloned.1.call-done = bf16[2048,1024]{1,0:T(8,128)(2,1)} async-done(((bf16[64,1024]{1,0:T(8,128)(2,1)}), bf16[2048,1024]{1,0:T(8,128)(2,1)}) %all-gather.20.cloned.1.call-update) | async-done | bytes 4194320 | tf_op jit(solution)/shard_map/all_gather | solution.py:82
  317.1 67.8 %all-gather.22.cloned.1.call-done = bf16[1024,3072]{1,0:T(8,128)(2,1)} async-done(((bf16[32,3072]{1,0:T(8,128)(2,1)}), bf16[1024,3072]{1,0:T(8,128)(2,1)}) %all-gather.22.cloned.1.call-update) | async-done | bytes 6291472 | tf_op jit(solution)/shard_map/all_gather | solution.py:155
  384.9 5.0 fusion.115
  389.8 65.6 %all-gather.24.cloned.1.call-done = bf16[1024,3072]{1,0:T(8,128)(2,1)} async-done(((bf16[32,3072]{1,0:T(8,128)(2,1)}), bf16[1024,3072]{1,0:T(8,128)(2,1)}) %all-gather.24.cloned.1.call-update) | async-done | bytes 6291472 | tf_op jit(solution)/shard_map/all_gather | solution.py:156
  455.5 4.9 fusion.116
  460.4 65.7 %all-gather.26.cloned.1.call-done = bf16[3072,1024]{1,0:T(8,128)(2,1)} async-done(((bf16[96,1024]{1,0:T(8,128)(2,1)}), bf16[3072,1024]{1,0:T(8,128)(2,1)}) %all-gather.26.cloned.1.call-update) | async-done | bytes 6291472 | tf_op jit(solution)/shard_map/all_gather | solution.py:157
  526.1 7.0 multiply_convert_fusion
  533.1 5.6 fusion.117
  545.3 81.1 %while.37 = (s32[]{:T(128)}, f32[128,8,2,128]{0,3,2,1:T(8,128)}, bf16[1024,8,128]{0,2,1:T(8,128)(2,1)}, bf16[1024,8,128]{0,2,1:T(8,128)(2,1)}, bf16[1024,8,128]{...) while((s32[]{:T(128)}, f32[128,8,2,128]{0,3,2,1:T(8,128)}, ...), condition=%wide.region_11.12_spmd.clone.clone, body=%wide.region_9.11_spmd.clone.sunk.clone | while | flops 339347968 | bytes 14166661 | solution.py:256
  626.4 3.9 copy.69
  636.0 10.5 fusion.56
  646.6 23.0 %reduce-scatter.25.cloned.1.call-done = bf16[128,1024]{1,0:T(8,128)(2,1)} async-done(((bf16[1024,1024]{1,0:T(8,128)(2,1)}), bf16[128,1024]{1,0:T(8,128)(2,1)}) %reduce-scatter.25.cloned.1.call-update) | async-done | bytes 262160
  674.3 39.7 %reduce-scatter.27.cloned.1.call-done = bf16[128,1024]{1,0:T(8,128)(2,1)} async-done(((bf16[1024,1024]{1,0:T(8,128)(2,1)}), bf16[128,1024]{1,0:T(8,128)(2,1)}) %reduce-scatter.27.cloned.1.call-update) | async-done | bytes 262160
  720.5 4.6 fusion.95
  726.2 5.1 fusion.97
  732.6 7.5 fusion.85
  741.2 5.3 fusion.63
  750.8 40.3 %all-reduce.8 = (f32[1024]{0:T(1024)S(1)}, f32[128]{0:T(128)S(1)}, f32[128]{0:T(128)S(1)}, f32[1024]{0:T(1024)S(1)}) all-reduce(f32[1024]{0:T(1024)S(1)} %get-tuple-element.423, f32[128]{0:T(128)S(1)} %get-tuple-element.417, f32[128]{0:T(128)S(1)} %get-tuple-element.419, ...), channel_id=4, replica_groups=mesh['seq'=4,'ctx'=8] {'seq','ctx'}, use_global_device_ids=true, to_apply=%region_18.19.clone | all-reduce | flops 2304 | bytes 18432
  794.5 168.7 %reduce-scatter.21.cloned.1.call-done = f32[32,6144]{1,0:T(8,128)} async-done(((f32[1024,6144]{1,0:T(8,128)}), f32[32,6144]{1,0:T(8,128)}) %reduce-scatter.21.cloned.1.call-update) | async-done | bytes 786448 | tf_op jit(solution)/shard_map/reduce_scatter | solution.py:198
  965.2 119.7 %reduce-scatter.15.cloned.1.call-done = f32[32,1024]{1,0:T(8,128)} async-done(((f32[1024,1024]{1,0:T(8,128)}), f32[32,1024]{1,0:T(8,128)}) %reduce-scatter.15.cloned.1.call-update) | async-done | bytes 131088 | tf_op jit(solution)/shard_map/reduce_scatter | solution.py:301
  1085.0 141.6 %reduce-scatter.17.cloned.1.call-done = f32[32,1024]{1,0:T(8,128)} async-done(((f32[1024,1024]{1,0:T(8,128)}), f32[32,1024]{1,0:T(8,128)}) %reduce-scatter.17.cloned.1.call-update) | async-done | bytes 131088 | tf_op jit(solution)/shard_map/reduce_scatter | solution.py:302
  1226.6 150.1 %reduce-scatter.13.cloned.1.call-done = f32[32,2048]{1,0:T(8,128)} async-done(((f32[1024,2048]{1,0:T(8,128)}), f32[32,2048]{1,0:T(8,128)}) %reduce-scatter.13.cloned.1.call-update) | async-done | bytes 262160 | tf_op jit(solution)/shard_map/reduce_scatter | solution.py:300
  1376.6 148.6 %reduce-scatter.19.cloned.1.call-done = f32[64,1024]{1,0:T(8,128)} async-done(((f32[2048,1024]{1,0:T(8,128)}), f32[64,1024]{1,0:T(8,128)}) %reduce-scatter.19.cloned.1.call-update) | async-done | bytes 262160 | tf_op jit(solution)/shard_map/reduce_scatter | solution.py:213
  1525.2 177.6 %reduce-scatter.23.cloned.1.call-done = f32[96,1024]{1,0:T(8,128)} async-done(((f32[3072,1024]{1,0:T(8,128)}), f32[96,1024]{1,0:T(8,128)}) %reduce-scatter.23.cloned.1.call-update) | async-done | bytes 393232 | tf_op jit(solution)/shard_map/reduce_scatter | solution.py:178
  (292 shorter events, 190.0 us)
Async XLA Ops:
  7.2 63.6 %copy-start.29 = (s32[1,1024]{1,0:T(1,128)S(1)}, s32[1,1024]{1,0:T(1,128)}, u32[]{:S(2)}) copy-start(s32[1,1024]{1,0:T(1,128)} %param.19) | copy-start | bytes 12292
  7.2 60.6 %all-gather.10.cloned.1.call-start = ((), (), s32[]{:S(2)}) async-start(), calls=%async_computation.8 | async-start | bytes 2162688 | tf_op jit(solution)/shard_map/all_gather | solution.py:79
  7.9 117.8 %all-gather.14.cloned.1.call-start = ((), (), s32[]{:S(2)}) async-start(), calls=%async_computation.10 | async-start | bytes 2162688 | tf_op jit(solution)/shard_map/all_gather | solution.py:78
  8.7 147.1 %all-gather.12.cloned.1.call-start = ((), (), s32[]{:S(2)}) async-start(), calls=%async_computation.9 | async-start | bytes 2359296 | tf_op jit(solution)/shard_map/all_gather | solution.py:109
  53.1 204.0 %copy-start.33 = (f32[128]{0:T(128)}, f32[128]{0:T(128)S(1)}, u32[]{:S(2)}) copy-start(f32[128]{0:T(128)S(1)} %add_rsqrt_fusion.3) | copy-start | bytes 1540
  70.7 115.6 %all-gather.16.cloned.1.call-start = ((), (), s32[]{:S(2)}) async-start(), calls=%async_computation.11 | async-start | bytes 2359296 | tf_op jit(solution)/shard_map/all_gather | solution.py:106
  70.7 58.9 %copy-start.36 = (f32[128]{0:T(128)}, f32[128]{0:T(128)S(1)}, u32[]{:S(2)}) copy-start(f32[128]{0:T(128)S(1)} %convert_element_type.132) | copy-start | bytes 1540
  71.6 189.3 %copy-start.24 = (f32[128,128]{0,1:T(8,128)}, f32[128,128]{0,1:T(8,128)S(1)}, u32[]{:S(2)}) copy-start(f32[128,128]{0,1:T(8,128)S(1)} %get-tuple-element.490) | copy-start | bytes 196612
  131.1 119.5 %all-gather.18.cloned.1.call-start = ((), (), s32[]{:S(2)}) async-start(), calls=%async_computation.12 | async-start | bytes 4325376 | tf_op jit(solution)/shard_map/all_gather | solution.py:77
  131.7 182.2 %all-gather.20.cloned.1.call-start = ((), (), s32[]{:S(2)}) async-start(), calls=%async_computation.13 | async-start | bytes 4325376 | tf_op jit(solution)/shard_map/all_gather | solution.py:82
  132.3 252.6 %all-gather.22.cloned.1.call-start = ((), (), s32[]{:S(2)}) async-start(), calls=%async_computation.14 | async-start | bytes 6488064 | tf_op jit(solution)/shard_map/all_gather | solution.py:155
  133.0 322.4 %all-gather.24.cloned.1.call-start = ((), (), s32[]{:S(2)}) async-start(), calls=%async_computation.15 | async-start | bytes 6488064 | tf_op jit(solution)/shard_map/all_gather | solution.py:156
  133.8 392.3 %all-gather.26.cloned.1.call-start = ((), (), s32[]{:S(2)}) async-start(), calls=%async_computation.16 | async-start | bytes 6488064 | tf_op jit(solution)/shard_map/all_gather | solution.py:157
  134.5 535.1 %reduce-scatter.25.cloned.1.call-start = ((), (), s32[]{:S(2)}) async-start(), calls=%async_computation.23 | async-start | bytes 2359296
  134.7 125.9 %copy-start.38 = (f32[128]{0:T(128)}, f32[128]{0:T(128)S(1)}, u32[]{:S(2)}) copy-start(f32[128]{0:T(128)S(1)} %convert_element_type.135) | copy-start | bytes 1540
  296.6 20.4 %copy-start.15 = (bf16[128,8,2,128]{0,3,2,1:T(8,128)(2,1)}, bf16[128,8,2,128]{0,3,2,1:T(8,128)(2,1)S(1)}, u32[]{:S(2)}) copy-start(bf16[128,8,2,128]{0,3,2,1:T(8,128)(2,1)S(1)} %get-tuple-element.309) | copy-start | bytes 1572868
  316.9 224.7 %copy-start.6 = (f32[128,1024]{1,0:T(8,128)}, f32[128,1024]{1,0:T(8,128)S(1)}, u32[]{:S(2)}) copy-start(f32[128,1024]{1,0:T(8,128)S(1)} %get-tuple-element.496) | copy-start | bytes 1572868
  317.1 138.4 %copy-start.13 = (bf16[128,1024]{1,0:T(8,128)(2,1)}, bf16[128,1024]{1,0:T(8,128)(2,1)S(1)}, u32[]{:S(2)}) copy-start(bf16[128,1024]{1,0:T(8,128)(2,1)S(1)} %multiply_convert_fusion.5) | copy-start | bytes 786436
  389.8 136.2 %copy-start.26 = (bf16[1,128,1024]{2,1,0:T(8,128)(2,1)S(1)}, bf16[1,128,1024]{2,1,0:T(8,128)(2,1)}, u32[]{:S(2)}) copy-start(bf16[1,128,1024]{2,1,0:T(8,128)(2,1)} %param.31) | copy-start | bytes 786436
  533.1 5.6 copy-start
  630.4 83.6 %reduce-scatter.27.cloned.1.call-start = ((), (), s32[]{:S(2)}) async-start(), calls=%async_computation.24 | async-start | bytes 2359296
  634.5 328.7 %reduce-scatter.21.cloned.1.call-start = ((), (), s32[]{:S(2)}) async-start(), calls=%async_computation.21 | async-start | bytes 25952256 | tf_op jit(solution)/shard_map/reduce_scatter | solution.py:198
  646.5 24.2 %copy-start.25 = (f32[128,128]{0,1:T(8,128)S(1)}, f32[128,128]{0,1:T(8,128)}, u32[]{:S(2)}) copy-start(f32[128,128]{0,1:T(8,128)} %copy-done.24) | copy-start | bytes 196612
  646.5 24.3 %copy-start.5 = (f32[128,8,128]{0,2,1:T(8,128)S(1)}, f32[128,8,128]{0,2,1:T(8,128)}, u32[]{:S(2)}) copy-start(f32[128,8,128]{0,2,1:T(8,128)} %copy-done.4) | copy-start | bytes 1572868
  646.5 24.3 %copy-start.31 = (f32[128,8]{0,1:T(8,128)S(1)}, f32[128,8]{0,1:T(8,128)}, u32[]{:S(2)}) copy-start(f32[128,8]{0,1:T(8,128)} %copy-done.30) | copy-start | bytes 12292
  646.5 24.3 %copy-start.37 = (f32[128]{0:T(128)S(1)}, f32[128]{0:T(128)}, u32[]{:S(2)}) copy-start(f32[128]{0:T(128)} %copy-done.36) | copy-start | bytes 1540
  646.5 438.4 %reduce-scatter.15.cloned.1.call-start = ((), (), s32[]{:S(2)}) async-start(), calls=%async_computation.18 | async-start | bytes 4325376 | tf_op jit(solution)/shard_map/reduce_scatter | solution.py:301
  674.3 552.3 %reduce-scatter.17.cloned.1.call-start = ((), (), s32[]{:S(2)}) async-start(), calls=%async_computation.19 | async-start | bytes 4325376 | tf_op jit(solution)/shard_map/reduce_scatter | solution.py:302
  717.8 658.8 %reduce-scatter.13.cloned.1.call-start = ((), (), s32[]{:S(2)}) async-start(), calls=%async_computation.17 | async-start | bytes 8650752 | tf_op jit(solution)/shard_map/reduce_scatter | solution.py:300
  725.1 800.2 %reduce-scatter.19.cloned.1.call-start = ((), (), s32[]{:S(2)}) async-start(), calls=%async_computation.20 | async-start | bytes 8650752 | tf_op jit(solution)/shard_map/reduce_scatter | solution.py:213
  731.3 971.5 %reduce-scatter.23.cloned.1.call-start = ((), (), s32[]{:S(2)}) async-start(), calls=%async_computation.22 | async-start | bytes 12976128 | tf_op jit(solution)/shard_map/reduce_scatter | solution.py:178
  741.2 6.1 copy-start.11
  (26 other events, 57.0 us)
Sparse Core Ops, SparseCore 0:
  10.9 56.8 all-gather.9
  70.6 55.0 all-gather.13
  128.2 27.5 all-gather.11
  158.1 28.1 all-gather.15
  189.0 61.6 all-gather.17
  253.4 60.5 all-gather.19
  316.8 68.0 all-gather.21
  387.7 67.6 all-gather.23
  458.3 67.6 all-gather.25
  630.5 39.0 reduce-scatter.24
  672.9 41.0 reduce-scatter.26
  720.3 242.8 reduce-scatter.20
  966.0 118.8 reduce-scatter.14
  1087.7 138.8 reduce-scatter.16
  1229.3 147.3 reduce-scatter.12
  1379.4 145.8 reduce-scatter.18
  1531.7 171.0 reduce-scatter.22
where the time goes:
time: 1720 us; the launch traced here: 1710 us
  waiting for transfers between devices  1360 us (79%)
  matrix products  162 us (9%)
  blocking collectives  80.2 us (5%)
  local copies, waits for them, and re-layouts  61.1 us (4%)
  other arithmetic  26.7 us (2%)
    reduce_scatter x1, waiting for transfers between devices, local(): lax.psum_scatter(jnp.dot(activation.T, upstream_low, preferred_element_ty...  178 us
    reduce_scatter x1, waiting for transfers between devices, local(): lax.psum_scatter(jnp.dot(second_input.T, both_low, preferred_element_type...  169 us
    reduce_scatter x1, waiting for transfers between devices, local(): lax.psum_scatter(query_term, ('seq', 'ctx'), scatter_dimension=0, tiled=T...  150 us
    reduce_scatter x1, waiting for transfers between devices, local(): lax.psum_scatter(jnp.dot(attention_low.T, middle_low, preferred_element_t...  149 us
    reduce_scatter x1, waiting for transfers between devices, local(): lax.psum_scatter(value_term, ('seq', 'ctx'), scatter_dimension=0, tiled=T...  142 us
    reduce_scatter x1, waiting for transfers between devices, local(): lax.psum_scatter(key_term, ('seq', 'ctx'), scatter_dimension=0, tiled=True)  120 us
    unnamed x2, blocking collectives  80.2 us
    all_gather x1, waiting for transfers between devices, local(): lax.all_gather(weight_gate, ('seq', 'ctx'), axis=0, tiled=True)  67.8 us
  transfers between devices with their start and end apart: 17, of which 17 were waited for; matrix products, arithmetic and copies ran while one was open for 8% of the time, Pallas kernels for 0%

commit v1 on v0

v1 whole, which is shorter than its diff:
```python
import jax
import jax.numpy as jnp
from jax import lax
from jax.sharding import PartitionSpec as P

QUERY_HEAD_COUNT = 16
KEY_VALUE_HEADS = 8
HEAD_DIMENSION = 128

EPS = 1e-06
THETA = 1000000.0
NEGATIVE = -1e30
BF = jnp.bfloat16
F32 = jnp.float32


def inverse_root(values):
    return lax.rsqrt(jnp.mean(values * values, axis=-1, keepdims=True) + EPS)


def angles(places, head_size):
    half_size = head_size // 2
    frequency = jnp.power(THETA, -jnp.arange(half_size, dtype=F32) * (2.0 / head_size))
    phases = places.astype(F32)[:, None] * frequency[None, :]
    phases = jnp.concatenate([phases, phases], axis=-1)
    return (jnp.cos(phases), jnp.sin(phases))


def rotate(values, cosines, sines):
    half_size = values.shape[-1] // 2
    turned = jnp.concatenate([-values[..., half_size:], values[..., :half_size]], axis=-1)
    return values * cosines + turned * sines


def rotate_back(upstream, cosines, sines):
    half_size = upstream.shape[-1] // 2
    scaled = upstream * sines
    turned = jnp.concatenate([scaled[..., half_size:], -scaled[..., :half_size]], axis=-1)
    return upstream * cosines + turned


def norm_backward(normed_grad, normed, inverse):
    return inverse * (normed_grad - normed * jnp.mean(normed_grad * normed, axis=-1, keepdims=True))


def dot(a, b):
    return jnp.dot(a, b, preferred_element_type=F32)


def local_of(mesh):
    seqs, ranks = mesh.shape["seq"], mesh.shape["ctx"]
    devices = seqs * ranks
    axes = ("seq", "ctx")

    def spread(shard, heads):
        rows, columns = shard.shape
        if heads and heads < ranks:
            blocks = shard.reshape(rows, heads, 1, columns // heads)
            blocks = jnp.broadcast_to(blocks, (rows, heads, ranks // heads, columns // heads))
            return blocks.reshape(rows, ranks, columns // heads)
        return shard.reshape(rows, ranks, columns // ranks)

    def fold(blocks, heads):
        rows, count, width = blocks.shape
        if heads and heads < ranks:
            return blocks.reshape(rows, heads, count // heads, width).sum(2).reshape(rows, heads * width)
        return blocks.reshape(rows, count * width)

    forth = [(seqs * r + j, j * ranks + r) for r in range(ranks) for j in range(seqs)]
    back = [(b, a) for a, b in forth]

    def local(
        hidden_states, positions, gain_first, weight_query, key_weight_matrix, value_weight_matrix,
        gain_query, gain_key, weight_output, gain_second, weight_gate, weight_up, weight_down,
        output_cotangent,
    ):
        tokens = hidden_states.shape[1]
        length = positions.shape[1]
        size = HEAD_DIMENSION
        group = QUERY_HEAD_COUNT // KEY_VALUE_HEADS
        my_q = QUERY_HEAD_COUNT // ranks
        my_k = max(1, KEY_VALUE_HEADS // ranks)
        scale = size ** (-0.5)
        places = positions[0]
        cosines, sines = angles(places, size)
        cosines, sines = cosines[:, None, :], sines[:, None, :]

        gains = jnp.concatenate([gain_first, gain_second, gain_query, gain_key])
        gains = lax.all_gather(gains, axes, axis=0).astype(F32)
        n1, n2, n3, n4 = (g.shape[0] for g in (gain_first, gain_second, gain_query, gain_key))
        first_scale = gains[:, :n1].reshape(-1)
        second_scale = gains[:, n1 : n1 + n2].reshape(-1)
        query_scale = gains[:, n1 + n2 : n1 + n2 + n3].reshape(-1)
        key_scale = gains[:, n1 + n2 + n3 :].reshape(-1)

        column_weights = jnp.concatenate(
            [
                spread(weight_query, 0),
                spread(key_weight_matrix, KEY_VALUE_HEADS),
                spread(value_weight_matrix, KEY_VALUE_HEADS),
                spread(weight_gate, 0),
                spread(weight_up, 0),
            ],
            axis=2,
        )
        column_weights = lax.all_to_all(column_weights, "ctx", split_axis=1, concat_axis=0, tiled=True)
        column_weights = lax.all_gather(column_weights[:, 0], "seq", axis=0, tiled=True)
        row_weights = jnp.concatenate([weight_output, weight_down], axis=0)
        row_weights = lax.all_gather(lax.ppermute(row_weights, axes, forth), "seq", axis=0)
        o_rows, d_rows = weight_output.shape[0], weight_down.shape[0]
        width = weight_output.shape[1]
        w_o = row_weights[:, :o_rows].reshape(-1, width)
        w_d = row_weights[:, o_rows:].reshape(-1, width)
        units = w_d.shape[0]
        attn_columns = (my_q + 2 * my_k) * size
        w_qkv = column_weights[:, :attn_columns]
        w_gu = column_weights[:, attn_columns:]

        x = lax.all_gather(hidden_states[0], "ctx", axis=0, tiled=True).astype(F32)
        g_low = lax.all_gather(output_cotangent[0], "ctx", axis=0, tiled=True)
        first_inverse = inverse_root(x)
        h1 = (x * first_inverse * first_scale).astype(BF)
        qkv = dot(h1, w_qkv)
        q_lin = qkv[:, : my_q * size].reshape(length, my_q, size)
        k_lin = qkv[:, my_q * size : (my_q + my_k) * size].reshape(length, my_k, size)
        v = qkv[:, (my_q + my_k) * size :].astype(BF).reshape(length, my_k, size)
        rq, rk = inverse_root(q_lin), inverse_root(k_lin)
        nq, nk = q_lin * rq, k_lin * rk
        qr = rotate(nq * query_scale, cosines, sines).astype(BF)
        kr = rotate(nk * key_scale, cosines, sines).astype(BF)
        mask = places[None, :] <= places[:, None]

        def scores(h):
            e = lax.dot_general(
                qr[:, h], kr[:, h // group], (((1,), (1,)), ((), ())), preferred_element_type=F32
            )
            return jnp.where(mask, e * scale, NEGATIVE)

        outs, probs = [], []
        for h in range(my_q):
            e = scores(h)
            p = jnp.exp(e - jnp.max(e, axis=-1, keepdims=True))
            p = p / jnp.sum(p, axis=-1, keepdims=True)
            probs.append(p)
            outs.append(dot(p.astype(BF), v[:, h // group]))
        o = jnp.concatenate(outs, axis=1).astype(BF)

        def scatter(part):
            return lax.psum_scatter(part.astype(BF), "ctx", scatter_dimension=0, tiled=True).astype(F32)

        x_own = hidden_states[0].astype(F32)
        y1 = x_own + scatter(dot(o, w_o))
        r2 = inverse_root(y1)
        second_normed = y1 * r2
        h2 = lax.all_gather((second_normed * second_scale).astype(BF), "ctx", axis=0, tiled=True)
        gu = dot(h2, w_gu)
        gate, up = gu[:, :units], gu[:, units:]
        sig = jax.nn.sigmoid(gate)
        silu = gate * sig
        act = (silu * up).astype(BF)
        layer_output = (y1 + scatter(dot(act, w_d))).astype(BF)

        d_act = dot(g_low, w_d.T)
        d_gate = (d_act * up * sig * (1.0 + gate * (1.0 - sig))).astype(BF)
        d_up = (d_act * silu).astype(BF)
        d_gu = jnp.concatenate([d_gate, d_up], axis=1)
        d_h2 = scatter(dot(d_gu, w_gu.T))
        second_term = jnp.sum(d_h2 * second_normed, axis=0)
        d_y1 = output_cotangent[0].astype(F32) + norm_backward(d_h2 * second_scale, second_normed, r2)
        d_y1_low = lax.all_gather(d_y1.astype(BF), "ctx", axis=0, tiled=True)
        d_o = dot(d_y1_low, w_o.T).astype(BF).reshape(length, my_q, size)

        d_q, d_k, d_v = [], [0.0] * my_k, [0.0] * my_k
        for h in range(my_q):
            p = probs[h]
            dp = lax.dot_general(
                d_o[:, h], v[:, h // group], (((1,), (1,)), ((), ())), preferred_element_type=F32
            )
            row = jnp.sum(p * dp, axis=-1, keepdims=True)
            de = (p * (dp - row) * scale).astype(BF)
            d_q.append(dot(de, kr[:, h // group]))
            d_k[h // group] += dot(de.T, qr[:, h])
            d_v[h // group] += dot(p.astype(BF).T, d_o[:, h])
        d_q, d_k, d_v = jnp.stack(d_q, 1), jnp.stack(d_k, 1), jnp.stack(d_v, 1)
        d_gq, d_gk = rotate_back(d_q, cosines, sines), rotate_back(d_k, cosines, sines)
        query_term = jnp.sum(d_gq * nq, axis=(0, 1))
        key_term = jnp.sum(d_gk * nk, axis=(0, 1))
        d_qlin = norm_backward(d_gq * query_scale, nq, rq).reshape(length, -1)
        d_klin = norm_backward(d_gk * key_scale, nk, rk).reshape(length, -1)
        d_qkv = jnp.concatenate([d_qlin, d_klin, d_v.reshape(length, -1)], axis=1).astype(BF)
        d_h1 = scatter(dot(d_qkv, w_qkv.T))
        r1 = inverse_root(x_own)
        first_normed = x_own * r1
        first_term = jnp.sum(d_h1 * first_normed, axis=0)
        hidden_gradient = d_y1 + norm_backward(d_h1 * first_scale, first_normed, r1)

        def rows_sum(part):
            part = lax.psum_scatter(part.astype(BF), "seq", scatter_dimension=0, tiled=True)
            return lax.ppermute(part, axes, back).astype(F32)

        delta_rows = jnp.concatenate(
            [dot(o.T, d_y1_low).reshape(seqs, o_rows, width), dot(act.T, g_low).reshape(seqs, d_rows, width)],
            axis=1,
        ).reshape(-1, width)
        delta_rows = rows_sum(delta_rows)
        delta_columns = jnp.concatenate([dot(h1.T, d_qkv), dot(h2.T, d_gu)], axis=1).astype(BF)
        delta_columns = lax.psum_scatter(delta_columns, "seq", scatter_dimension=0, tiled=True)
        own = delta_columns.shape[0] // ranks
        delta_columns = lax.all_to_all(
            delta_columns.reshape(ranks, own, -1), "ctx", split_axis=0, concat_axis=0, tiled=True
        )
        delta_columns = jnp.moveaxis(delta_columns, 0, 1).astype(F32)
        cuts = [my_q * size, (my_q + my_k) * size, (my_q + 2 * my_k) * size, attn_columns + units]
        parts = jnp.split(delta_columns, cuts, axis=2)
        delta_query = fold(parts[0], 0)
        delta_key = fold(parts[1], KEY_VALUE_HEADS)
        delta_value = fold(parts[2], KEY_VALUE_HEADS)
        delta_gate, delta_up = fold(parts[3], 0), fold(parts[4], 0)

        terms = lax.psum(jnp.concatenate([first_term, second_term, query_term, key_term]), axes)
        me = lax.axis_index("seq") * ranks + lax.axis_index("ctx")
        w = width

        def mine(start, n):
            return lax.dynamic_slice_in_dim(terms, start + me * n, n)

        return (
            layer_output[None],
            hidden_gradient[None],
            mine(0, n1),
            delta_query,
            delta_key,
            delta_value,
            mine(2 * w, n3),
            mine(2 * w + size, n4),
            delta_rows[:o_rows],
            mine(w, n2),
            delta_gate,
            delta_up,
            delta_rows[o_rows:],
        )

    return local


def solution(mesh):
    token = P("seq", "ctx", None)
    flat = P(("seq", "ctx"))
    rows = P(("seq", "ctx"), None)
    return jax.shard_map(
        local_of(mesh),
        mesh=mesh,
        in_specs=(token, P("seq", None), flat, rows, rows, rows, flat, flat, rows, flat, rows, rows, rows, token),
        out_specs=(token, token, flat, rows, rows, rows, flat, flat, rows, flat, rows, rows, rows),
        check_vma=False,
    )
```

time: 1720 us -> 572 us (0.33)
  waiting for transfers between devices: 1360 us -> 301 us
  matrix products: 162 us -> 54.9 us
  local copies, waits for them, and re-layouts: 61.1 us -> 26.3 us
  blocking collectives: 80.2 us -> 107 us
  starting transfers between devices: 0.94 us -> 21.3 us
    reduce_scatter x6, waiting for transfers between devices: 906 us -> 143 us  [the longest x4 133 us: scatter(): lax.psum_scatter(part.astype(BF), 'ctx', scatter_dimension=0, tiled=True)]
    all_gather x9 -> x6, waiting for transfers between devices: 390 us -> 130 us  [the longest x1 51.3 us: local(): lax.all_gather(column_weights[:, 0], 'seq', axis=0, tiled=True)]
    dot_general x76 -> x24, matrix products: 162 us -> 54.9 us  [the longest x20 45.1 us: dot(): return jnp.dot(a, b, preferred_element_type=F32)]
    unnamed x19 -> x12, waiting for transfers between devices: 67.4 us -> 1.38 us
    psum x0 -> x1, blocking collectives: none -> 42.3 us  [local(): lax.psum(jnp.concatenate([first_term, second_term, query_term, key_term])...]
    unnamed x2 -> x1, blocking collectives: 80.2 us -> 40.2 us
    ppermute x0 -> x2, waiting for transfers between devices: none -> 26.6 us  [the longest x1 21.6 us: rows_sum(): return lax.ppermute(part, axes, back).astype(F32)]
    all_to_all x0 -> x1, blocking collectives: none -> 24.4 us  [local(): lax.all_to_all(column_weights, 'ctx', split_axis=1, concat_axis=0, tiled=...]
  transfers between devices with their start and end apart: 17 -> 15, of which waited for: 17 -> 12; matrix products, arithmetic and copies ran while one was open for 8% -> 9% of each run, Pallas kernels for 0% -> 0%
where the time goes in v1:
time: 572 us; the launch traced here: 562 us
  waiting for transfers between devices  301 us (53%)
  blocking collectives  107 us (19%)
  matrix products  54.9 us (10%)
  other arithmetic  36.8 us (6%)
  local copies, waits for them, and re-layouts  26.3 us (5%)
  starting transfers between devices  21.3 us (4%)
  between operations  15.4 us (3%)
    reduce_scatter x4, waiting for transfers between devices, scatter(): lax.psum_scatter(part.astype(BF), 'ctx', scatter_dimension=0, tiled=True)  133 us
    all_gather x1, waiting for transfers between devices, local(): lax.all_gather(column_weights[:, 0], 'seq', axis=0, tiled=True)  51.3 us
    dot_general x20, matrix products, dot(): return jnp.dot(a, b, preferred_element_type=F32)  45.1 us
    psum x1, blocking collectives, local(): lax.psum(jnp.concatenate([first_term, second_term, query_term, key_term])...  42.3 us
    unnamed x1, blocking collectives  40.2 us
    all_gather x1, waiting for transfers between devices, local(): lax.all_gather((second_normed * second_scale).astype(BF), 'ctx', axis=0,...  27.8 us
    all_gather x1, waiting for transfers between devices, local(): d_y1_low = lax.all_gather(d_y1.astype(BF), 'ctx', axis=0, tiled=True)  24.9 us
    all_to_all x1, blocking collectives, local(): lax.all_to_all(column_weights, 'ctx', split_axis=1, concat_axis=0, tiled=...  24.4 us
  transfers between devices with their start and end apart: 15, of which 12 were waited for; matrix products, arithmetic and copies ran while one was open for 9% of the time, Pallas kernels for 0%

profile of v1, /device:TPU:9, one launch (start us, length us, event | category | flops | bytes accessed | tf_op | source)
XLA Modules:
  0.0 562.4 jit_solution(8720464472376751434)
XLA Ops:
  8.3 3.7 collective-permute-start
  12.0 5.0 collective-permute-done
  22.5 24.4 %all_to_all.20 = bf16[32,8,1280]{2,0,1:T(8,128)(2,1)} all-to-all(bf16[32,8,1280]{2,0,1:T(8,128)(2,1)S(1)} %copy.47), channel_id=1, replica_groups=mesh['seq'=4,'ctx'=8] {'ctx'}, dimensions={1} | all-to-all | bytes 1310720 | tf_op jit(solution)/shard_map/all_to_all | solution.py:106
  47.4 40.2 %all-reduce = bf16[2304]{0:T(1024)(128)(2,1)S(1)} all-reduce(bf16[2304]{0:T(1024)(128)(2,1)S(1)} %dynamic-update-slice), channel_id=3, replica_groups=mesh['seq'=4,'ctx'=8] {'seq','ctx'}, use_global_device_ids=true, to_apply=%add | all-reduce | flops 2304 | bytes 9216
  93.3 51.3 %all-gather.11.cloned.1.call-done = bf16[1024,1280]{1,0:T(8,128)(2,1)} async-done(((bf16[256,1280]{1,0:T(8,128)(2,1)}), bf16[1024,1280]{1,0:T(8,128)(2,1)}) %all-gather.11.cloned.1.call-update) | async-done | bytes 2621456 | tf_op jit(solution)/shard_map/all_gather | solution.py:107
  144.6 2.6 fusion.36
  152.8 2.3 fusion.4
  155.1 2.6 fusion.3
  164.2 41.7 %reduce-scatter.7.cloned.1.call-done = bf16[128,1024]{1,0:T(8,128)(2,1)} async-done(((bf16[1024,1024]{1,0:T(8,128)(2,1)}), bf16[128,1024]{1,0:T(8,128)(2,1)}) %reduce-scatter.7.cloned.1.call-update) | async-done | bytes 262160 | tf_op jit(solution)/shard_map/reduce_scatter | solution.py:149
  209.5 27.8 %all-gather.13.cloned.1.call-done = bf16[1024,1024]{1,0:T(8,128)(2,1)} async-done(((bf16[128,1024]{1,0:T(8,128)(2,1)}), bf16[1024,1024]{1,0:T(8,128)(2,1)}) %all-gather.13.cloned.1.call-update) | async-done | bytes 2097168 | tf_op jit(solution)/shard_map/all_gather | solution.py:155
  237.3 5.5 fusion.22
  242.8 24.0 %all-gather.21.cloned.1.call-done = bf16[1,1024,1024]{2,1,0:T(8,128)(2,1)} async-done(((bf16[1,128,1024]{2,1,0:T(8,128)(2,1)}), bf16[1,1024,1024]{2,1,0:T(8,128)(2,1)}) %all-gather.21.cloned.1.call-update) | async-done | bytes 2097168 | tf_op jit(solution)/shard_map/all_gather | solution.py:120
  266.8 4.2 fusion.15
  272.2 3.2 convolution_convert_fusion.3
  275.5 40.6 %reduce-scatter.11.cloned.1.call-done = bf16[128,1024]{1,0:T(8,128)(2,1)} async-done(((bf16[1024,1024]{1,0:T(8,128)(2,1)}), bf16[128,1024]{1,0:T(8,128)(2,1)}) %reduce-scatter.11.cloned.1.call-update) | async-done | bytes 262160 | tf_op jit(solution)/shard_map/reduce_scatter | solution.py:149
  319.4 3.5 fusion.18
  322.9 24.9 %all-gather.15.cloned.1.call-done = bf16[1024,1024]{1,0:T(8,128)(2,1)} async-done(((bf16[128,1024]{1,0:T(8,128)(2,1)}), bf16[1024,1024]{1,0:T(8,128)(2,1)}) %all-gather.15.cloned.1.call-update) | async-done | bytes 2097168 | tf_op jit(solution)/shard_map/all_gather | solution.py:170
  347.8 2.5 convolution_convert_fusion.7
  350.7 4.0 multiply_reduce_fusion
  354.6 3.7 multiply_reduce_fusion.1
  358.4 7.8 %multiply_convert_fusion = (bf16[1024,1024]{0,1:T(8,128)(2,1)}, bf16[1024,1024]{0,1:T(8,128)(2,1)}) fusion(f32[1024,1024]{0,1:T(8,128)S(1)} %copy-done.1, f32[1024,1024]{0,1:T(8,128)} %get-tuple-element.63, f32[1024]{0:T(1024)S(1)} %get-tuple-element.62, f32[1024,1024]{0,1:T(8,128)S(1)} %copy-done.4, f32[1024,1024]{0,1:T(8,128)} %get-tuple-element.61, ...), kind=kLoop, calls=%fused_computation.7 | loop fusion | flops 8388608 | bytes 20979712 | tf_op jit(solution)/shard_map/convert_element_type | solution.py:180
  372.6 9.4 %reduce-scatter.13.cloned.1.call-start = ((), (), s32[]{:S(2)}) async-start(), calls=%async_computation.14 | async-start | bytes 2359296 | tf_op jit(solution)/shard_map/reduce_scatter | solution.py:149
  395.7 3.9 convolution_convert_fusion.1
  399.7 4.0 convolution_convert_fusion.4
  408.2 2.7 convolution_convert_fusion
  410.9 3.0 collective-permute-start.1
  413.9 21.6 %collective-permute-done.1 = bf16[160,1024]{1,0:T(8,128)(2,1)S(1)} collective-permute-done((bf16[160,1024]{1,0:T(8,128)(2,1)}, bf16[160,1024]{1,0:T(8,128)(2,1)S(1)}, u32[]{:S(2)}, u32[]{:S(2)}) %collective-permute-start.1) | collective-permute-done | bytes 327712 | tf_op jit(solution)/shard_map/ppermute | solution.py:199
  437.0 12.9 %reduce-scatter.13.cloned.1.call-done = bf16[128,1024]{1,0:T(8,128)(2,1)} async-done(((bf16[1024,1024]{1,0:T(8,128)(2,1)}), bf16[128,1024]{1,0:T(8,128)(2,1)}) %reduce-scatter.13.cloned.1.call-update) | async-done | bytes 262160 | tf_op jit(solution)/shard_map/reduce_scatter | solution.py:149
  451.2 42.3 %psum.7 = f32[2304]{0:T(1024)S(1)} all-reduce(f32[2304]{0:T(1024)S(1)} %pad_maximum_fusion.14), channel_id=1, replica_groups=mesh['seq'=4,'ctx'=8] {'seq','ctx'}, use_global_device_ids=true, to_apply=%region_24.25 | all-reduce | flops 2304 | bytes 18432 | tf_op jit(solution)/shard_map/psum | solution.py:220
  494.1 10.5 %reduce-scatter.15.cloned.1.call-done = bf16[256,1280]{0,1:T(8,128)(2,1)} async-done(((bf16[1024,1280]{0,1:T(8,128)(2,1)}), bf16[256,1280]{0,1:T(8,128)(2,1)}) %reduce-scatter.15.cloned.1.call-update) | async-done | bytes 655376 | tf_op jit(solution)/shard_map/reduce_scatter | solution.py:207
  506.8 4.5 all-to-all-start.1
  511.9 37.4 %reduce-scatter.9.cloned.1.call-done = bf16[128,1024]{1,0:T(8,128)(2,1)} async-done(((bf16[1024,1024]{1,0:T(8,128)(2,1)}), bf16[128,1024]{1,0:T(8,128)(2,1)}) %reduce-scatter.9.cloned.1.call-update) | async-done | bytes 262160 | tf_op jit(solution)/shard_map/reduce_scatter | solution.py:149
  (230 shorter events, 69.5 us)
Async XLA Ops:
  7.2 81.0 %all-gather.19.cloned.1.call-start = ((), (), s32[]{:S(2)}) async-start(), calls=%async_computation.18 | async-start | bytes 1638400 | tf_op jit(solution)/shard_map/all_gather | solution.py:109
  8.3 8.7 %collective-permute-start = (bf16[160,1024]{1,0:T(8,128)(2,1)S(1)}, bf16[160,1024]{1,0:T(8,128)(2,1)S(1)}, u32[]{:S(2)}, u32[]{:S(2)}) collective-permute-start(bf16[160,1024]{1,0:T(8,128)(2,1)S(1)} %pad_maximum_fusion.13), channel_id=1, source_target_pairs={{0,0},{1,8},{2,16},{3,24},{4,1},{5,9},{6,17},{7,25},{8,2},{9,10},{... | collective-permute-start | bytes 983048 | tf_op jit(solution)/shard_map/ppermute | solution.py:109
  17.8 73.3 %all-gather.17.cloned.1.call-start = ((), (), s32[]{:S(2)}) async-start(), calls=%async_computation.17 | async-start | bytes 2359296 | tf_op jit(solution)/shard_map/all_gather | solution.py:119
  18.5 126.1 %all-gather.11.cloned.1.call-start = ((), (), s32[]{:S(2)}) async-start(), calls=%async_computation.8 | async-start | bytes 3276800 | tf_op jit(solution)/shard_map/all_gather | solution.py:107
  22.3 24.7 %copy-start.45 = (s32[1,1024]{1,0:T(1,128)S(1)}, s32[1,1024]{1,0:T(1,128)}, u32[]{:S(2)}) copy-start(s32[1,1024]{1,0:T(1,128)} %param.15) | copy-start | bytes 12292
  22.3 24.8 %copy-start.46 = (bf16[4]{0:T(256)(128)(2,1)S(1)}, bf16[4]{0:T(256)(128)(2,1)}, u32[]{:S(2)}) copy-start(bf16[4]{0:T(256)(128)(2,1)} %param.21) | copy-start | bytes 28
  22.3 24.8 %copy-start.47 = (bf16[4]{0:T(256)(128)(2,1)S(1)}, bf16[4]{0:T(256)(128)(2,1)}, u32[]{:S(2)}) copy-start(bf16[4]{0:T(256)(128)(2,1)} %param.20) | copy-start | bytes 28
  22.3 24.8 %copy-start.48 = (bf16[32]{0:T(256)(128)(2,1)S(1)}, bf16[32]{0:T(256)(128)(2,1)}, u32[]{:S(2)}) copy-start(bf16[32]{0:T(256)(128)(2,1)} %param.23) | copy-start | bytes 196
  22.3 24.8 %copy-start.49 = (bf16[32]{0:T(256)(128)(2,1)S(1)}, bf16[32]{0:T(256)(128)(2,1)}, u32[]{:S(2)}) copy-start(bf16[32]{0:T(256)(128)(2,1)} %param.16) | copy-start | bytes 196
  46.9 158.9 %reduce-scatter.7.cloned.1.call-start = ((), (), s32[]{:S(2)}) async-start(), calls=%async_computation.9 | async-start | bytes 2359296 | tf_op jit(solution)/shard_map/reduce_scatter | solution.py:149
  89.3 71.6 %copy-start.27 = (bf16[4,64,1024]{2,1,0:T(8,128)(2,1)}, bf16[4,64,1024]{2,1,0:T(8,128)(2,1)S(1)}, u32[]{:S(2)}) copy-start(bf16[4,64,1024]{2,1,0:T(8,128)(2,1)S(1)} %slice.126) | copy-start | bytes 1572868
  91.1 53.6 %copy-start.25 = (bf16[1,1024,1024]{2,1,0:T(8,128)(2,1)S(1)}, bf16[1,1024,1024]{2,1,0:T(8,128)(2,1)}, u32[]{:S(2)}) copy-start(bf16[1,1024,1024]{2,1,0:T(8,128)(2,1)} %all-gather.17.cloned.1.call-done) | copy-start | bytes 6291460
  161.6 44.2 %copy-start.10 = (bf16[1,128,1024]{2,1,0:T(8,128)(2,1)S(1)}, bf16[1,128,1024]{2,1,0:T(8,128)(2,1)}, u32[]{:S(2)}) copy-start(bf16[1,128,1024]{2,1,0:T(8,128)(2,1)} %param.14) | copy-start | bytes 786436
  163.8 45.7 %copy-start.30 = (bf16[640,1024]{1,0:T(8,128)(2,1)S(1)}, bf16[640,1024]{1,0:T(8,128)(2,1)}, u32[]{:S(2)}) copy-start(bf16[640,1024]{1,0:T(8,128)(2,1)} %all-gather.19.cloned.1.call-done) | copy-start | bytes 3932164
  163.8 73.5 %all-gather.13.cloned.1.call-start = ((), (), s32[]{:S(2)}) async-start(), calls=%async_computation.10 | async-start | bytes 2359296 | tf_op jit(solution)/shard_map/all_gather | solution.py:155
  208.8 58.0 %all-gather.21.cloned.1.call-start = ((), (), s32[]{:S(2)}) async-start(), calls=%async_computation.19 | async-start | bytes 2359296 | tf_op jit(solution)/shard_map/all_gather | solution.py:120
  209.4 106.8 %reduce-scatter.11.cloned.1.call-start = ((), (), s32[]{:S(2)}) async-start(), calls=%async_computation.12 | async-start | bytes 2359296 | tf_op jit(solution)/shard_map/reduce_scatter | solution.py:149
  209.5 57.3 %copy-start.36 = (bf16[4,96,1024]{2,1,0:T(8,128)(2,1)}, bf16[4,96,1024]{2,1,0:T(8,128)(2,1)S(1)}, u32[]{:S(2)}) copy-start(bf16[4,96,1024]{2,1,0:T(8,128)(2,1)S(1)} %slice.131) | copy-start | bytes 2359300
  271.0 48.4 %copy-start.52 = (bf16[1024,384]{0,1:T(8,128)(2,1)}, bf16[1024,384]{0,1:T(8,128)(2,1)S(1)}, u32[]{:S(2)}) copy-start(bf16[1024,384]{0,1:T(8,128)(2,1)S(1)} %get-tuple-element.31) | copy-start | bytes 2359300
  275.4 40.7 %copy-start.11 = (bf16[128,1024]{1,0:T(8,128)(2,1)S(1)}, bf16[128,1024]{1,0:T(8,128)(2,1)}, u32[]{:S(2)}) copy-start(bf16[128,1024]{1,0:T(8,128)(2,1)} %reduce-scatter.7.cloned.1.call-done) | copy-start | bytes 786436
  275.4 42.0 %copy-start.20 = (bf16[1,128,1024]{2,1,0:T(8,128)(2,1)S(1)}, bf16[1,128,1024]{2,1,0:T(8,128)(2,1)}, u32[]{:S(2)}) copy-start(bf16[1,128,1024]{2,1,0:T(8,128)(2,1)} %param.27) | copy-start | bytes 786436
  275.4 72.4 %all-gather.15.cloned.1.call-start = ((), (), s32[]{:S(2)}) async-start(), calls=%async_computation.13 | async-start | bytes 2359296 | tf_op jit(solution)/shard_map/all_gather | solution.py:170
  319.3 91.6 %reduce-scatter.17.cloned.1.call-start = ((), (), s32[]{:S(2)}) async-start(), calls=%async_computation.16 | async-start | bytes 1638400 | tf_op jit(solution)/shard_map/reduce_scatter | solution.py:198
  319.4 28.4 %copy-start.28 = (bf16[4,64,1024]{2,1,0:T(8,128)(2,1)S(1)}, bf16[4,64,1024]{2,1,0:T(8,128)(2,1)}, u32[]{:S(2)}) copy-start(bf16[4,64,1024]{2,1,0:T(8,128)(2,1)} %copy-done.27) | copy-start | bytes 1572868
  372.6 77.3 %reduce-scatter.13.cloned.1.call-start = ((), (), s32[]{:S(2)}) async-start(), calls=%async_computation.14 | async-start | bytes 2359296 | tf_op jit(solution)/shard_map/reduce_scatter | solution.py:149
  399.6 105.0 %reduce-scatter.15.cloned.1.call-start = ((), (), s32[]{:S(2)}) async-start(), calls=%async_computation.15 | async-start | bytes 3276800 | tf_op jit(solution)/shard_map/reduce_scatter | solution.py:207
  406.9 142.4 %reduce-scatter.9.cloned.1.call-start = ((), (), s32[]{:S(2)}) async-start(), calls=%async_computation.11 | async-start | bytes 2359296 | tf_op jit(solution)/shard_map/reduce_scatter | solution.py:149
  410.9 24.6 %collective-permute-start.1 = (bf16[160,1024]{1,0:T(8,128)(2,1)}, bf16[160,1024]{1,0:T(8,128)(2,1)S(1)}, u32[]{:S(2)}, u32[]{:S(2)}) collective-permute-start(bf16[160,1024]{1,0:T(8,128)(2,1)} %reduce-scatter.17.cloned.1.call-done), channel_id=1, source_target_pairs={{0,0},{8,1},{16,2},{24,3},{1,4},{9,5},{17,6},{25,7},{2,8},{10,9},{... | collective-permute-start | bytes 983048 | tf_op jit(solution)/shard_map/ppermute | solution.py:199
  436.2 113.1 %copy-start.21 = (bf16[1,128,1024]{2,1,0:T(8,128)(2,1)S(1)}, bf16[1,128,1024]{2,1,0:T(8,128)(2,1)}, u32[]{:S(2)}) copy-start(bf16[1,128,1024]{2,1,0:T(8,128)(2,1)} %param.27) | copy-start | bytes 786436
  436.2 113.1 %copy-start.22 = (bf16[128,1024]{1,0:T(8,128)(2,1)S(1)}, bf16[128,1024]{1,0:T(8,128)(2,1)}, u32[]{:S(2)}) copy-start(bf16[128,1024]{1,0:T(8,128)(2,1)} %reduce-scatter.11.cloned.1.call-done) | copy-start | bytes 786436
  449.9 99.4 %copy-start.35 = (bf16[128,1024]{1,0:T(8,128)(2,1)S(1)}, bf16[128,1024]{1,0:T(8,128)(2,1)}, u32[]{:S(2)}) copy-start(bf16[128,1024]{1,0:T(8,128)(2,1)} %reduce-scatter.13.cloned.1.call-done) | copy-start | bytes 786436
  506.8 44.8 %all-to-all-start.1 = ((bf16[8,32,1280]{2,1,0:T(8,128)(2,1)}), bf16[8,32,1280]{2,1,0:T(8,128)(2,1)S(1)}, u32[]{:S(2)}, u32[]{:S(2)}) async-start(bf16[8,32,1280]{2,1,0:T(8,128)(2,1)} %bitcast.35), calls=%async_computation.6 | async-start | bytes 1310720 | tf_op jit(solution)/shard_map/all_to_all | solution.py:209
  (39 other events, 117.6 us)
Sparse Core Ops, SparseCore 0:
  17.9 42.3 all-gather.18
  62.2 28.8 all-gather.16
  92.6 51.9 all-gather.10
  163.9 41.9 reduce-scatter.6
  208.9 28.3 all-gather.12
  239.0 27.7 all-gather.20
  275.6 40.5 reduce-scatter.10
  319.5 28.3 all-gather.14
  372.7 28.7 reduce-scatter.16
  404.6 45.2 reduce-scatter.12
  452.2 52.2 reduce-scatter.14
  507.7 41.5 reduce-scatter.8

commit v2 on v1

--- a/solution.py
+++ b/solution.py
@@ -1,6 +1,11 @@
+import types
+
 import jax
 import jax.numpy as jnp
+import numpy as np
 from jax import lax
+from jax.experimental import pallas as pl
+from jax.experimental.pallas import tpu as pltpu
 from jax.sharding import PartitionSpec as P
 
 QUERY_HEAD_COUNT = 16
@@ -12,10 +17,844 @@
 NEGATIVE = -1e30
 BF = jnp.bfloat16
 F32 = jnp.float32
+MESH = pl.DeviceIdType.MESH
+RUN = 64
+BLOCK = 256
+
+
+def nn(a, b):
+    return jnp.dot(a, b, preferred_element_type=F32)
+
+
+def nt(a, b):
+    return lax.dot_general(a, b, (((1,), (1,)), ((), ())), preferred_element_type=F32)
+
+
+def tn(a, b):
+    return lax.dot_general(a, b, (((0,), (0,)), ((), ())), preferred_element_type=F32)
+
+
+def loop(low, high, body):
+    def step(i, carry):
+        body(i)
+        return carry
+
+    lax.fori_loop(low, high, step, 0)
+
+
+def rows_of(start, size):
+    return pl.ds(pl.multiple_of(start, size), size)
 
 
 def inverse_root(values):
     return lax.rsqrt(jnp.mean(values * values, axis=-1, keepdims=True) + EPS)
+
+
+def norm_backward(normed_grad, normed, inverse):
+    return inverse * (normed_grad - normed * jnp.mean(normed_grad * normed, axis=-1, keepdims=True))
+
+
+def layer_kernel(dims, refs):
+    S, C, T, L, D = dims.S, dims.C, dims.T, dims.L, dims.D
+    H, RW, OR, DR, AC, U = dims.H, dims.RW, dims.OR, dims.DR, dims.AC, dims.U
+    HD = HEAD_DIMENSION
+    PR = C * RW
+    NR = L // RUN
+    NB = L // BLOCK
+    CH = C // 2
+    scale = HD ** (-0.5)
+    r = refs
+    s = lax.axis_index("seq")
+    c = lax.axis_index("ctx")
+    chip = lax.div(c, 2)
+    core = lax.rem(c, 2)
+    chip_y, chip_x = lax.div(chip, 2), lax.rem(chip, 2)
+    sibling = chip * 2 + (1 - core)
+    flat = s * C + c
+    to_s, to_c = lax.rem(flat, S), lax.div(flat, S)
+    from_flat = S * c + s
+    from_s, from_c = lax.div(from_flat, C), lax.rem(from_flat, C)
+    moved = (to_s * C + to_c) != flat
+
+    def partner(i):
+        x = lax.rem(chip_x + lax.rem(i, 2), 2)
+        y = lax.rem(chip_y + lax.div(i, 2), 2)
+        return y * 2 + x
+
+    def remote(src, dst, send, recv, **where):
+        return pltpu.make_async_remote_copy(
+            src_ref=src, dst_ref=dst, send_sem=send, recv_sem=recv, device_id=where, device_id_type=MESH
+        )
+
+    def local(src, dst, sem):
+        return pltpu.make_async_copy(src, dst, sem)
+
+    def arrived(dst, sem):
+        pltpu.make_async_copy(dst, dst, sem).wait()
+
+    barrier = pltpu.get_barrier_semaphore()
+
+    def hello(**where):
+        pl.semaphore_signal(barrier, inc=1, device_id=where, device_id_type=MESH)
+
+    loop(1, C, lambda i: hello(ctx=lax.rem(c + i, C)))
+    loop(1, S, lambda i: hello(seq=lax.rem(s + i, S)))
+
+    @pl.when(moved)
+    def _():
+        hello(seq=to_s, ctx=to_c)
+        hello(seq=from_s, ctx=from_c)
+
+    @pl.when(moved)
+    def _():
+        pl.semaphore_wait(barrier, C + S)
+
+    @pl.when(jnp.logical_not(moved))
+    def _():
+        pl.semaphore_wait(barrier, C + S - 2)
+
+    def runs_of(b):
+        return pl.ds(b * (BLOCK // RUN), BLOCK // RUN)
+
+    def own_x():
+        return r.x_all[pl.ds(c * (T // RUN), T // RUN)].reshape(T, D).astype(F32)
+
+    X, G, H2, DY = 0, 1, 2, 3
+    whole = {X: r.x_all, G: r.g_all, H2: r.h2_all, DY: r.dy_all}
+
+    def block(kind, j):
+        if kind == X:
+            return whole[kind].at[pl.ds(j * (T // RUN), T // RUN)]
+        return whole[kind].at[rows_of(j * T, T)]
+
+    def gather_send(kind, src):
+        def go(i):
+            remote(src, block(kind, c), r.ag_send.at[kind, i], r.ag_recv.at[kind, c],
+                   ctx=partner(i) * 2 + core).start()
+
+        loop(1, CH, go)
+        remote(src, block(kind, c), r.ag_send.at[kind, 0], r.ag_recv.at[kind, c], ctx=sibling).start()
+
+    def gather_relay(kind, i):
+        j = partner(i) * 2 + core
+        arrived(block(kind, j), r.ag_recv.at[kind, j])
+        remote(block(kind, j), block(kind, j), r.ag_send.at[kind, CH - 1 + i], r.ag_recv.at[kind, j],
+               ctx=sibling).start()
+
+    def gather_other(kind, i):
+        j = partner(i) * 2 + (1 - core)
+        arrived(block(kind, j), r.ag_recv.at[kind, j])
+
+    def gather_done(kind):
+        def go(i):
+            arrived(block(kind, c), r.ag_send.at[kind, i])
+
+        loop(0, 2 * CH - 1, go)
+
+    def scatter_pair(kind, i, partial):
+        r.pair[i] = partial
+        r.s1[i] = r.pair[i, rows_of((1 - core) * T, T), :].astype(BF)
+        remote(r.s1.at[i], r.r1.at[1 if kind == 1 else 0, i], r.rs_send.at[kind, i],
+               r.r1_recv.at[kind, i], ctx=sibling).start()
+
+    def scatter_chips(kind):
+        bank = 1 if kind == 1 else 0
+
+        def go(i):
+            arrived(r.r1.at[bank, i], r.r1_recv.at[kind, i])
+            mine = r.pair[i, rows_of(core * T, T), :] + r.r1[bank, i].astype(F32)
+            r.s2[i] = mine.astype(BF)
+            remote(r.s2.at[i], r.r2.at[bank, i], r.rs_send.at[kind, CH + i],
+                   r.r2_recv.at[kind, i], ctx=partner(i) * 2 + core).start()
+
+        loop(1, CH, go)
+
+    def scatter_sum(kind):
+        bank = 1 if kind == 1 else 0
+        arrived(r.r1.at[bank, 0], r.r1_recv.at[kind, 0])
+        total = r.pair[0, rows_of(core * T, T), :] + r.r1[bank, 0].astype(F32)
+        for i in range(1, CH):
+            arrived(r.r2.at[bank, i], r.r2_recv.at[kind, i])
+            total = total + r.r2[bank, i].astype(F32)
+        return total
+
+    def scatter_done(kind):
+        loop(0, CH, lambda i: arrived(r.s1.at[0], r.rs_send.at[kind, i]))
+        loop(1, CH, lambda i: arrived(r.s2.at[1], r.rs_send.at[kind, CH + i]))
+
+    QKV, OUT, GU, DOWN = 0, 1, 2, 3
+    held = {QKV: (r.w_qkv, PR), OUT: (r.w_o, OR), GU: (r.w_gu, PR), DOWN: (r.w_d, DR)}
+
+    def plane(w, b):
+        ref, size = held[w]
+        return ref.at[rows_of(b * size, size)]
+
+    def weight_start(w):
+        @pl.when(s < S - 1)
+        def _():
+            remote(plane(w, s), plane(w, s), r.z_send.at[w, 0, 0], r.z_recv.at[w, s], seq=s + 1).start()
+
+        @pl.when(s > 0)
+        def _():
+            remote(plane(w, s), plane(w, s), r.z_send.at[w, 1, 0], r.z_recv.at[w, s], seq=s - 1).start()
+
+    def weight_hop(w, t):
+        below, above = s - 1 - t, s + 1 + t
+
+        @pl.when(below >= 0)
+        def _():
+            arrived(plane(w, below), r.z_recv.at[w, below])
+
+            @pl.when(s < S - 1)
+            def _():
+                remote(plane(w, below), plane(w, below), r.z_send.at[w, 0, t + 1],
+                       r.z_recv.at[w, below], seq=s + 1).start()
+
+        @pl.when(above <= S - 1)
+        def _():
+            arrived(plane(w, above), r.z_recv.at[w, above])
+
+            @pl.when(s > 0)
+            def _():
+                remote(plane(w, above), plane(w, above), r.z_send.at[w, 1, t + 1],
+                       r.z_recv.at[w, above], seq=s - 1).start()
+
+    def weight_done(w):
+        for t in range(S - 1):
+            @pl.when(jnp.logical_and(s - t >= 0, s < S - 1))
+            def _():
+                arrived(plane(w, s), r.z_send.at[w, 0, t])
+
+            @pl.when(jnp.logical_and(s + t <= S - 1, s > 0))
+            def _():
+                arrived(plane(w, s), r.z_send.at[w, 1, t])
+
+    sent = {QKV: (r.g_qkv, PR), OUT: (r.g_o, OR), GU: (r.g_gu, PR), DOWN: (r.g_d, DR)}
+    got = {QKV: r.t_qkv, OUT: r.t_o, GU: r.t_gu, DOWN: r.t_d}
+    summed = {QKV: r.u_qkv, OUT: r.u_o, GU: r.u_gu, DOWN: r.u_d}
+
+    def grad_send(w, i, p):
+        ref, size = sent[w]
+        remote(ref.at[rows_of(p * size, size)], got[w].at[s], r.gz_send.at[w, i], r.gz_recv.at[w, s],
+               seq=p).start()
+
+    def grad_sum(w):
+        ref, size = sent[w]
+        total = ref[rows_of(s * size, size), :].astype(F32)
+        for i in range(1, S):
+            p = lax.rem(s + i, S)
+            arrived(got[w].at[p], r.gz_recv.at[w, p])
+            total = total + got[w][p].astype(F32)
+        summed[w][...] = total.astype(BF)
+
+    def grad_done(w):
+        loop(1, S, lambda i: arrived(got[w].at[0], r.gz_send.at[w, i]))
+
+    final = {QKV: r.f_qkv, GU: r.f_gu, OUT: r.f_o, DOWN: r.f_d}
+
+    def columns_send(n, w):
+        def go(i):
+            j = lax.rem(c + i, C)
+            remote(summed[w].at[rows_of(j * RW, RW)], final[w].at[c], r.gp_send.at[n, i],
+                   r.gp_recv.at[n, c], ctx=j).start()
+
+        loop(1, C, go)
+        final[w][c] = summed[w][rows_of(c * RW, RW), :]
+
+    def columns_arrive(n, w):
+        loop(1, C, lambda i: arrived(final[w].at[lax.rem(c + i, C)], r.gp_recv.at[n, lax.rem(c + i, C)]))
+
+    def columns_done(n, w):
+        loop(1, C, lambda i: arrived(final[w].at[0], r.gp_send.at[n, i]))
+
+    def rows_send(n, w):
+        @pl.when(moved)
+        def _():
+            remote(summed[w], final[w], r.row_send.at[n], r.row_recv.at[n], seq=from_s, ctx=from_c).start()
+
+        @pl.when(jnp.logical_not(moved))
+        def _():
+            final[w][...] = summed[w][...]
+
+    def rows_arrive(n, w):
+        @pl.when(moved)
+        def _():
+            arrived(final[w], r.row_recv.at[n])
+
+    def rows_done(n, w):
+        @pl.when(moved)
+        def _():
+            arrived(final[w], r.row_send.at[n])
+
+    gains_own = r.gains_all.at[flat]
+    gain_copy = local(r.gains_in, gains_own, r.gain_recv.at[s])
+    gain_copy.start()
+
+    def gain_go(i):
+        remote(r.gains_in, gains_own, r.gain_send.at[i], r.gain_recv.at[s],
+               ctx=lax.rem(c + i, C)).start()
+
+    loop(1, C, gain_go)
+
+    def qkv_piece(j):
+        return (
+            (r.wq_in.at[:, rows_of(j * H * HD, H * HD)], slice(0, H * HD)),
+            (r.wk_in.at[:, rows_of(j * HD, HD)], slice(H * HD, (H + 1) * HD)),
+            (r.wv_in.at[:, rows_of(j * HD, HD)], slice((H + 1) * HD, (H + 2) * HD)),
+        )
+
+    def gu_piece(j):
+        return (
+            (r.wg_in.at[:, rows_of(j * U, U)], slice(0, U)),
+            (r.wu_in.at[:, rows_of(j * U, U)], slice(U, 2 * U)),
+        )
+
+    def spread(n, w, piece):
+        ref = held[w][0]
+        own = rows_of(s * PR + c * RW, RW)
+
+        def go(i):
+            j = lax.rem(c + i, C)
+            for src, columns in piece(j):
+                remote(src, ref.at[own, columns], r.w_send.at[n], r.w_recv.at[n], ctx=j).start()
+
+        loop(1, C, go)
+        for src, columns in piece(c):
+            local(src, ref.at[own, columns], r.w_recv.at[n]).start()
+
+    def spread_arrive(n, w):
+        arrived(plane(w, s), r.w_recv.at[n])
+
+    def spread_done(n, w):
+        ref = held[w][0]
+        arrived(ref.at[pl.ds(0, (C - 1) * RW)], r.w_send.at[n])
+
+    def move(n, w, src):
+        @pl.when(moved)
+        def _():
+            remote(src, held[w][0].at[rows_of(to_s * held[w][1], held[w][1])], r.m_send.at[n],
+                   r.m_recv.at[n], seq=to_s, ctx=to_c).start()
+
+        @pl.when(jnp.logical_not(moved))
+        def _():
+            local(src, plane(w, s), r.m_recv.at[n]).start()
+
+    def move_arrive(n, w):
+        arrived(plane(w, s), r.m_recv.at[n])
+
+    def move_done(n, w):
+        @pl.when(moved)
+        def _():
+            arrived(plane(w, s), r.m_send.at[n])
+
+    spread(0, QKV, qkv_piece)
+    local(r.x_in, block(X, c), r.local_sem.at[0]).start()
+    local(r.table_in, r.table, r.local_sem.at[1]).start()
+    gather_send(X, r.x_in)
+    move(0, OUT, r.wo_in)
+
+    arrived(r.gains_all.at[pl.ds(s * C, C)], r.gain_recv.at[s])
+
+    def gain_far(i):
+        mine = r.gains_all.at[pl.ds(s * C, C)]
+        remote(mine, mine, r.gain_send.at[C + i], r.gain_recv.at[s], seq=lax.rem(s + i, S)).start()
+
+    loop(1, S, gain_far)
+    spread_arrive(0, QKV)
+    weight_start(QKV)
+    move_arrive(0, OUT)
+    weight_start(OUT)
+    spread(1, GU, gu_piece)
+    move(1, DOWN, r.wd_in)
+
+    arrived(r.table, r.local_sem.at[1])
+
+    def tables(b):
+        rows = rows_of(b * T, T)
+        both = r.table[rows, :]
+        other = pltpu.roll(both, HD // 2, 1)
+        first = lax.broadcasted_iota(jnp.int32, (T, HD), 1) < HD // 2
+        r.cosine[rows, :] = jnp.where(first, both, other)
+        r.sine[rows, :] = jnp.where(first, -other, both)
+
+    loop(0, L // T, tables)
+
+    def gain_block(i):
+        p = lax.rem(s + i, S)
+        arrived(r.gains_all.at[pl.ds(p * C, C)], r.gain_recv.at[p])
+
+    loop(1, S, gain_block)
+    gains = jnp.sum(r.gains_all[...], axis=1).astype(BF)
+
+    def gain_vector(offset, count):
+        width = count * S * C
+        shift = count.bit_length() - 1
+        column = lax.broadcasted_iota(jnp.int32, (HD, width), 1)
+        row = lax.broadcasted_iota(jnp.int32, (HD, width), 0)
+        pick = jnp.where(row == offset + (column & (count - 1)), 1.0, 0.0).astype(BF)
+        spread_out = nn(gains, pick)
+        owner = lax.broadcasted_iota(jnp.int32, (S * C, width), 0)
+        place = lax.broadcasted_iota(jnp.int32, (S * C, width), 1) >> shift
+        return jnp.sum(jnp.where(owner == place, spread_out, 0.0), axis=0, keepdims=True)
+
+    n1 = D // (S * C)
+    n3 = HD // (S * C)
+    r.gain1[...] = gain_vector(0, n1)
+    r.gain2[...] = gain_vector(n1, n1)
+    r.gainq[...] = gain_vector(2 * n1, n3)
+    r.gaink[...] = gain_vector(2 * n1 + n3, n3)
+
+    arrived(block(X, c), r.local_sem.at[0])
+    loop(1, CH, lambda i: gather_relay(X, i))
+    arrived(block(X, sibling), r.ag_recv.at[X, sibling])
+    loop(1, CH, lambda i: gather_other(X, i))
+    weight_hop(QKV, 0)
+    local(r.g_in, block(G, c), r.local_sem.at[2]).start()
+    gather_send(G, r.g_in)
+
+    def first_norm(k):
+        x = r.x_all[r.order[1, k]].astype(F32)
+        r.h1[rows_of(k * RUN, RUN), :] = (x * inverse_root(x) * r.gain1[...]).astype(BF)
+
+    loop(0, NR, first_norm)
+    weight_hop(OUT, 0)
+    weight_hop(QKV, 1)
+    weight_hop(OUT, 1)
+    spread_arrive(1, GU)
+    weight_start(GU)
+    weight_hop(QKV, 2)
+    weight_hop(OUT, 2)
+
+    def rotate(u, rows):
+        return u * r.cosine[rows, :] + pltpu.roll(u, HD // 2, 1) * r.sine[rows, :]
+
+    def rotate_back(u, rows):
+        return u * r.cosine[rows, :] - pltpu.roll(u, HD // 2, 1) * r.sine[rows, :]
+
+    def project(b):
+        rows = rows_of(b * BLOCK, BLOCK)
+        acc = nn(r.h1[rows, :], r.w_qkv[...])
+        for h in range(H):
+            u = acc[:, h * HD : (h + 1) * HD]
+            r.q_lin[h, rows, :] = u
+            r.q_rot[h, rows, :] = rotate(u * inverse_root(u) * r.gainq[...], rows).astype(BF)
+        u = acc[:, H * HD : (H + 1) * HD]
+        r.k_lin[rows, :] = u
+        k = rotate(u * inverse_root(u) * r.gaink[...], rows)
+        r.k_rot[rows, :] = k.astype(BF)
+        r.k_t[:, rows] = k.T.astype(BF)
+        v = acc[:, (H + 1) * HD :]
+        r.v[rows, :] = v.astype(BF)
+        r.v_t[:, rows] = v.T.astype(BF)
+
+    loop(0, NB, project)
+    gather_relay_g = lambda i: gather_relay(G, i)
+    loop(1, CH, gather_relay_g)
+
+    def attend(qb):
+        cols = rows_of(qb * BLOCK, BLOCK)
+
+        def keys(kb, carry):
+            rows = rows_of(kb * BLOCK, BLOCK)
+            key = r.k_rot[rows, :]
+            value_t = r.v_t[:, rows]
+            ahead = lax.broadcasted_iota(jnp.int32, (BLOCK, BLOCK), 0) - lax.broadcasted_iota(
+                jnp.int32, (BLOCK, BLOCK), 1
+            )
+            allowed = ahead <= (qb - kb) * BLOCK
+            out = []
+            for h in range(H):
+                acc, total = carry[2 * h], carry[2 * h + 1]
+                e = jnp.exp(nt(key, r.q_rot[h, cols, :]) * scale)
+                e = jnp.where(allowed, e, 0.0)
+                low = e.astype(BF)
+                r.e[h, rows, cols] = low
+                out += [acc + nn(value_t, low), total + jnp.sum(e, axis=0, keepdims=True)]
+            return tuple(out)
+
+        zero = (jnp.zeros((HD, BLOCK), F32), jnp.zeros((1, BLOCK), F32)) * H
+        done = lax.fori_loop(0, qb + 1, keys, zero)
+        for h in range(H):
+            inverse = 1.0 / done[2 * h + 1]
+            o = done[2 * h] * inverse
+            r.l_inv[h, :, cols] = jnp.broadcast_to(inverse, (8, BLOCK))
+            r.o_t[h, :, cols] = o
+            r.o_sorted[runs_of(qb), :, h * HD : (h + 1) * HD] = o.T.astype(BF).reshape(-1, RUN, HD)
+
+    loop(0, NB, attend)
+    weight_hop(GU, 0)
+    move_arrive(1, DOWN)
+    weight_start(DOWN)
+
+    def unsort(i):
+        r.o[rows_of(i * RUN, RUN), :] = r.o_sorted[r.order[0, i]]
+
+    loop(0, NR, unsort)
+
+    def out_chip(i):
+        scatter_pair(0, i, nn(r.o[rows_of(partner(i) * 2 * T, 2 * T), :], r.w_o[...]))
+
+    loop(0, CH, out_chip)
+    scatter_chips(0)
+    weight_hop(GU, 1)
+    y1 = own_x() + scatter_sum(0)
+    scatter_done(0)
+    r.y1[...] = y1
+    h2_own = (y1 * inverse_root(y1) * r.gain2[...]).astype(BF)
+    r.h2_all[rows_of(c * T, T), :] = h2_own
+    gather_send(H2, block(H2, c))
+
+    weight_hop(GU, 2)
+    weight_hop(DOWN, 0)
+    weight_hop(DOWN, 1)
+    arrived(block(G, c), r.local_sem.at[2])
+    arrived(block(G, sibling), r.ag_recv.at[G, sibling])
+    loop(1, CH, lambda i: gather_other(G, i))
+    weight_hop(DOWN, 2)
+
+    def act_grad(b):
+        rows = rows_of(b * BLOCK, BLOCK)
+        r.d_act[rows, :] = nt(r.g_all[rows, :], r.w_d[...])
+
+    loop(0, NB, act_grad)
+    arrived(block(H2, sibling), r.ag_recv.at[H2, sibling])
+
+    def feed(i):
+        @pl.when(i > 0)
+        def _():
+            gather_relay(H2, i)
+            gather_other(H2, i)
+
+        rows = rows_of(partner(i) * 2 * T, 2 * T)
+        h2 = r.h2_all[rows, :]
+        gate = nn(h2, r.w_gu[:, :U])
+        up = nn(h2, r.w_gu[:, U:])
+        sig = 1.0 / (1.0 + jnp.exp(-gate))
+        silu = gate * sig
+        r.act[rows, :] = (silu * up).astype(BF)
+        d_act = r.d_act[rows, :]
+        d_gate = (d_act * up * sig * (1.0 + gate * (1.0 - sig))).astype(BF)
+        d_up = (d_act * silu).astype(BF)
+        r.d_gu[rows, :U] = d_gate
+        r.d_gu[rows, U:] = d_up
+        scatter_pair(2, i, nt(r.d_gu[rows, :], r.w_gu[...]))
+
+    loop(0, CH, feed)
+    scatter_chips(2)
+
+    def down_grad(m):
+        cols = rows_of(m * HD, HD)
+        r.g_d[cols, :] = tn(r.act[:, cols], r.g_all[...]).astype(BF)
+
+    loop(0, U // HD, down_grad)
+    loop(1, S, lambda i: grad_send(DOWN, i, lax.rem(s + i, S)))
+
+    def gu_grad(i):
+        p = lax.rem(s + i, S)
+        cols = rows_of(p * PR, PR)
+        r.g_gu[cols, :] = tn(r.h2_all[:, cols], r.d_gu[...]).astype(BF)
+
+        @pl.when(i < S)
+        def _():
+            grad_send(GU, i, p)
+
+    loop(1, S + 1, gu_grad)
+
+    d_h2 = scatter_sum(2)
+    scatter_done(2)
+    y1 = r.y1[...]
+    r2 = inverse_root(y1)
+    normed = y1 * r2
+    term2 = jnp.sum(d_h2 * normed, axis=0, keepdims=True)
+    d_y1 = r.g_all[rows_of(c * T, T), :].astype(F32) + norm_backward(d_h2 * r.gain2[...], normed, r2)
+    r.d_y1[...] = d_y1
+    r.dy_all[rows_of(c * T, T), :] = d_y1.astype(BF)
+    gather_send(DY, block(DY, c))
+    WT = D // HD
+    for k in range(WT):
+        r.terms[WT + k : WT + k + 1, :] = term2[:, k * HD : (k + 1) * HD]
+
+    def last_chip(i):
+        scatter_pair(1, i, nn(r.act[rows_of(partner(i) * 2 * T, 2 * T), :], r.w_d[...]))
+
+    loop(0, CH, last_chip)
+    arrived(block(DY, sibling), r.ag_recv.at[DY, sibling])
+
+    def out_grad(i):
+        @pl.when(i > 0)
+        def _():
+            gather_relay(DY, i)
+            gather_other(DY, i)
+
+        rows = rows_of(partner(i) * 2 * T, 2 * T)
+        d_o = nt(r.dy_all[rows, :], r.w_o[...]).astype(BF)
+        r.d_o[pl.ds(partner(i) * (2 * T // RUN), 2 * T // RUN)] = d_o.reshape(-1, RUN, H * HD)
+
+    loop(0, CH, out_grad)
+    scatter_chips(1)
+
+    def out_weight(m):
+        cols = rows_of(m * HD, HD)
+        r.g_o[cols, :] = tn(r.o[:, cols], r.dy_all[...]).astype(BF)
+
+    loop(0, H * HD // HD, out_weight)
+    loop(1, S, lambda i: grad_send(OUT, i, lax.rem(s + i, S)))
+
+    def sort(k):
+        r.d_o_sorted[rows_of(k * RUN, RUN), :] = r.d_o[r.order[1, k]]
+
+    loop(0, NR, sort)
+    r.d_k[...] = jnp.zeros_like(r.d_k)
+    r.d_v[...] = jnp.zeros_like(r.d_v)
+    r.sums[...] = jnp.zeros_like(r.sums)
+
+    def attend_back(qb):
+        cols = rows_of(qb * BLOCK, BLOCK)
+        d_o_t, d_o_low, row, factor = [], [], [], []
+        for h in range(H):
+            t = r.d_o_sorted[cols, h * HD : (h + 1) * HD].astype(F32).T
+            inverse = r.l_inv[h, 0:1, cols]
+            row.append(jnp.sum(t * r.o_t[h, :, cols], axis=0, keepdims=True))
+            factor.append(inverse * scale)
+            r.do_t[h] = t.astype(BF)
+            r.do_l[h] = (t * inverse).T.astype(BF)
+
+        def keys(kb, carry):
+            rows = rows_of(kb * BLOCK, BLOCK)
+            value = r.v[rows, :]
+            key_t = r.k_t[:, rows]
+            out = []
+            d_k = r.d_k[rows, :]
+            d_v = r.d_v[rows, :]
+            for h in range(H):
+                e = r.e[h, rows, cols]
+                dp = nn(value, r.do_t[h])
+                de = (e.astype(F32) * ((dp - row[h]) * factor[h])).astype(BF)
+                out.append(carry[h] + nn(key_t, de))
+                d_k = d_k + nn(de, r.q_rot[h, cols, :])
+                d_v = d_v + nn(e, r.do_l[h])
+            r.d_k[rows, :] = d_k
+            r.d_v[rows, :] = d_v
+            return tuple(out)
+
+        done = lax.fori_loop(0, qb + 1, keys, (jnp.zeros((HD, BLOCK), F32),) * H)
+        for h in range(H):
+            d_g = rotate_back(done[h].T, cols)
+            u = r.q_lin[h, cols, :]
+            inverse = inverse_root(u)
+            normed = u * inverse
+            r.sums[0:1, :] += jnp.sum(d_g * normed, axis=0, keepdims=True)
+            d_lin = norm_backward(d_g * r.gainq[...], normed, inverse).astype(BF)
+            r.d_qkv[runs_of(qb), :, h * HD : (h + 1) * HD] = d_lin.reshape(-1, RUN, HD)
+
+    loop(0, NB, attend_back)
+
+    def key_back(b):
+        rows = rows_of(b * BLOCK, BLOCK)
+        d_g = rotate_back(r.d_k[rows, :], rows)
+        u = r.k_lin[rows, :]
+        inverse = inverse_root(u)
+        normed = u * inverse
+        r.sums[1:2, :] += jnp.sum(d_g * normed, axis=0, keepdims=True)
+        d_lin = norm_backward(d_g * r.gaink[...], normed, inverse).astype(BF)
+        r.d_qkv[runs_of(b), :, H * HD : (H + 1) * HD] = d_lin.reshape(-1, RUN, HD)
+        r.d_qkv[runs_of(b), :, (H + 1) * HD :] = r.d_v[rows, :].astype(BF).reshape(-1, RUN, HD)
+
+    loop(0, NB, key_back)
+
+    def qkv_grad(i):
+        p = lax.rem(s + i, S)
+        cols = rows_of(p * PR, PR)
+        r.g_qkv[cols, :] = tn(r.h1[:, cols], r.d_qkv[...].reshape(L, AC)).astype(BF)
+
+        @pl.when(i < S)
+        def _():
+            grad_send(QKV, i, p)
+
+    loop(1, S + 1, qkv_grad)
+
+    r.layer_out[...] = (r.y1[...] + scatter_sum(1)).astype(BF)
+    scatter_done(1)
+
+    def in_chip(i):
+        j = partner(i) * 2
+        parts = []
+        for k in range(2 * T // RUN):
+            parts.append(r.d_qkv[r.order[0, j * (T // RUN) + k]])
+        scatter_pair(3, i, nt(jnp.concatenate(parts, axis=0), r.w_qkv[...]))
+
+    loop(0, CH, in_chip)
+    scatter_chips(3)
+    grad_sum(DOWN)
+    rows_send(1, DOWN)
+    grad_sum(GU)
+    columns_send(1, GU)
+    grad_sum(OUT)
+    rows_send(0, OUT)
+    d_h1 = scatter_sum(3)
+    x = own_x()
+    r1 = inverse_root(x)
+    normed = x * r1
+    term1 = jnp.sum(d_h1 * normed, axis=0, keepdims=True)
+    r.hidden_grad[...] = r.d_y1[...] + norm_backward(d_h1 * r.gain1[...], normed, r1)
+    for k in range(WT):
+        r.terms[k : k + 1, :] = term1[:, k * HD : (k + 1) * HD]
+    r.terms[2 * WT : 2 * WT + 8, :] = r.sums[...]
+
+    def terms_far(i):
+        remote(r.terms, r.terms_z.at[s], r.t_send.at[i], r.t_recv.at[s],
+               seq=lax.rem(s + i, S)).start()
+
+    loop(1, S, terms_far)
+    grad_sum(QKV)
+    columns_send(0, QKV)
+    total = r.terms[...]
+    for i in range(1, S):
+        p = lax.rem(s + i, S)
+        arrived(r.terms_z.at[p], r.t_recv.at[p])
+        total = total + r.terms_z[p]
+    r.terms_sum[...] = total
+
+    def terms_near(i):
+        remote(r.terms_sum, r.terms_p.at[c], r.t_send.at[S + i], r.t_recv.at[S + c],
+               ctx=lax.rem(c + i, C)).start()
+
+    loop(1, C, terms_near)
+
+    rows_arrive(1, DOWN)
+    r.delta_down[...] = r.f_d[...].astype(F32)
+    rows_arrive(0, OUT)
+    r.delta_out[...] = r.f_o[...].astype(F32)
+    columns_arrive(1, GU)
+    for j in range(C):
+        r.delta_gate[:, j * U : (j + 1) * U] = r.f_gu[j, :, :U].astype(F32)
+        r.delta_up[:, j * U : (j + 1) * U] = r.f_gu[j, :, U:].astype(F32)
+    columns_arrive(0, QKV)
+    for j in range(C):
+        r.delta_query[:, j * H * HD : (j + 1) * H * HD] = r.f_qkv[j, :, : H * HD].astype(F32)
+        r.delta_key[:, j * HD : (j + 1) * HD] = r.f_qkv[j, :, H * HD : (H + 1) * HD].astype(F32)
+        r.delta_value[:, j * HD : (j + 1) * HD] = r.f_qkv[j, :, (H + 1) * HD :].astype(F32)
+    total = r.terms_sum[...]
+    for i in range(1, C):
+        j = lax.rem(c + i, C)
+        arrived(r.terms_p.at[j], r.t_recv.at[S + j])
+        total = total + r.terms_p[j]
+    r.terms_out[...] = total
+
+    loop(1, C, lambda i: arrived(gains_own, r.gain_send.at[i]))
+    loop(1, S, lambda i: arrived(r.gains_all.at[pl.ds(0, C)], r.gain_send.at[C + i]))
+    for kind in (X, G, H2, DY):
+        gather_done(kind)
+    spread_done(0, QKV)
+    spread_done(1, GU)
+    move_done(0, OUT)
+    move_done(1, DOWN)
+    for w in (QKV, OUT, GU, DOWN):
+        weight_done(w)
+        grad_done(w)
+    columns_done(0, QKV)
+    columns_done(1, GU)
+    rows_done(0, OUT)
+    rows_done(1, DOWN)
+    scatter_done(3)
+    loop(1, S, lambda i: arrived(r.terms, r.t_send.at[i]))
+    loop(1, C, lambda i: arrived(r.terms, r.t_send.at[S + i]))
+
+
+def fused_layer(mesh, args):
+    (x, positions, gain1, wq, wk, wv, gainq, gaink, wo, gain2, wg, wu, wd, g) = args
+    S, C = mesh.shape["seq"], mesh.shape["ctx"]
+    T, D = x.shape[1:]
+    L = positions.shape[1]
+    HD = HEAD_DIMENSION
+    H = QUERY_HEAD_COUNT // C
+    RW, OR, DR = wq.shape[0], wo.shape[0], wd.shape[0]
+    U = wg.shape[1] // C
+    AC = (H + 2) * HD
+    PR = C * RW
+    CH = C // 2
+    dims = types.SimpleNamespace(S=S, C=C, T=T, L=L, D=D, H=H, RW=RW, OR=OR, DR=DR, AC=AC, U=U)
+    packed = jnp.concatenate([gain1, gain2, gainq, gaink]).astype(F32)
+    packed = jnp.pad(packed[None, :], ((0, 7), (0, HD - packed.shape[0])))
+    half = HD // 2
+    frequency = np.power(THETA, -np.arange(half) * (2.0 / HD))
+    phases = np.arange(L)[:, None] * frequency[None, :]
+    table = jnp.asarray(np.concatenate([np.cos(phases), np.sin(phases)], axis=1), F32)
+    TR = 2 * (D // HD) + 8
+    run = positions[0, ::RUN] // RUN
+    spot = jnp.arange(L // RUN, dtype=jnp.int32)
+    place = jnp.sum(jnp.where(run[None, :] == spot[:, None], spot[None, :], 0), axis=1)
+    order = jnp.stack([run, place]).astype(jnp.int32)
+    inputs = dict(
+        order=order, x_in=x.reshape(T // RUN, RUN, D), g_in=g[0], gains_in=packed, wq_in=wq, wk_in=wk, wv_in=wv, wo_in=wo,
+        wg_in=wg, wu_in=wu, wd_in=wd, table_in=table,
+    )
+    outputs = dict(
+        layer_out=((T, D), BF), hidden_grad=((T, D), F32), delta_query=((RW, C * H * HD), F32),
+        delta_key=((RW, C * HD), F32), delta_value=((RW, C * HD), F32), delta_out=((OR, D), F32),
+        delta_gate=((RW, C * U), F32), delta_up=((RW, C * U), F32), delta_down=((DR, D), F32),
+        terms_out=((TR, HD), F32),
+    )
+    V, DMA = pltpu.VMEM, pltpu.SemaphoreType.DMA
+    scratch = dict(
+        x_all=V((L // RUN, RUN, D), BF), g_all=V((L, D), BF), h2_all=V((L, D), BF), dy_all=V((L, D), BF),
+        h1=V((L, D), BF), w_qkv=V((D, AC), BF), w_o=V((H * HD, D), BF), w_gu=V((D, 2 * U), BF),
+        w_d=V((U, D), BF), gains_all=V((S * C, 8, HD), F32), table=V((L, HD), F32),
+        cosine=V((L, HD), F32), sine=V((L, HD), F32), gain1=V((1, D), F32), gain2=V((1, D), F32),
+        gainq=V((1, HD), F32), gaink=V((1, HD), F32), q_lin=V((H, L, HD), F32), k_lin=V((L, HD), F32),
+        q_rot=V((H, L, HD), BF), k_rot=V((L, HD), BF), v=V((L, HD), BF), k_t=V((HD, L), BF),
+        v_t=V((HD, L), BF), e=V((H, L, L), BF), l_inv=V((H, 8, L), F32), o_t=V((H, HD, L), F32),
+        o_sorted=V((L // RUN, RUN, H * HD), BF), o=V((L, H * HD), BF), y1=V((T, D), F32), d_act=V((L, U), F32),
+        act=V((L, U), BF), d_gu=V((L, 2 * U), BF), d_y1=V((T, D), F32), d_o=V((L // RUN, RUN, H * HD), BF),
+        d_o_sorted=V((L, H * HD), BF), do_t=V((H, HD, BLOCK), BF), do_l=V((H, BLOCK, HD), BF),
+        d_k=V((L, HD), F32), d_v=V((L, HD), F32), d_qkv=V((L // RUN, RUN, AC), BF), sums=V((8, HD), F32),
+        pair=V((CH, 2 * T, D), F32), s1=V((CH, T, D), BF), r1=V((2, CH, T, D), BF),
+        s2=V((CH, T, D), BF), r2=V((2, CH, T, D), BF),
+        g_qkv=V((D, AC), BF), g_o=V((H * HD, D), BF), g_gu=V((D, 2 * U), BF), g_d=V((U, D), BF),
+        t_qkv=V((S, PR, AC), BF), t_o=V((S, OR, D), BF), t_gu=V((S, PR, 2 * U), BF), t_d=V((S, DR, D), BF),
+        u_qkv=V((PR, AC), BF), u_o=V((OR, D), BF), u_gu=V((PR, 2 * U), BF), u_d=V((DR, D), BF),
+        f_qkv=V((C, RW, AC), BF), f_o=V((OR, D), BF), f_gu=V((C, RW, 2 * U), BF), f_d=V((DR, D), BF),
+        terms=V((TR, HD), F32), terms_z=V((S, TR, HD), F32), terms_sum=V((TR, HD), F32),
+        terms_p=V((C, TR, HD), F32),
+        ag_send=DMA((4, 2 * CH)), ag_recv=DMA((4, C)), rs_send=DMA((4, 2 * CH)), r1_recv=DMA((4, CH)),
+        r2_recv=DMA((4, CH)), z_send=DMA((4, 2, S)), z_recv=DMA((4, S)), gz_send=DMA((4, S)),
+        gz_recv=DMA((4, S)), gp_send=DMA((2, C)), gp_recv=DMA((2, C)), row_send=DMA((2,)),
+        row_recv=DMA((2,)), w_send=DMA((2,)), w_recv=DMA((2,)), m_send=DMA((2,)), m_recv=DMA((2,)),
+        gain_send=DMA((C + S,)), gain_recv=DMA((S,)), t_send=DMA((S + C,)), t_recv=DMA((S + C,)),
+        local_sem=DMA((3,)),
+    )
+    names = list(inputs) + list(outputs) + list(scratch)
+
+    def kernel(*refs):
+        layer_kernel(dims, types.SimpleNamespace(**dict(zip(names, refs))))
+
+    in_specs = [
+        pl.BlockSpec(memory_space=pltpu.SMEM if name == "order" else pl.ANY) for name in inputs
+    ]
+    results = pl.pallas_call(
+        kernel,
+        out_shape=[jax.ShapeDtypeStruct(*v) for v in outputs.values()],
+        in_specs=in_specs,
+        out_specs=[pl.BlockSpec(memory_space=pltpu.VMEM)] * len(outputs),
+        scratch_shapes=list(scratch.values()),
+        compiler_params=pltpu.CompilerParams(
+            collective_id=0, has_side_effects=True, vmem_limit_bytes=67043328
+        ),
+        name="layer",
+    )(*inputs.values())
+    out = types.SimpleNamespace(**dict(zip(outputs, results)))
+    terms = out.terms_out.reshape(-1)
+    me = lax.axis_index("seq") * C + lax.axis_index("ctx")
+
+    def mine(start, array):
+        n = array.shape[0]
+        return lax.dynamic_slice_in_dim(terms, start + me * n, n)
+
+    return (
+        out.layer_out[None], out.hidden_grad[None], mine(0, gain1), out.delta_query,
+        out.delta_key, out.delta_value, mine(2 * D, gainq), mine(2 * D + HD, gaink),
+        out.delta_out, mine(D, gain2), out.delta_gate, out.delta_up, out.delta_down,
+    )
 
 
 def angles(places, head_size):
@@ -37,10 +876,6 @@
     scaled = upstream * sines
     turned = jnp.concatenate([scaled[..., half_size:], -scaled[..., :half_size]], axis=-1)
     return upstream * cosines + turned
-
-
-def norm_backward(normed_grad, normed, inverse):
-    return inverse * (normed_grad - normed * jnp.mean(normed_grad * normed, axis=-1, keepdims=True))
 
 
 def dot(a, b):
@@ -247,8 +1082,21 @@
     token = P("seq", "ctx", None)
     flat = P(("seq", "ctx"))
     rows = P(("seq", "ctx"), None)
+    general = local_of(mesh)
+
+    def body(*args):
+        tokens, length = args[0].shape[1], args[1].shape[1]
+        fits = (
+            mesh.shape["ctx"] == KEY_VALUE_HEADS == 8
+            and length <= 1024
+            and length % BLOCK == 0
+            and tokens % RUN == 0
+            and HEAD_DIMENSION % (mesh.shape["seq"] * mesh.shape["ctx"]) == 0
+        )
+        return fused_layer(mesh, args) if fits else general(*args)
+
     return jax.shard_map(
-        local_of(mesh),
+        body,
         mesh=mesh,
         in_specs=(token, P("seq", None), flat, rows, rows, rows, flat, flat, rows, flat, rows, rows, rows, token),
         out_specs=(token, token, flat, rows, rows, rows, flat, flat, rows, flat, rows, rows, rows),

time: 572 us -> 215 us (0.38); the launches traced: 562 us -> 213 us
  waiting for transfers between devices: 301 us -> 0 us
  Pallas kernels: 0 us -> 198 us
  blocking collectives: 107 us -> 0 us
  matrix products: 54.9 us -> 0 us
  other arithmetic: 36.8 us -> 1.38 us
  starting transfers between devices: 21.3 us -> 0 us
  between operations: 15.4 us -> 0.7 us
  local copies, waits for them, and re-layouts: 26.3 us -> 13 us
    pallas_call x0 -> x1, Pallas kernels: none -> 198 us  [fused_layer(): pl.pallas_call(kernel, out_shape=[jax.ShapeDtypeStruct(*v) for v in outpu...]
    reduce_scatter x6 -> x0, waiting for transfers between devices: 143 us -> none  [the longest x4 133 us: scatter(): lax.psum_scatter(part.astype(BF), 'ctx', scatter_dimension=0, tiled=True)]
    all_gather x6 -> x0, waiting for transfers between devices: 130 us -> none  [the longest x1 51.3 us: local(): lax.all_gather(column_weights[:, 0], 'seq', axis=0, tiled=True)]
    dot_general x24 -> x0, matrix products: 54.9 us -> none  [the longest x20 45.1 us: dot(): return jnp.dot(a, b, preferred_element_type=F32)]
    psum x1 -> x0, blocking collectives: 42.3 us -> none  [local(): lax.psum(jnp.concatenate([first_term, second_term, query_term, key_term])...]
    unnamed x1 -> x0, blocking collectives: 40.2 us -> none
    ppermute x2 -> x0, waiting for transfers between devices: 26.6 us -> none  [the longest x1 21.6 us: rows_sum(): return lax.ppermute(part, axes, back).astype(F32)]
    all_to_all x1 -> x0, blocking collectives: 24.4 us -> none  [local(): lax.all_to_all(column_weights, 'ctx', split_axis=1, concat_axis=0, tiled=...]
  transfers between devices with their start and end apart: 15 -> 0, of which waited for: 12 -> 0; matrix products, arithmetic and copies ran while one was open for 9% -> 0% of each run, Pallas kernels for 0% -> 0%
where the time goes in v2:
time: 215 us; the launch traced here: 213 us
  Pallas kernels  198 us (92%)
  local copies, waits for them, and re-layouts  13 us (6%)
    pallas_call x1, Pallas kernels, fused_layer(): pl.pallas_call(kernel, out_shape=[jax.ShapeDtypeStruct(*v) for v in outpu...  198 us
    unnamed x33, local copies, waits for them, and re-layouts  9.5 us

profile of v2, /device:TPU:9, one launch (start us, length us, event | category | flops | bytes accessed | tf_op | source)
XLA Modules:
  0.0 212.8 jit_solution(9095606438730653252)
XLA Ops:
  0.7 0.8 slice.3
  1.4 0.1 select_reduce_fusion
  1.6 0.6 pad_add_fusion.refs_0_
  2.2 0.0 copy-start.11
  2.2 0.0 copy-start.8
  2.2 0.0 copy-start.9
  2.2 0.6 copy-done.11
  2.8 0.0 copy-done.8
  2.8 0.0 copy-done.9
  2.8 0.0 copy-done.10
  2.9 0.7 fusion.9.refs_3_
  3.5 197.8 %layer.1 = (bf16[128,1024]{1,0:T(8,128)(2,1)}, f32[128,1024]{1,0:T(8,128)}, f32[32,2048]{1,0:T(8,128)}, f32[32,1024]{1,0:T(8,128)}, f32[32,1024]{1,0:T(8,128)}, ...) custom-call(s32[2,16]{1,0:T(2,128)} %pad_add_fusion.refs_0_, ...), custom_call_target="tpu_custom_call" | custom-call | tf_op jit(solution)/shard_map/layer/pallas_call | solution.py:834
  201.3 0.0 copy-start
  201.3 1.3 fusion.13
  202.6 1.3 fusion.14
  204.0 1.7 copy.37
  205.6 0.0 copy-done
  205.7 0.8 copy.38
  206.4 0.3 copy-done.5
  206.7 0.7 copy.39
  207.5 0.3 copy-done.7
  207.7 0.7 copy.40
  208.4 0.0 copy-done.6
  208.4 0.7 copy.41
  209.1 0.0 copy-done.4
  209.1 0.7 copy.42
  209.8 0.0 copy-done.3
  209.8 0.7 copy.43
  210.5 0.4 copy-done.2
  210.9 0.7 copy.44
  211.7 0.4 copy-done.1
  212.0 0.7 copy.45
  (10 shorter events, 0.0 us)
Async XLA Ops:
  2.2 0.7 copy-start.11
  2.2 0.7 copy-start.8
  2.2 0.7 copy-start.9
  2.2 0.7 copy-start.10
  201.3 4.4 %copy-start = (f32[128,1024]{1,0:T(8,128)S(1)}, f32[128,1024]{1,0:T(8,128)}, u32[]{:S(2)}) copy-start(f32[128,1024]{1,0:T(8,128)} %get-tuple-element.24) | copy-start | bytes 1572868
  205.7 1.1 copy-start.5
  206.7 1.0 copy-start.7
  206.7 1.7 copy-start.6
  207.7 1.3 copy-start.4
  208.4 1.4 copy-start.3
  209.8 1.1 copy-start.2
  210.9 1.1 copy-start.1

commit v3 on v2

--- a/solution.py
+++ b/solution.py
@@ -157,17 +157,24 @@
         remote(r.s1.at[i], r.r1.at[1 if kind == 1 else 0, i], r.rs_send.at[kind, i],
                r.r1_recv.at[kind, i], ctx=sibling).start()
 
-    def scatter_chips(kind):
+    def scatter_chip(kind, i):
         bank = 1 if kind == 1 else 0
-
-        def go(i):
-            arrived(r.r1.at[bank, i], r.r1_recv.at[kind, i])
-            mine = r.pair[i, rows_of(core * T, T), :] + r.r1[bank, i].astype(F32)
-            r.s2[i] = mine.astype(BF)
-            remote(r.s2.at[i], r.r2.at[bank, i], r.rs_send.at[kind, CH + i],
-                   r.r2_recv.at[kind, i], ctx=partner(i) * 2 + core).start()
-
-        loop(1, CH, go)
+        arrived(r.r1.at[bank, i], r.r1_recv.at[kind, i])
+        mine = r.pair[i, rows_of(core * T, T), :] + r.r1[bank, i].astype(F32)
+        r.s2[i] = mine.astype(BF)
+        remote(r.s2.at[i], r.r2.at[bank, i], r.rs_send.at[kind, CH + i],
+               r.r2_recv.at[kind, i], ctx=partner(i) * 2 + core).start()
+
+    def scatter(kind, partial):
+        def go(k):
+            i = lax.rem(k + 1, CH)
+            scatter_pair(kind, i, partial(i))
+
+            @pl.when(k > 0)
+            def _():
+                scatter_chip(kind, k)
+
+        loop(0, CH, go)
 
     def scatter_sum(kind):
         bank = 1 if kind == 1 else 0
@@ -182,21 +189,27 @@
         loop(0, CH, lambda i: arrived(r.s1.at[0], r.rs_send.at[kind, i]))
         loop(1, CH, lambda i: arrived(r.s2.at[1], r.rs_send.at[kind, CH + i]))
 
-    QKV, OUT, GU, DOWN = 0, 1, 2, 3
-    held = {QKV: (r.w_qkv, PR), OUT: (r.w_o, OR), GU: (r.w_gu, PR), DOWN: (r.w_d, DR)}
+    QKV, GATE, UP, OUT, DOWN = 0, 1, 2, 3, 4
 
     def plane(w, b):
-        ref, size = held[w]
-        return ref.at[rows_of(b * size, size)]
-
-    def weight_start(w):
+        if w == QKV:
+            return r.w_qkv.at[rows_of(b * PR, PR)]
+        if w == GATE:
+            return r.w_gu.at[rows_of(b * PR, PR), pl.ds(0, U)]
+        if w == UP:
+            return r.w_gu.at[rows_of(b * PR, PR), pl.ds(U, U)]
+        return (r.z_o if w == OUT else r.z_d).at[b]
+
+    def weight_start(w, src=None):
+        src = plane(w, s) if src is None else src
+
         @pl.when(s < S - 1)
         def _():
-            remote(plane(w, s), plane(w, s), r.z_send.at[w, 0, 0], r.z_recv.at[w, s], seq=s + 1).start()
+            remote(src, plane(w, s), r.z_send.at[w, 0, 0], r.z_recv.at[w, s], seq=s + 1).start()
 
         @pl.when(s > 0)
         def _():
-            remote(plane(w, s), plane(w, s), r.z_send.at[w, 1, 0], r.z_recv.at[w, s], seq=s - 1).start()
+            remote(src, plane(w, s), r.z_send.at[w, 1, 0], r.z_recv.at[w, s], seq=s - 1).start()
 
     def weight_hop(w, t):
         below, above = s - 1 - t, s + 1 + t
@@ -229,26 +242,66 @@
             def _():
                 arrived(plane(w, s), r.z_send.at[w, 1, t])
 
+    GU = GATE
     sent = {QKV: (r.g_qkv, PR), OUT: (r.g_o, OR), GU: (r.g_gu, PR), DOWN: (r.g_d, DR)}
     got = {QKV: r.t_qkv, OUT: r.t_o, GU: r.t_gu, DOWN: r.t_d}
+    halfway = {QKV: r.c_qkv, OUT: r.c_o, GU: r.c_gu, DOWN: r.c_d}
     summed = {QKV: r.u_qkv, OUT: r.u_o, GU: r.u_gu, DOWN: r.u_d}
-
-    def grad_send(w, i, p):
+    side = jnp.where(s >= 2, 1, 0)
+
+    def grad_rows(w, p):
         ref, size = sent[w]
-        remote(ref.at[rows_of(p * size, size)], got[w].at[s], r.gz_send.at[w, i], r.gz_recv.at[w, s],
-               seq=p).start()
+        return ref.at[rows_of(p * size, size)]
+
+    def grad_order(i):
+        return jnp.where(s < 2, lax.rem(3 - i + s, S), lax.rem(i + (3 - s) * 3, S))
+
+    def grad_direct(w, p):
+        remote(grad_rows(w, p), got[w].at[side], r.gz_send.at[w, p], r.gz_recv.at[w, side], seq=p).start()
+
+    def grad_out(w, p):
+        far_up = jnp.logical_and(s == 0, p >= 2)
+        far_down = jnp.logical_and(s == S - 1, p <= 1)
+        later = jnp.logical_or(
+            jnp.logical_and(s == 1, p >= 2), jnp.logical_and(s == 2, p <= 1)
+        )
+
+        @pl.when(far_up)
+        def _():
+            remote(grad_rows(w, p), halfway[w].at[p - 2], r.gz_send.at[w, p], r.gc_recv.at[w, p - 2],
+                   seq=1).start()
+
+        @pl.when(far_down)
+        def _():
+            remote(grad_rows(w, p), halfway[w].at[p], r.gz_send.at[w, p], r.gc_recv.at[w, p], seq=2).start()
+
+        others = jnp.logical_or(jnp.logical_or(far_up, far_down), jnp.logical_or(later, p == s))
+
+        @pl.when(jnp.logical_not(others))
+        def _():
+            grad_direct(w, p)
+
+    def grad_combine(w, k):
+        @pl.when(jnp.logical_or(s == 1, s == 2))
+        def _():
+            p = jnp.where(s == 1, 3 - k, k)
+            slot = jnp.where(s == 1, 1 - k, k)
+            ref, size = sent[w]
+            rows = rows_of(p * size, size)
+            arrived(halfway[w].at[slot], r.gc_recv.at[w, slot])
+            ref[rows, :] = (ref[rows, :].astype(F32) + halfway[w][slot].astype(F32)).astype(BF)
+            grad_direct(w, p)
 
     def grad_sum(w):
         ref, size = sent[w]
         total = ref[rows_of(s * size, size), :].astype(F32)
-        for i in range(1, S):
-            p = lax.rem(s + i, S)
-            arrived(got[w].at[p], r.gz_recv.at[w, p])
-            total = total + got[w][p].astype(F32)
+        for i in range(2):
+            arrived(got[w].at[i], r.gz_recv.at[w, i])
+            total = total + got[w][i].astype(F32)
         summed[w][...] = total.astype(BF)
 
     def grad_done(w):
-        loop(1, S, lambda i: arrived(got[w].at[0], r.gz_send.at[w, i]))
+        loop(1, S, lambda i: arrived(got[w].at[0], r.gz_send.at[w, lax.rem(s + i, S)]))
 
     final = {QKV: r.f_qkv, GU: r.f_gu, OUT: r.f_o, DOWN: r.f_d}
 
@@ -309,8 +362,10 @@
             (r.wu_in.at[:, rows_of(j * U, U)], slice(U, 2 * U)),
         )
 
+    columns_of = {QKV: r.w_qkv, GU: r.w_gu}
+
     def spread(n, w, piece):
-        ref = held[w][0]
+        ref = columns_of[w]
         own = rows_of(s * PR + c * RW, RW)
 
         def go(i):
@@ -323,36 +378,55 @@
             local(src, ref.at[own, columns], r.w_recv.at[n]).start()
 
     def spread_arrive(n, w):
-        arrived(plane(w, s), r.w_recv.at[n])
+        arrived(columns_of[w].at[rows_of(s * PR, PR)], r.w_recv.at[n])
 
     def spread_done(n, w):
-        ref = held[w][0]
-        arrived(ref.at[pl.ds(0, (C - 1) * RW)], r.w_send.at[n])
-
-    def move(n, w, src):
-        @pl.when(moved)
-        def _():
-            remote(src, held[w][0].at[rows_of(to_s * held[w][1], held[w][1])], r.m_send.at[n],
-                   r.m_recv.at[n], seq=to_s, ctx=to_c).start()
-
-        @pl.when(jnp.logical_not(moved))
-        def _():
-            local(src, plane(w, s), r.m_recv.at[n]).start()
-
-    def move_arrive(n, w):
-        arrived(plane(w, s), r.m_recv.at[n])
-
-    def move_done(n, w):
-        @pl.when(moved)
-        def _():
-            arrived(plane(w, s), r.m_send.at[n])
-
+        arrived(columns_of[w].at[pl.ds(0, (C - 1) * RW)], r.w_send.at[n])
+
+    rows_ref = {OUT: (r.w_o, OR), DOWN: (r.w_d, DR)}
+
+    def deal(n, w):
+        ref, size = rows_ref[w]
+
+        def go(b):
+            d = C * b + c
+            rank, spot = lax.div(d, S), lax.rem(d, S)
+            dst = ref.at[rows_of(spot * size, size)]
+
+            @pl.when(rank != c)
+            def _():
+                remote(plane(w, b), dst, r.m_send.at[n, b], r.m_recv.at[n], ctx=rank).start()
+
+            @pl.when(rank == c)
+            def _():
+                local(plane(w, b), dst, r.m_recv.at[n]).start()
+
+        loop(0, S, go)
+
+    def deal_arrive(n, w):
+        arrived(rows_ref[w][0], r.m_recv.at[n])
+
+    def deal_done(n, w):
+        def go(b):
+            @pl.when(lax.div(C * b + c, S) != c)
+            def _():
+                arrived(plane(w, 0), r.m_send.at[n, b])
+
+        loop(0, S, go)
+
+    def own_rows(n, w, src):
+        local(src, plane(w, s), r.local_sem.at[3 + n]).start()
+        weight_start(w, src)
+
+    own_rows(0, OUT, r.wo_in)
     spread(0, QKV, qkv_piece)
     local(r.x_in, block(X, c), r.local_sem.at[0]).start()
     local(r.table_in, r.table, r.local_sem.at[1]).start()
     gather_send(X, r.x_in)
-    move(0, OUT, r.wo_in)
-
+    spread(1, GU, gu_piece)
+    weight_hop(OUT, 0)
+    spread_arrive(0, QKV)
+    weight_start(QKV)
     arrived(r.gains_all.at[pl.ds(s * C, C)], r.gain_recv.at[s])
 
     def gain_far(i):
@@ -360,12 +434,7 @@
         remote(mine, mine, r.gain_send.at[C + i], r.gain_recv.at[s], seq=lax.rem(s + i, S)).start()
 
     loop(1, S, gain_far)
-    spread_arrive(0, QKV)
-    weight_start(QKV)
-    move_arrive(0, OUT)
-    weight_start(OUT)
-    spread(1, GU, gu_piece)
-    move(1, DOWN, r.wd_in)
+    weight_hop(OUT, 1)
 
     arrived(r.table, r.local_sem.at[1])
 
@@ -378,6 +447,14 @@
         r.sine[rows, :] = jnp.where(first, -other, both)
 
     loop(0, L // T, tables)
+    weight_hop(OUT, 2)
+    arrived(plane(OUT, s), r.local_sem.at[3])
+    deal(0, OUT)
+    weight_hop(QKV, 0)
+    arrived(block(X, c), r.local_sem.at[0])
+    loop(1, CH, lambda i: gather_relay(X, i))
+    local(r.g_in, block(G, c), r.local_sem.at[2]).start()
+    gather_send(G, r.g_in)
 
     def gain_block(i):
         p = lax.rem(s + i, S)
@@ -404,26 +481,18 @@
     r.gainq[...] = gain_vector(2 * n1, n3)
     r.gaink[...] = gain_vector(2 * n1 + n3, n3)
 
-    arrived(block(X, c), r.local_sem.at[0])
-    loop(1, CH, lambda i: gather_relay(X, i))
     arrived(block(X, sibling), r.ag_recv.at[X, sibling])
     loop(1, CH, lambda i: gather_other(X, i))
-    weight_hop(QKV, 0)
-    local(r.g_in, block(G, c), r.local_sem.at[2]).start()
-    gather_send(G, r.g_in)
 
     def first_norm(k):
         x = r.x_all[r.order[1, k]].astype(F32)
         r.h1[rows_of(k * RUN, RUN), :] = (x * inverse_root(x) * r.gain1[...]).astype(BF)
 
     loop(0, NR, first_norm)
-    weight_hop(OUT, 0)
     weight_hop(QKV, 1)
-    weight_hop(OUT, 1)
     spread_arrive(1, GU)
-    weight_start(GU)
+    weight_start(GATE)
     weight_hop(QKV, 2)
-    weight_hop(OUT, 2)
 
     def rotate(u, rows):
         return u * r.cosine[rows, :] + pltpu.roll(u, HD // 2, 1) * r.sine[rows, :]
@@ -448,10 +517,14 @@
         r.v_t[:, rows] = v.T.astype(BF)
 
     loop(0, NB, project)
-    gather_relay_g = lambda i: gather_relay(G, i)
-    loop(1, CH, gather_relay_g)
+    loop(1, CH, lambda i: gather_relay(G, i))
 
     def attend(qb):
+        @pl.when(qb == NB - 2)
+        def _():
+            weight_hop(GATE, 0)
+            weight_start(UP)
+
         cols = rows_of(qb * BLOCK, BLOCK)
 
         def keys(kb, carry):
@@ -482,21 +555,18 @@
             r.o_sorted[runs_of(qb), :, h * HD : (h + 1) * HD] = o.T.astype(BF).reshape(-1, RUN, HD)
 
     loop(0, NB, attend)
-    weight_hop(GU, 0)
-    move_arrive(1, DOWN)
-    weight_start(DOWN)
-
     def unsort(i):
         r.o[rows_of(i * RUN, RUN), :] = r.o_sorted[r.order[0, i]]
 
     loop(0, NR, unsort)
 
-    def out_chip(i):
-        scatter_pair(0, i, nn(r.o[rows_of(partner(i) * 2 * T, 2 * T), :], r.w_o[...]))
-
-    loop(0, CH, out_chip)
-    scatter_chips(0)
-    weight_hop(GU, 1)
+    deal_arrive(0, OUT)
+    scatter(0, lambda i: nn(r.o[rows_of(partner(i) * 2 * T, 2 * T), :], r.w_o[...]))
+    weight_hop(GATE, 1)
+    own_rows(1, DOWN, r.wd_in)
+    weight_hop(UP, 0)
+    weight_hop(GATE, 2)
+    weight_hop(UP, 1)
     y1 = own_x() + scatter_sum(0)
     scatter_done(0)
     r.y1[...] = y1
@@ -504,19 +574,10 @@
     r.h2_all[rows_of(c * T, T), :] = h2_own
     gather_send(H2, block(H2, c))
 
-    weight_hop(GU, 2)
-    weight_hop(DOWN, 0)
-    weight_hop(DOWN, 1)
+    weight_hop(UP, 2)
     arrived(block(G, c), r.local_sem.at[2])
     arrived(block(G, sibling), r.ag_recv.at[G, sibling])
     loop(1, CH, lambda i: gather_other(G, i))
-    weight_hop(DOWN, 2)
-
-    def act_grad(b):
-        rows = rows_of(b * BLOCK, BLOCK)
-        r.d_act[rows, :] = nt(r.g_all[rows, :], r.w_d[...])
-
-    loop(0, NB, act_grad)
     arrived(block(H2, sibling), r.ag_recv.at[H2, sibling])
 
     def feed(i):
@@ -524,6 +585,14 @@
         def _():
             gather_relay(H2, i)
             gather_other(H2, i)
+
+        @pl.when(i == 1)
+        def _():
+            weight_hop(DOWN, 0)
+
+        @pl.when(i == 2)
+        def _():
+            weight_hop(DOWN, 1)
 
         rows = rows_of(partner(i) * 2 * T, 2 * T)
         h2 = r.h2_all[rows, :]
@@ -532,33 +601,40 @@
         sig = 1.0 / (1.0 + jnp.exp(-gate))
         silu = gate * sig
         r.act[rows, :] = (silu * up).astype(BF)
-        d_act = r.d_act[rows, :]
-        d_gate = (d_act * up * sig * (1.0 + gate * (1.0 - sig))).astype(BF)
-        d_up = (d_act * silu).astype(BF)
-        r.d_gu[rows, :U] = d_gate
-        r.d_gu[rows, U:] = d_up
-        scatter_pair(2, i, nt(r.d_gu[rows, :], r.w_gu[...]))
+        r.slope[rows, :] = up * sig * (1.0 + gate * (1.0 - sig))
+        r.silu[rows, :] = silu
 
     loop(0, CH, feed)
-    scatter_chips(2)
+    weight_hop(DOWN, 2)
+    arrived(plane(DOWN, s), r.local_sem.at[4])
+    deal(1, DOWN)
+    deal_arrive(1, DOWN)
+
+    def feed_back(i):
+        rows = rows_of(partner(i) * 2 * T, 2 * T)
+        d_act = nt(r.g_all[rows, :], r.w_d[...])
+        r.d_gu[rows, :U] = (d_act * r.slope[rows, :]).astype(BF)
+        r.d_gu[rows, U:] = (d_act * r.silu[rows, :]).astype(BF)
+        return nt(r.d_gu[rows, :], r.w_gu[...])
+
+    scatter(2, feed_back)
 
     def down_grad(m):
         cols = rows_of(m * HD, HD)
         r.g_d[cols, :] = tn(r.act[:, cols], r.g_all[...]).astype(BF)
 
     loop(0, U // HD, down_grad)
-    loop(1, S, lambda i: grad_send(DOWN, i, lax.rem(s + i, S)))
+    loop(0, S, lambda i: grad_out(DOWN, grad_order(i)))
 
     def gu_grad(i):
-        p = lax.rem(s + i, S)
+        p = grad_order(i)
         cols = rows_of(p * PR, PR)
         r.g_gu[cols, :] = tn(r.h2_all[:, cols], r.d_gu[...]).astype(BF)
-
-        @pl.when(i < S)
-        def _():
-            grad_send(GU, i, p)
-
-    loop(1, S + 1, gu_grad)
+        grad_out(GU, p)
+
+    loop(0, S, gu_grad)
+    grad_combine(DOWN, 0)
+    grad_combine(DOWN, 1)
 
     d_h2 = scatter_sum(2)
     scatter_done(2)
@@ -574,10 +650,7 @@
     for k in range(WT):
         r.terms[WT + k : WT + k + 1, :] = term2[:, k * HD : (k + 1) * HD]
 
-    def last_chip(i):
-        scatter_pair(1, i, nn(r.act[rows_of(partner(i) * 2 * T, 2 * T), :], r.w_d[...]))
-
-    loop(0, CH, last_chip)
+    scatter(1, lambda i: nn(r.act[rows_of(partner(i) * 2 * T, 2 * T), :], r.w_d[...]))
     arrived(block(DY, sibling), r.ag_recv.at[DY, sibling])
 
     def out_grad(i):
@@ -591,14 +664,14 @@
         r.d_o[pl.ds(partner(i) * (2 * T // RUN), 2 * T // RUN)] = d_o.reshape(-1, RUN, H * HD)
 
     loop(0, CH, out_grad)
-    scatter_chips(1)
 
     def out_weight(m):
         cols = rows_of(m * HD, HD)
         r.g_o[cols, :] = tn(r.o[:, cols], r.dy_all[...]).astype(BF)
 
     loop(0, H * HD // HD, out_weight)
-    loop(1, S, lambda i: grad_send(OUT, i, lax.rem(s + i, S)))
+    loop(0, S, lambda i: grad_out(OUT, grad_order(i)))
+    grad_combine(GU, 0)
 
     def sort(k):
         r.d_o_sorted[rows_of(k * RUN, RUN), :] = r.d_o[r.order[1, k]]
@@ -663,17 +736,16 @@
     loop(0, NB, key_back)
 
     def qkv_grad(i):
-        p = lax.rem(s + i, S)
+        p = grad_order(i)
         cols = rows_of(p * PR, PR)
         r.g_qkv[cols, :] = tn(r.h1[:, cols], r.d_qkv[...].reshape(L, AC)).astype(BF)
-
-        @pl.when(i < S)
-        def _():
-            grad_send(QKV, i, p)
-
-    loop(1, S + 1, qkv_grad)
-
-    r.layer_out[...] = (r.y1[...] + scatter_sum(1)).astype(BF)
+        grad_out(QKV, p)
+
+    loop(0, S, qkv_grad)
+    grad_combine(GU, 1)
+
+    r.y_out[...] = (r.y1[...] + scatter_sum(1)).astype(BF)
+    local(r.y_out, r.layer_out, r.out_sem.at[0]).start()
     scatter_done(1)
 
     def in_chip(i):
@@ -681,22 +753,23 @@
         parts = []
         for k in range(2 * T // RUN):
             parts.append(r.d_qkv[r.order[0, j * (T // RUN) + k]])
-        scatter_pair(3, i, nt(jnp.concatenate(parts, axis=0), r.w_qkv[...]))
-
-    loop(0, CH, in_chip)
-    scatter_chips(3)
+        return nt(jnp.concatenate(parts, axis=0), r.w_qkv[...])
+
+    scatter(3, in_chip)
     grad_sum(DOWN)
     rows_send(1, DOWN)
+    grad_combine(OUT, 0)
+    grad_combine(OUT, 1)
     grad_sum(GU)
     columns_send(1, GU)
-    grad_sum(OUT)
-    rows_send(0, OUT)
+    grad_combine(QKV, 0)
     d_h1 = scatter_sum(3)
     x = own_x()
     r1 = inverse_root(x)
     normed = x * r1
     term1 = jnp.sum(d_h1 * normed, axis=0, keepdims=True)
-    r.hidden_grad[...] = r.d_y1[...] + norm_backward(d_h1 * r.gain1[...], normed, r1)
+    r.x_grad[...] = r.d_y1[...] + norm_backward(d_h1 * r.gain1[...], normed, r1)
+    local(r.x_grad, r.hidden_grad, r.out_sem.at[1]).start()
     for k in range(WT):
         r.terms[k : k + 1, :] = term1[:, k * HD : (k + 1) * HD]
     r.terms[2 * WT : 2 * WT + 8, :] = r.sums[...]
@@ -706,6 +779,9 @@
                seq=lax.rem(s + i, S)).start()
 
     loop(1, S, terms_far)
+    grad_combine(QKV, 1)
+    grad_sum(OUT)
+    rows_send(0, OUT)
     grad_sum(QKV)
     columns_send(0, QKV)
     total = r.terms[...]
@@ -722,24 +798,20 @@
     loop(1, C, terms_near)
 
     rows_arrive(1, DOWN)
-    r.delta_down[...] = r.f_d[...].astype(F32)
+    local(r.f_d, r.down_out, r.out_sem.at[2]).start()
+    columns_arrive(1, GU)
+    local(r.f_gu, r.gu_out, r.out_sem.at[3]).start()
     rows_arrive(0, OUT)
-    r.delta_out[...] = r.f_o[...].astype(F32)
-    columns_arrive(1, GU)
-    for j in range(C):
-        r.delta_gate[:, j * U : (j + 1) * U] = r.f_gu[j, :, :U].astype(F32)
-        r.delta_up[:, j * U : (j + 1) * U] = r.f_gu[j, :, U:].astype(F32)
+    local(r.f_o, r.o_out, r.out_sem.at[4]).start()
     columns_arrive(0, QKV)
-    for j in range(C):
-        r.delta_query[:, j * H * HD : (j + 1) * H * HD] = r.f_qkv[j, :, : H * HD].astype(F32)
-        r.delta_key[:, j * HD : (j + 1) * HD] = r.f_qkv[j, :, H * HD : (H + 1) * HD].astype(F32)
-        r.delta_value[:, j * HD : (j + 1) * HD] = r.f_qkv[j, :, (H + 1) * HD :].astype(F32)
+    local(r.f_qkv, r.qkv_out, r.out_sem.at[5]).start()
     total = r.terms_sum[...]
     for i in range(1, C):
         j = lax.rem(c + i, C)
         arrived(r.terms_p.at[j], r.t_recv.at[S + j])
         total = total + r.terms_p[j]
-    r.terms_out[...] = total
+    r.terms_all[...] = total
+    local(r.terms_all, r.terms_out, r.out_sem.at[6]).start()
 
     loop(1, C, lambda i: arrived(gains_own, r.gain_send.at[i]))
     loop(1, S, lambda i: arrived(r.gains_all.at[pl.ds(0, C)], r.gain_send.at[C + i]))
@@ -747,10 +819,11 @@
         gather_done(kind)
     spread_done(0, QKV)
     spread_done(1, GU)
-    move_done(0, OUT)
-    move_done(1, DOWN)
+    deal_done(0, OUT)
+    deal_done(1, DOWN)
+    for w in (QKV, GATE, UP, OUT, DOWN):
+        weight_done(w)
     for w in (QKV, OUT, GU, DOWN):
-        weight_done(w)
         grad_done(w)
     columns_done(0, QKV)
     columns_done(1, GU)
@@ -759,6 +832,41 @@
     scatter_done(3)
     loop(1, S, lambda i: arrived(r.terms, r.t_send.at[i]))
     loop(1, C, lambda i: arrived(r.terms, r.t_send.at[S + i]))
+    pairs = (
+        (r.y_out, r.layer_out), (r.x_grad, r.hidden_grad), (r.f_d, r.down_out), (r.f_gu, r.gu_out),
+        (r.f_o, r.o_out), (r.f_qkv, r.qkv_out), (r.terms_all, r.terms_out),
+    )
+    for k, (src, dst) in enumerate(pairs):
+        local(src, dst, r.out_sem.at[k]).wait()
+
+
+def finish_kernel(dims, refs):
+    S, C, D, H, U = dims.S, dims.C, dims.D, dims.H, dims.U
+    HD = HEAD_DIMENSION
+    r = refs
+    me = lax.axis_index("seq") * C + lax.axis_index("ctx")
+    r.layer_res[...] = r.layer_out[...]
+    r.hidden_res[...] = r.hidden_grad[...]
+    r.delta_down[...] = r.down_out[...].astype(F32)
+    r.delta_out[...] = r.o_out[...].astype(F32)
+    for j in range(C):
+        r.delta_gate[:, j * U : (j + 1) * U] = r.gu_out[j, :, :U].astype(F32)
+        r.delta_up[:, j * U : (j + 1) * U] = r.gu_out[j, :, U:].astype(F32)
+        r.delta_query[:, j * H * HD : (j + 1) * H * HD] = r.qkv_out[j, :, : H * HD].astype(F32)
+        r.delta_key[:, j * HD : (j + 1) * HD] = r.qkv_out[j, :, H * HD : (H + 1) * HD].astype(F32)
+        r.delta_value[:, j * HD : (j + 1) * HD] = r.qkv_out[j, :, (H + 1) * HD :].astype(F32)
+
+    def own(ref, first_row, count):
+        start = me * count
+        row = r.terms_out[pl.ds(first_row + lax.div(start, HD), 1), :]
+        back = lax.rem(HD - lax.rem(start, HD), HD)
+        ref[...] = pltpu.roll(jnp.broadcast_to(row, (8, HD)), back, 1)[0:1, :count]
+
+    n1, n3 = D // (S * C), HD // (S * C)
+    own(r.change1, 0, n1)
+    own(r.change2, D // HD, n1)
+    own(r.changeq, 2 * (D // HD), n3)
+    own(r.changek, 2 * (D // HD) + 1, n3)
 
 
 def fused_layer(mesh, args):
@@ -789,11 +897,17 @@
         order=order, x_in=x.reshape(T // RUN, RUN, D), g_in=g[0], gains_in=packed, wq_in=wq, wk_in=wk, wv_in=wv, wo_in=wo,
         wg_in=wg, wu_in=wu, wd_in=wd, table_in=table,
     )
+    TR_shape = ((TR, HD), F32)
     outputs = dict(
-        layer_out=((T, D), BF), hidden_grad=((T, D), F32), delta_query=((RW, C * H * HD), F32),
-        delta_key=((RW, C * HD), F32), delta_value=((RW, C * HD), F32), delta_out=((OR, D), F32),
+        layer_out=((T, D), BF), hidden_grad=((T, D), F32), qkv_out=((C, RW, AC), BF), o_out=((OR, D), BF),
+        gu_out=((C, RW, 2 * U), BF), down_out=((DR, D), BF), terms_out=TR_shape,
+    )
+    n1, n3 = D // (S * C), HD // (S * C)
+    final = dict(
+        layer_res=((T, D), BF), hidden_res=((T, D), F32), change1=((1, n1), F32),
+        delta_query=((RW, C * H * HD), F32), delta_key=((RW, C * HD), F32), delta_value=((RW, C * HD), F32),
+        changeq=((1, n3), F32), changek=((1, n3), F32), delta_out=((OR, D), F32), change2=((1, n1), F32),
         delta_gate=((RW, C * U), F32), delta_up=((RW, C * U), F32), delta_down=((DR, D), F32),
-        terms_out=((TR, HD), F32),
     )
     V, DMA = pltpu.VMEM, pltpu.SemaphoreType.DMA
     scratch = dict(
@@ -804,24 +918,26 @@
         gainq=V((1, HD), F32), gaink=V((1, HD), F32), q_lin=V((H, L, HD), F32), k_lin=V((L, HD), F32),
         q_rot=V((H, L, HD), BF), k_rot=V((L, HD), BF), v=V((L, HD), BF), k_t=V((HD, L), BF),
         v_t=V((HD, L), BF), e=V((H, L, L), BF), l_inv=V((H, 8, L), F32), o_t=V((H, HD, L), F32),
-        o_sorted=V((L // RUN, RUN, H * HD), BF), o=V((L, H * HD), BF), y1=V((T, D), F32), d_act=V((L, U), F32),
+        o_sorted=V((L // RUN, RUN, H * HD), BF), o=V((L, H * HD), BF), y1=V((T, D), F32), slope=V((L, U), F32), silu=V((L, U), F32),
         act=V((L, U), BF), d_gu=V((L, 2 * U), BF), d_y1=V((T, D), F32), d_o=V((L // RUN, RUN, H * HD), BF),
         d_o_sorted=V((L, H * HD), BF), do_t=V((H, HD, BLOCK), BF), do_l=V((H, BLOCK, HD), BF),
         d_k=V((L, HD), F32), d_v=V((L, HD), F32), d_qkv=V((L // RUN, RUN, AC), BF), sums=V((8, HD), F32),
         pair=V((CH, 2 * T, D), F32), s1=V((CH, T, D), BF), r1=V((2, CH, T, D), BF),
         s2=V((CH, T, D), BF), r2=V((2, CH, T, D), BF),
         g_qkv=V((D, AC), BF), g_o=V((H * HD, D), BF), g_gu=V((D, 2 * U), BF), g_d=V((U, D), BF),
-        t_qkv=V((S, PR, AC), BF), t_o=V((S, OR, D), BF), t_gu=V((S, PR, 2 * U), BF), t_d=V((S, DR, D), BF),
+        t_qkv=V((2, PR, AC), BF), t_o=V((2, OR, D), BF), t_gu=V((2, PR, 2 * U), BF), t_d=V((2, DR, D), BF),
+        c_qkv=V((2, PR, AC), BF), c_o=V((2, OR, D), BF), c_gu=V((2, PR, 2 * U), BF), c_d=V((2, DR, D), BF),
+        z_o=V((S, OR, D), BF), z_d=V((S, DR, D), BF), y_out=V((T, D), BF), x_grad=V((T, D), F32), terms_all=V(*TR_shape),
         u_qkv=V((PR, AC), BF), u_o=V((OR, D), BF), u_gu=V((PR, 2 * U), BF), u_d=V((DR, D), BF),
         f_qkv=V((C, RW, AC), BF), f_o=V((OR, D), BF), f_gu=V((C, RW, 2 * U), BF), f_d=V((DR, D), BF),
         terms=V((TR, HD), F32), terms_z=V((S, TR, HD), F32), terms_sum=V((TR, HD), F32),
         terms_p=V((C, TR, HD), F32),
         ag_send=DMA((4, 2 * CH)), ag_recv=DMA((4, C)), rs_send=DMA((4, 2 * CH)), r1_recv=DMA((4, CH)),
-        r2_recv=DMA((4, CH)), z_send=DMA((4, 2, S)), z_recv=DMA((4, S)), gz_send=DMA((4, S)),
-        gz_recv=DMA((4, S)), gp_send=DMA((2, C)), gp_recv=DMA((2, C)), row_send=DMA((2,)),
-        row_recv=DMA((2,)), w_send=DMA((2,)), w_recv=DMA((2,)), m_send=DMA((2,)), m_recv=DMA((2,)),
+        r2_recv=DMA((4, CH)), z_send=DMA((5, 2, S)), z_recv=DMA((5, S)), gz_send=DMA((5, S)),
+        gz_recv=DMA((5, 2)), gc_recv=DMA((5, 2)), gp_send=DMA((2, C)), gp_recv=DMA((2, C)), row_send=DMA((2,)),
+        row_recv=DMA((2,)), w_send=DMA((2,)), w_recv=DMA((2,)), m_send=DMA((2, S)), m_recv=DMA((2,)),
         gain_send=DMA((C + S,)), gain_recv=DMA((S,)), t_send=DMA((S + C,)), t_recv=DMA((S + C,)),
-        local_sem=DMA((3,)),
+        local_sem=DMA((5,)), out_sem=DMA((7,)),
     )
     names = list(inputs) + list(outputs) + list(scratch)
 
@@ -835,26 +951,28 @@
         kernel,
         out_shape=[jax.ShapeDtypeStruct(*v) for v in outputs.values()],
         in_specs=in_specs,
-        out_specs=[pl.BlockSpec(memory_space=pltpu.VMEM)] * len(outputs),
+        out_specs=[pl.BlockSpec(memory_space=pl.ANY)] * len(outputs),
         scratch_shapes=list(scratch.values()),
         compiler_params=pltpu.CompilerParams(
             collective_id=0, has_side_effects=True, vmem_limit_bytes=67043328
         ),
         name="layer",
     )(*inputs.values())
-    out = types.SimpleNamespace(**dict(zip(outputs, results)))
-    terms = out.terms_out.reshape(-1)
-    me = lax.axis_index("seq") * C + lax.axis_index("ctx")
-
-    def mine(start, array):
-        n = array.shape[0]
-        return lax.dynamic_slice_in_dim(terms, start + me * n, n)
-
-    return (
-        out.layer_out[None], out.hidden_grad[None], mine(0, gain1), out.delta_query,
-        out.delta_key, out.delta_value, mine(2 * D, gainq), mine(2 * D + HD, gaink),
-        out.delta_out, mine(D, gain2), out.delta_gate, out.delta_up, out.delta_down,
-    )
+    finish_names = list(outputs) + list(final)
+
+    def finish(*refs):
+        finish_kernel(dims, types.SimpleNamespace(**dict(zip(finish_names, refs))))
+
+    out = pl.pallas_call(
+        finish,
+        out_shape=[jax.ShapeDtypeStruct(*v) for v in final.values()],
+        in_specs=[pl.BlockSpec(memory_space=pltpu.VMEM)] * len(outputs),
+        out_specs=[pl.BlockSpec(memory_space=pltpu.VMEM)] * len(final),
+        name="finish",
+    )(*results)
+    one_axis = [k for k, v in enumerate(final.values()) if v[0][0] == 1]
+    out = [o.reshape(-1) if k in one_axis else o for k, o in enumerate(out)]
+    return (out[0][None], out[1][None], *out[2:])
 
 
 def angles(places, head_size):
@@ -1088,6 +1206,7 @@
         tokens, length = args[0].shape[1], args[1].shape[1]
         fits = (
             mesh.shape["ctx"] == KEY_VALUE_HEADS == 8
+            and mesh.shape["seq"] == 4
             and length <= 1024
             and length % BLOCK == 0
             and tokens % RUN == 0

time: 215 us -> 200 us (0.930)
  local copies, waits for them, and re-layouts: 13 us -> 0.89 us
    unnamed x33 -> x8, local copies, waits for them, and re-layouts: 9.5 us -> 0.11 us
    pallas_call x1, Pallas kernels: 198 us -> 194 us  [fused_layer(): pl.pallas_call(kernel, out_shape=[jax.ShapeDtypeStruct(*v) for v in outpu...]
    pallas_call x0 -> x1, Pallas kernels: none -> 3.04 us  [fused_layer(): pl.pallas_call(finish, out_shape=[jax.ShapeDtypeStruct(*v) for v in final...]
    dynamic_slice x2 -> x0, local copies, waits for them, and re-layouts: 2.67 us -> none  [mine(): return lax.dynamic_slice_in_dim(terms, start + me * n, n)]
where the time goes in v3:
time: 200 us
  Pallas kernels  197 us (98%)
    pallas_call x1, Pallas kernels, fused_layer(): pl.pallas_call(kernel, out_shape=[jax.ShapeDtypeStruct(*v) for v in outpu...  194 us

profile of v3, /device:TPU:9, one launch (start us, length us, event | category | flops | bytes accessed | tf_op | source)
XLA Modules:
  0.0 199.8 jit_solution(3167383652812813681)
XLA Ops:
  0.6 0.8 slice.3
  1.5 0.1 select_reduce_fusion
  1.6 0.0 copy-start
  1.6 0.0 copy-start.1
  1.6 0.0 copy-start.2
  1.6 0.0 copy-start.3
  1.6 0.6 pad_add_fusion.refs_0_
  2.2 0.0 copy-done
  2.2 0.0 copy-done.1
  2.2 0.0 copy-done.2
  2.3 0.0 copy-done.3
  2.3 0.7 fusion.9.refs_3_
  2.9 193.8 %layer.1 = (bf16[128,1024]{1,0:T(8,128)(2,1)}, f32[128,1024]{1,0:T(8,128)}, bf16[8,32,512]{2,1,0:T(8,128)(2,1)}, bf16[64,1024]{1,0:T(8,128)(2,1)}, bf16[8,32,768...) custom-call(s32[2,16]{1,0:T(2,128)} %pad_add_fusion.refs_0_, bf16[2,64,1024]{2,1,0:T(8,128)(2,1)} %bitcast.15, ...), custom_call_target="tpu_custom_call" | custom-call | tf_op jit(solution)/shard_map/layer/pallas_call | solution.py:950
  196.7 3.0 %finish.1 = (bf16[128,1024]{1,0:T(8,128)(2,1)}, f32[128,1024]{1,0:T(8,128)}, f32[1,32]{1,0:T(1,128)}, f32[32,2048]{1,0:T(8,128)}, f32[32,1024]{1,0:T(8,128)}, /*...) custom-call(bf16[128,1024]{1,0:T(8,128)(2,1)} %get-tuple-element.33., ...), custom_call_target="tpu_custom_call" | custom-call | tf_op jit(solution)/shard_map/finish/pallas_call | solution.py:966
  (2 shorter events, 0.0 us)
Async XLA Ops:
  1.6 0.7 copy-start
  1.6 0.7 copy-start.1
  1.6 0.7 copy-start.2
  1.6 0.7 copy-start.3

commit v4 on v3

--- a/solution.py
+++ b/solution.py
@@ -71,11 +71,6 @@
     chip_y, chip_x = lax.div(chip, 2), lax.rem(chip, 2)
     sibling = chip * 2 + (1 - core)
     flat = s * C + c
-    to_s, to_c = lax.rem(flat, S), lax.div(flat, S)
-    from_flat = S * c + s
-    from_s, from_c = lax.div(from_flat, C), lax.rem(from_flat, C)
-    moved = (to_s * C + to_c) != flat
-
     def partner(i):
         x = lax.rem(chip_x + lax.rem(i, 2), 2)
         y = lax.rem(chip_y + lax.div(i, 2), 2)
@@ -100,18 +95,7 @@
     loop(1, C, lambda i: hello(ctx=lax.rem(c + i, C)))
     loop(1, S, lambda i: hello(seq=lax.rem(s + i, S)))
 
-    @pl.when(moved)
-    def _():
-        hello(seq=to_s, ctx=to_c)
-        hello(seq=from_s, ctx=from_c)
-
-    @pl.when(moved)
-    def _():
-        pl.semaphore_wait(barrier, C + S)
-
-    @pl.when(jnp.logical_not(moved))
-    def _():
-        pl.semaphore_wait(barrier, C + S - 2)
+    pl.semaphore_wait(barrier, C - 1 + S - 1)
 
     def runs_of(b):
         return pl.ds(b * (BLOCK // RUN), BLOCK // RUN)
@@ -127,18 +111,31 @@
             return whole[kind].at[pl.ds(j * (T // RUN), T // RUN)]
         return whole[kind].at[rows_of(j * T, T)]
 
+    def half(ref, k):
+        part = pl.ds(k * (D // 2), D // 2)
+        return ref.at[:, :, part] if len(ref.shape) == 3 else ref.at[:, part]
+
     def gather_send(kind, src):
-        def go(i):
+        for i in (1, 2):
             remote(src, block(kind, c), r.ag_send.at[kind, i], r.ag_recv.at[kind, c],
                    ctx=partner(i) * 2 + core).start()
-
-        loop(1, CH, go)
         remote(src, block(kind, c), r.ag_send.at[kind, 0], r.ag_recv.at[kind, c], ctx=sibling).start()
 
     def gather_relay(kind, i):
         j = partner(i) * 2 + core
         arrived(block(kind, j), r.ag_recv.at[kind, j])
-        remote(block(kind, j), block(kind, j), r.ag_send.at[kind, CH - 1 + i], r.ag_recv.at[kind, j],
+
+        @pl.when(i == 1)
+        def _():
+            part = half(block(kind, j), 0)
+            remote(part, part, r.ag_send.at[kind, 3], r.ag_recv.at[kind, j], ctx=partner(2) * 2 + core).start()
+
+        @pl.when(i == 2)
+        def _():
+            part = half(block(kind, j), 1)
+            remote(part, part, r.ag_send.at[kind, 7], r.ag_recv.at[kind, j], ctx=partner(1) * 2 + core).start()
+
+        remote(block(kind, j), block(kind, j), r.ag_send.at[kind, 3 + i], r.ag_recv.at[kind, j],
                ctx=sibling).start()
 
     def gather_other(kind, i):
@@ -146,10 +143,10 @@
         arrived(block(kind, j), r.ag_recv.at[kind, j])
 
     def gather_done(kind):
-        def go(i):
+        for i in (0, 1, 2, 4, 5, 6):
             arrived(block(kind, c), r.ag_send.at[kind, i])
-
-        loop(0, 2 * CH - 1, go)
+        for i in (3, 7):
+            arrived(half(block(kind, c), 0), r.ag_send.at[kind, i])
 
     def scatter_pair(kind, i, partial):
         r.pair[i] = partial
@@ -162,38 +159,67 @@
         arrived(r.r1.at[bank, i], r.r1_recv.at[kind, i])
         mine = r.pair[i, rows_of(core * T, T), :] + r.r1[bank, i].astype(F32)
         r.s2[i] = mine.astype(BF)
-        remote(r.s2.at[i], r.r2.at[bank, i], r.rs_send.at[kind, CH + i],
-               r.r2_recv.at[kind, i], ctx=partner(i) * 2 + core).start()
+
+        def to(k, slot, send, recv):
+            remote(half(r.s2.at[i], k), half(r.r2.at[bank, slot], k), r.rs_send.at[kind, send],
+                   r.r2_recv.at[kind, recv], ctx=partner(1 + k) * 2 + core).start()
+
+        @pl.when(i == 1)
+        def _():
+            to(0, 0, CH, 0)
+
+        @pl.when(i == 2)
+        def _():
+            to(1, 0, CH + 1, 1)
+
+        @pl.when(i == 3)
+        def _():
+            to(0, 1, CH + 2, 2)
+            to(1, 1, CH + 3, 3)
 
     def scatter(kind, partial):
         def go(k):
-            i = lax.rem(k + 1, CH)
+            i = jnp.where(k == 0, 3, jnp.where(k == 3, 0, k))
             scatter_pair(kind, i, partial(i))
 
             @pl.when(k > 0)
             def _():
-                scatter_chip(kind, k)
+                scatter_chip(kind, jnp.where(k == 1, 3, k - 1))
 
         loop(0, CH, go)
+
+    def scatter_mid(kind):
+        bank = 1 if kind == 1 else 0
+        for k in (0, 1):
+            i = 2 - k
+            part = slice(k * (D // 2), (k + 1) * (D // 2))
+            arrived(half(r.r2.at[bank, 1], k), r.r2_recv.at[kind, 2 + k])
+            mine = r.pair[i, rows_of(core * T, T), part] + r.r1[bank, i, :, part].astype(F32)
+            r.s3[:, part] = (mine + r.r2[bank, 1, :, part].astype(F32)).astype(BF)
+            remote(half(r.s3, k), half(r.r2.at[bank, 2], k), r.rs_send.at[kind, CH + 4 + k],
+                   r.r2_recv.at[kind, 4 + k], ctx=partner(i) * 2 + core).start()
 
     def scatter_sum(kind):
         bank = 1 if kind == 1 else 0
         arrived(r.r1.at[bank, 0], r.r1_recv.at[kind, 0])
+        for k in (0, 1):
+            arrived(half(r.r2.at[bank, 0], k), r.r2_recv.at[kind, k])
+            arrived(half(r.r2.at[bank, 2], k), r.r2_recv.at[kind, 4 + k])
         total = r.pair[0, rows_of(core * T, T), :] + r.r1[bank, 0].astype(F32)
-        for i in range(1, CH):
-            arrived(r.r2.at[bank, i], r.r2_recv.at[kind, i])
-            total = total + r.r2[bank, i].astype(F32)
-        return total
+        return total + r.r2[bank, 0].astype(F32) + r.r2[bank, 2].astype(F32)
 
     def scatter_done(kind):
         loop(0, CH, lambda i: arrived(r.s1.at[0], r.rs_send.at[kind, i]))
-        loop(1, CH, lambda i: arrived(r.s2.at[1], r.rs_send.at[kind, CH + i]))
-
-    QKV, GATE, UP, OUT, DOWN = 0, 1, 2, 3, 4
+        loop(CH, CH + 6, lambda i: arrived(half(r.s3, 0), r.rs_send.at[kind, i]))
+
+    QKV, GATE, UP, OUT, DOWN, QKV2 = 0, 1, 2, 3, 4, 5
+    PH = PR // 2
 
     def plane(w, b):
         if w == QKV:
-            return r.w_qkv.at[rows_of(b * PR, PR)]
+            return r.w_qkv.at[rows_of(b * PR, PH)]
+        if w == QKV2:
+            return r.w_qkv.at[rows_of(b * PR + PH, PH)]
         if w == GATE:
             return r.w_gu.at[rows_of(b * PR, PR), pl.ds(0, U)]
         if w == UP:
@@ -211,6 +237,37 @@
         def _():
             remote(src, plane(w, s), r.z_send.at[w, 1, 0], r.z_recv.at[w, s], seq=s - 1).start()
 
+    rows_ref = {OUT: (0, r.w_o, OR), DOWN: (1, r.w_d, DR)}
+
+    def deal(w, b, src=None):
+        n, ref, size = rows_ref[w]
+        src = plane(w, b) if src is None else src
+        d = C * b + c
+        rank, spot = lax.div(d, S), lax.rem(d, S)
+        dst = ref.at[rows_of(spot * size, size)]
+
+        @pl.when(rank != c)
+        def _():
+            remote(src, dst, r.m_send.at[n, b], r.m_recv.at[n], ctx=rank).start()
+
+        @pl.when(rank == c)
+        def _():
+            local(src, dst, r.m_recv.at[n]).start()
+
+    def deal_arrive(w):
+        n, ref, size = rows_ref[w]
+        arrived(ref, r.m_recv.at[n])
+
+    def deal_done(w):
+        n, ref, size = rows_ref[w]
+
+        def go(b):
+            @pl.when(lax.div(C * b + c, S) != c)
+            def _():
+                arrived(plane(w, 0), r.m_send.at[n, b])
+
+        loop(0, S, go)
+
     def weight_hop(w, t):
         below, above = s - 1 - t, s + 1 + t
 
@@ -223,6 +280,9 @@
                 remote(plane(w, below), plane(w, below), r.z_send.at[w, 0, t + 1],
                        r.z_recv.at[w, below], seq=s + 1).start()
 
+            if w in rows_ref:
+                deal(w, below)
+
         @pl.when(above <= S - 1)
         def _():
             arrived(plane(w, above), r.z_recv.at[w, above])
@@ -231,6 +291,9 @@
             def _():
                 remote(plane(w, above), plane(w, above), r.z_send.at[w, 1, t + 1],
                        r.z_recv.at[w, above], seq=s - 1).start()
+
+            if w in rows_ref:
+                deal(w, above)
 
     def weight_done(w):
         for t in range(S - 1):
@@ -243,7 +306,7 @@
                 arrived(plane(w, s), r.z_send.at[w, 1, t])
 
     GU = GATE
-    sent = {QKV: (r.g_qkv, PR), OUT: (r.g_o, OR), GU: (r.g_gu, PR), DOWN: (r.g_d, DR)}
+    sent = {QKV: (r.g_qkv, PR), OUT: (r.h_o, OR), GU: (r.g_gu, PR), DOWN: (r.h_d, DR)}
     got = {QKV: r.t_qkv, OUT: r.t_o, GU: r.t_gu, DOWN: r.t_d}
     halfway = {QKV: r.c_qkv, OUT: r.c_o, GU: r.c_gu, DOWN: r.c_d}
     summed = {QKV: r.u_qkv, OUT: r.u_o, GU: r.u_gu, DOWN: r.u_d}
@@ -303,7 +366,7 @@
     def grad_done(w):
         loop(1, S, lambda i: arrived(got[w].at[0], r.gz_send.at[w, lax.rem(s + i, S)]))
 
-    final = {QKV: r.f_qkv, GU: r.f_gu, OUT: r.f_o, DOWN: r.f_d}
+    final = {QKV: r.f_qkv, GU: r.f_gu}
 
     def columns_send(n, w):
         def go(i):
@@ -320,24 +383,39 @@
     def columns_done(n, w):
         loop(1, C, lambda i: arrived(final[w].at[0], r.gp_send.at[n, i]))
 
-    def rows_send(n, w):
-        @pl.when(moved)
-        def _():
-            remote(summed[w], final[w], r.row_send.at[n], r.row_recv.at[n], seq=from_s, ctx=from_c).start()
-
-        @pl.when(jnp.logical_not(moved))
-        def _():
-            final[w][...] = summed[w][...]
-
-    def rows_arrive(n, w):
-        @pl.when(moved)
-        def _():
-            arrived(final[w], r.row_recv.at[n])
-
-    def rows_done(n, w):
-        @pl.when(moved)
-        def _():
-            arrived(final[w], r.row_send.at[n])
+    undealt = {OUT: (0, r.g_o, r.h_o, OR), DOWN: (1, r.g_d, r.h_d, DR)}
+
+    def undeal(w):
+        n, src, dst, size = undealt[w]
+
+        def go(j):
+            d = S * c + j
+            b, place = lax.div(d, C), lax.rem(d, C)
+            here, there = src.at[rows_of(j * size, size)], dst.at[rows_of(b * size, size)]
+
+            @pl.when(place != c)
+            def _():
+                remote(here, there, r.u_send.at[n, j], r.u_recv.at[n], ctx=place).start()
+
+            @pl.when(place == c)
+            def _():
+                local(here, there, r.u_recv.at[n]).start()
+
+        loop(0, S, go)
+
+    def undeal_arrive(w):
+        n, src, dst, size = undealt[w]
+        arrived(dst, r.u_recv.at[n])
+
+    def undeal_done(w):
+        n, src, dst, size = undealt[w]
+
+        def go(j):
+            @pl.when(lax.rem(S * c + j, C) != c)
+            def _():
+                arrived(src.at[pl.ds(0, size)], r.u_send.at[n, j])
+
+        loop(0, S, go)
 
     gains_own = r.gains_all.at[flat]
     gain_copy = local(r.gains_in, gains_own, r.gain_recv.at[s])
@@ -383,50 +461,17 @@
     def spread_done(n, w):
         arrived(columns_of[w].at[pl.ds(0, (C - 1) * RW)], r.w_send.at[n])
 
-    rows_ref = {OUT: (r.w_o, OR), DOWN: (r.w_d, DR)}
-
-    def deal(n, w):
-        ref, size = rows_ref[w]
-
-        def go(b):
-            d = C * b + c
-            rank, spot = lax.div(d, S), lax.rem(d, S)
-            dst = ref.at[rows_of(spot * size, size)]
-
-            @pl.when(rank != c)
-            def _():
-                remote(plane(w, b), dst, r.m_send.at[n, b], r.m_recv.at[n], ctx=rank).start()
-
-            @pl.when(rank == c)
-            def _():
-                local(plane(w, b), dst, r.m_recv.at[n]).start()
-
-        loop(0, S, go)
-
-    def deal_arrive(n, w):
-        arrived(rows_ref[w][0], r.m_recv.at[n])
-
-    def deal_done(n, w):
-        def go(b):
-            @pl.when(lax.div(C * b + c, S) != c)
-            def _():
-                arrived(plane(w, 0), r.m_send.at[n, b])
-
-        loop(0, S, go)
-
-    def own_rows(n, w, src):
-        local(src, plane(w, s), r.local_sem.at[3 + n]).start()
-        weight_start(w, src)
-
-    own_rows(0, OUT, r.wo_in)
+    weight_start(OUT, r.wo_in)
     spread(0, QKV, qkv_piece)
     local(r.x_in, block(X, c), r.local_sem.at[0]).start()
     local(r.table_in, r.table, r.local_sem.at[1]).start()
     gather_send(X, r.x_in)
+    deal(OUT, s, r.wo_in)
     spread(1, GU, gu_piece)
     weight_hop(OUT, 0)
     spread_arrive(0, QKV)
     weight_start(QKV)
+    weight_start(QKV2)
     arrived(r.gains_all.at[pl.ds(s * C, C)], r.gain_recv.at[s])
 
     def gain_far(i):
@@ -434,7 +479,6 @@
         remote(mine, mine, r.gain_send.at[C + i], r.gain_recv.at[s], seq=lax.rem(s + i, S)).start()
 
     loop(1, S, gain_far)
-    weight_hop(OUT, 1)
 
     arrived(r.table, r.local_sem.at[1])
 
@@ -447,12 +491,12 @@
         r.sine[rows, :] = jnp.where(first, -other, both)
 
     loop(0, L // T, tables)
-    weight_hop(OUT, 2)
-    arrived(plane(OUT, s), r.local_sem.at[3])
-    deal(0, OUT)
+    arrived(block(X, c), r.local_sem.at[0])
     weight_hop(QKV, 0)
-    arrived(block(X, c), r.local_sem.at[0])
-    loop(1, CH, lambda i: gather_relay(X, i))
+    gather_relay(X, 1)
+    gather_relay(X, 2)
+    weight_hop(QKV2, 0)
+    gather_relay(X, 3)
     local(r.g_in, block(G, c), r.local_sem.at[2]).start()
     gather_send(G, r.g_in)
 
@@ -490,9 +534,13 @@
 
     loop(0, NR, first_norm)
     weight_hop(QKV, 1)
+    weight_hop(QKV2, 1)
+    weight_hop(OUT, 1)
+    weight_start(DOWN, r.wd_in)
+    deal(DOWN, s, r.wd_in)
     spread_arrive(1, GU)
-    weight_start(GATE)
     weight_hop(QKV, 2)
+    weight_hop(QKV2, 2)
 
     def rotate(u, rows):
         return u * r.cosine[rows, :] + pltpu.roll(u, HD // 2, 1) * r.sine[rows, :]
@@ -517,13 +565,18 @@
         r.v_t[:, rows] = v.T.astype(BF)
 
     loop(0, NB, project)
-    loop(1, CH, lambda i: gather_relay(G, i))
 
     def attend(qb):
         @pl.when(qb == NB - 2)
         def _():
-            weight_hop(GATE, 0)
-            weight_start(UP)
+            gather_relay(G, 1)
+            gather_relay(G, 2)
+            weight_hop(OUT, 2)
+
+        @pl.when(qb == NB - 1)
+        def _():
+            weight_hop(DOWN, 0)
+            weight_start(GATE)
 
         cols = rows_of(qb * BLOCK, BLOCK)
 
@@ -560,13 +613,14 @@
 
     loop(0, NR, unsort)
 
-    deal_arrive(0, OUT)
+    gather_relay(G, 3)
+    deal_arrive(OUT)
     scatter(0, lambda i: nn(r.o[rows_of(partner(i) * 2 * T, 2 * T), :], r.w_o[...]))
-    weight_hop(GATE, 1)
-    own_rows(1, DOWN, r.wd_in)
-    weight_hop(UP, 0)
-    weight_hop(GATE, 2)
-    weight_hop(UP, 1)
+    weight_hop(DOWN, 1)
+    weight_start(UP)
+    weight_hop(GATE, 0)
+    scatter_mid(0)
+    weight_hop(DOWN, 2)
     y1 = own_x() + scatter_sum(0)
     scatter_done(0)
     r.y1[...] = y1
@@ -574,57 +628,46 @@
     r.h2_all[rows_of(c * T, T), :] = h2_own
     gather_send(H2, block(H2, c))
 
-    weight_hop(UP, 2)
+    weight_hop(GATE, 1)
     arrived(block(G, c), r.local_sem.at[2])
     arrived(block(G, sibling), r.ag_recv.at[G, sibling])
     loop(1, CH, lambda i: gather_other(G, i))
+    deal_arrive(DOWN)
+
+    def act_grad(b):
+        rows = rows_of(b * BLOCK, BLOCK)
+        r.d_act[rows, :] = nt(r.g_all[rows, :], r.w_d[...])
+
+    loop(0, NB, act_grad)
+    weight_hop(UP, 0)
+    gather_relay(H2, 1)
+    gather_relay(H2, 2)
+    weight_hop(GATE, 2)
+    weight_hop(UP, 1)
+    gather_relay(H2, 3)
     arrived(block(H2, sibling), r.ag_recv.at[H2, sibling])
+    loop(1, CH, lambda i: gather_other(H2, i))
+
+    def feed_gate(b):
+        rows = rows_of(b * BLOCK, BLOCK)
+        r.gate[rows, :] = nn(r.h2_all[rows, :], r.w_gu[:, :U])
+
+    loop(0, NB, feed_gate)
+    weight_hop(UP, 2)
 
     def feed(i):
-        @pl.when(i > 0)
-        def _():
-            gather_relay(H2, i)
-            gather_other(H2, i)
-
-        @pl.when(i == 1)
-        def _():
-            weight_hop(DOWN, 0)
-
-        @pl.when(i == 2)
-        def _():
-            weight_hop(DOWN, 1)
-
         rows = rows_of(partner(i) * 2 * T, 2 * T)
-        h2 = r.h2_all[rows, :]
-        gate = nn(h2, r.w_gu[:, :U])
-        up = nn(h2, r.w_gu[:, U:])
+        up = nn(r.h2_all[rows, :], r.w_gu[:, U:])
+        gate = r.gate[rows, :]
         sig = 1.0 / (1.0 + jnp.exp(-gate))
         silu = gate * sig
         r.act[rows, :] = (silu * up).astype(BF)
-        r.slope[rows, :] = up * sig * (1.0 + gate * (1.0 - sig))
-        r.silu[rows, :] = silu
-
-    loop(0, CH, feed)
-    weight_hop(DOWN, 2)
-    arrived(plane(DOWN, s), r.local_sem.at[4])
-    deal(1, DOWN)
-    deal_arrive(1, DOWN)
-
-    def feed_back(i):
-        rows = rows_of(partner(i) * 2 * T, 2 * T)
-        d_act = nt(r.g_all[rows, :], r.w_d[...])
-        r.d_gu[rows, :U] = (d_act * r.slope[rows, :]).astype(BF)
-        r.d_gu[rows, U:] = (d_act * r.silu[rows, :]).astype(BF)
+        d_act = r.d_act[rows, :]
+        r.d_gu[rows, :U] = (d_act * up * sig * (1.0 + gate * (1.0 - sig))).astype(BF)
+        r.d_gu[rows, U:] = (d_act * silu).astype(BF)
         return nt(r.d_gu[rows, :], r.w_gu[...])
 
-    scatter(2, feed_back)
-
-    def down_grad(m):
-        cols = rows_of(m * HD, HD)
-        r.g_d[cols, :] = tn(r.act[:, cols], r.g_all[...]).astype(BF)
-
-    loop(0, U // HD, down_grad)
-    loop(0, S, lambda i: grad_out(DOWN, grad_order(i)))
+    scatter(2, feed)
 
     def gu_grad(i):
         p = grad_order(i)
@@ -633,9 +676,13 @@
         grad_out(GU, p)
 
     loop(0, S, gu_grad)
-    grad_combine(DOWN, 0)
-    grad_combine(DOWN, 1)
-
+    scatter_mid(2)
+
+    def down_grad(m):
+        cols = rows_of(m * HD, HD)
+        r.g_d[cols, :] = tn(r.act[:, cols], r.g_all[...]).astype(BF)
+
+    loop(0, U // HD, down_grad)
     d_h2 = scatter_sum(2)
     scatter_done(2)
     y1 = r.y1[...]
@@ -650,13 +697,20 @@
     for k in range(WT):
         r.terms[WT + k : WT + k + 1, :] = term2[:, k * HD : (k + 1) * HD]
 
-    scatter(1, lambda i: nn(r.act[rows_of(partner(i) * 2 * T, 2 * T), :], r.w_d[...]))
     arrived(block(DY, sibling), r.ag_recv.at[DY, sibling])
 
     def out_grad(i):
+        @pl.when(i == 1)
+        def _():
+            gather_relay(DY, 1)
+            gather_relay(DY, 2)
+
+        @pl.when(i == 3)
+        def _():
+            gather_relay(DY, 3)
+
         @pl.when(i > 0)
         def _():
-            gather_relay(DY, i)
             gather_other(DY, i)
 
         rows = rows_of(partner(i) * 2 * T, 2 * T)
@@ -670,7 +724,8 @@
         r.g_o[cols, :] = tn(r.o[:, cols], r.dy_all[...]).astype(BF)
 
     loop(0, H * HD // HD, out_weight)
-    loop(0, S, lambda i: grad_out(OUT, grad_order(i)))
+    undeal(DOWN)
+    undeal(OUT)
     grad_combine(GU, 0)
 
     def sort(k):
@@ -682,6 +737,12 @@
     r.sums[...] = jnp.zeros_like(r.sums)
 
     def attend_back(qb):
+        @pl.when(qb == NB - 1)
+        def _():
+            undeal_arrive(DOWN)
+            loop(0, S, lambda i: grad_out(DOWN, grad_order(i)))
+            grad_combine(GU, 1)
+
         cols = rows_of(qb * BLOCK, BLOCK)
         d_o_t, d_o_low, row, factor = [], [], [], []
         for h in range(H):
@@ -734,6 +795,8 @@
         r.d_qkv[runs_of(b), :, (H + 1) * HD :] = r.d_v[rows, :].astype(BF).reshape(-1, RUN, HD)
 
     loop(0, NB, key_back)
+    undeal_arrive(OUT)
+    loop(0, S, lambda i: grad_out(OUT, grad_order(i)))
 
     def qkv_grad(i):
         p = grad_order(i)
@@ -742,11 +805,6 @@
         grad_out(QKV, p)
 
     loop(0, S, qkv_grad)
-    grad_combine(GU, 1)
-
-    r.y_out[...] = (r.y1[...] + scatter_sum(1)).astype(BF)
-    local(r.y_out, r.layer_out, r.out_sem.at[0]).start()
-    scatter_done(1)
 
     def in_chip(i):
         j = partner(i) * 2
@@ -756,13 +814,11 @@
         return nt(jnp.concatenate(parts, axis=0), r.w_qkv[...])
 
     scatter(3, in_chip)
-    grad_sum(DOWN)
-    rows_send(1, DOWN)
-    grad_combine(OUT, 0)
-    grad_combine(OUT, 1)
+    grad_combine(DOWN, 0)
+    scatter_mid(3)
     grad_sum(GU)
     columns_send(1, GU)
-    grad_combine(QKV, 0)
+    grad_combine(DOWN, 1)
     d_h1 = scatter_sum(3)
     x = own_x()
     r1 = inverse_root(x)
@@ -779,9 +835,21 @@
                seq=lax.rem(s + i, S)).start()
 
     loop(1, S, terms_far)
+    scatter_done(3)
+    grad_combine(OUT, 0)
+    scatter(1, lambda i: nn(r.act[rows_of(partner(i) * 2 * T, 2 * T), :], r.w_d[...]))
+    grad_combine(OUT, 1)
+    scatter_mid(1)
+    columns_arrive(1, GU)
+    local(r.f_gu, r.gu_out, r.out_sem.at[3]).start()
+    grad_sum(DOWN)
+    local(r.u_d, r.down_out, r.out_sem.at[2]).start()
+    grad_combine(QKV, 0)
+    r.y_out[...] = (r.y1[...] + scatter_sum(1)).astype(BF)
+    local(r.y_out, r.layer_out, r.out_sem.at[0]).start()
     grad_combine(QKV, 1)
     grad_sum(OUT)
-    rows_send(0, OUT)
+    local(r.u_o, r.o_out, r.out_sem.at[4]).start()
     grad_sum(QKV)
     columns_send(0, QKV)
     total = r.terms[...]
@@ -797,12 +865,6 @@
 
     loop(1, C, terms_near)
 
-    rows_arrive(1, DOWN)
-    local(r.f_d, r.down_out, r.out_sem.at[2]).start()
-    columns_arrive(1, GU)
-    local(r.f_gu, r.gu_out, r.out_sem.at[3]).start()
-    rows_arrive(0, OUT)
-    local(r.f_o, r.o_out, r.out_sem.at[4]).start()
     columns_arrive(0, QKV)
     local(r.f_qkv, r.qkv_out, r.out_sem.at[5]).start()
     total = r.terms_sum[...]
@@ -819,22 +881,22 @@
         gather_done(kind)
     spread_done(0, QKV)
     spread_done(1, GU)
-    deal_done(0, OUT)
-    deal_done(1, DOWN)
-    for w in (QKV, GATE, UP, OUT, DOWN):
+    deal_done(OUT)
+    deal_done(DOWN)
+    undeal_done(OUT)
+    undeal_done(DOWN)
+    for w in (QKV, QKV2, GATE, UP, OUT, DOWN):
         weight_done(w)
     for w in (QKV, OUT, GU, DOWN):
         grad_done(w)
     columns_done(0, QKV)
     columns_done(1, GU)
-    rows_done(0, OUT)
-    rows_done(1, DOWN)
-    scatter_done(3)
+    scatter_done(1)
     loop(1, S, lambda i: arrived(r.terms, r.t_send.at[i]))
     loop(1, C, lambda i: arrived(r.terms, r.t_send.at[S + i]))
     pairs = (
-        (r.y_out, r.layer_out), (r.x_grad, r.hidden_grad), (r.f_d, r.down_out), (r.f_gu, r.gu_out),
-        (r.f_o, r.o_out), (r.f_qkv, r.qkv_out), (r.terms_all, r.terms_out),
+        (r.y_out, r.layer_out), (r.x_grad, r.hidden_grad), (r.u_d, r.down_out), (r.f_gu, r.gu_out),
+        (r.u_o, r.o_out), (r.f_qkv, r.qkv_out), (r.terms_all, r.terms_out),
     )
     for k, (src, dst) in enumerate(pairs):
         local(src, dst, r.out_sem.at[k]).wait()
@@ -918,26 +980,26 @@
         gainq=V((1, HD), F32), gaink=V((1, HD), F32), q_lin=V((H, L, HD), F32), k_lin=V((L, HD), F32),
         q_rot=V((H, L, HD), BF), k_rot=V((L, HD), BF), v=V((L, HD), BF), k_t=V((HD, L), BF),
         v_t=V((HD, L), BF), e=V((H, L, L), BF), l_inv=V((H, 8, L), F32), o_t=V((H, HD, L), F32),
-        o_sorted=V((L // RUN, RUN, H * HD), BF), o=V((L, H * HD), BF), y1=V((T, D), F32), slope=V((L, U), F32), silu=V((L, U), F32),
+        o_sorted=V((L // RUN, RUN, H * HD), BF), o=V((L, H * HD), BF), y1=V((T, D), F32), gate=V((L, U), F32), d_act=V((L, U), F32),
         act=V((L, U), BF), d_gu=V((L, 2 * U), BF), d_y1=V((T, D), F32), d_o=V((L // RUN, RUN, H * HD), BF),
         d_o_sorted=V((L, H * HD), BF), do_t=V((H, HD, BLOCK), BF), do_l=V((H, BLOCK, HD), BF),
         d_k=V((L, HD), F32), d_v=V((L, HD), F32), d_qkv=V((L // RUN, RUN, AC), BF), sums=V((8, HD), F32),
         pair=V((CH, 2 * T, D), F32), s1=V((CH, T, D), BF), r1=V((2, CH, T, D), BF),
-        s2=V((CH, T, D), BF), r2=V((2, CH, T, D), BF),
+        s2=V((CH, T, D), BF), r2=V((2, 3, T, D), BF), s3=V((T, D), BF),
         g_qkv=V((D, AC), BF), g_o=V((H * HD, D), BF), g_gu=V((D, 2 * U), BF), g_d=V((U, D), BF),
         t_qkv=V((2, PR, AC), BF), t_o=V((2, OR, D), BF), t_gu=V((2, PR, 2 * U), BF), t_d=V((2, DR, D), BF),
         c_qkv=V((2, PR, AC), BF), c_o=V((2, OR, D), BF), c_gu=V((2, PR, 2 * U), BF), c_d=V((2, DR, D), BF),
         z_o=V((S, OR, D), BF), z_d=V((S, DR, D), BF), y_out=V((T, D), BF), x_grad=V((T, D), F32), terms_all=V(*TR_shape),
         u_qkv=V((PR, AC), BF), u_o=V((OR, D), BF), u_gu=V((PR, 2 * U), BF), u_d=V((DR, D), BF),
-        f_qkv=V((C, RW, AC), BF), f_o=V((OR, D), BF), f_gu=V((C, RW, 2 * U), BF), f_d=V((DR, D), BF),
+        f_qkv=V((C, RW, AC), BF), h_o=V((S * OR, D), BF), f_gu=V((C, RW, 2 * U), BF), h_d=V((S * DR, D), BF),
         terms=V((TR, HD), F32), terms_z=V((S, TR, HD), F32), terms_sum=V((TR, HD), F32),
         terms_p=V((C, TR, HD), F32),
-        ag_send=DMA((4, 2 * CH)), ag_recv=DMA((4, C)), rs_send=DMA((4, 2 * CH)), r1_recv=DMA((4, CH)),
-        r2_recv=DMA((4, CH)), z_send=DMA((5, 2, S)), z_recv=DMA((5, S)), gz_send=DMA((5, S)),
-        gz_recv=DMA((5, 2)), gc_recv=DMA((5, 2)), gp_send=DMA((2, C)), gp_recv=DMA((2, C)), row_send=DMA((2,)),
-        row_recv=DMA((2,)), w_send=DMA((2,)), w_recv=DMA((2,)), m_send=DMA((2, S)), m_recv=DMA((2,)),
+        ag_send=DMA((4, 2 * CH)), ag_recv=DMA((4, C)), rs_send=DMA((4, CH + 6)), r1_recv=DMA((4, CH)),
+        r2_recv=DMA((4, 6)), z_send=DMA((6, 2, S)), z_recv=DMA((6, S)), gz_send=DMA((5, S)),
+        gz_recv=DMA((5, 2)), gc_recv=DMA((5, 2)), gp_send=DMA((2, C)), gp_recv=DMA((2, C)), u_send=DMA((2, S)),
+        u_recv=DMA((2,)), w_send=DMA((2,)), w_recv=DMA((2,)), m_send=DMA((2, S)), m_recv=DMA((2,)),
         gain_send=DMA((C + S,)), gain_recv=DMA((S,)), t_send=DMA((S + C,)), t_recv=DMA((S + C,)),
-        local_sem=DMA((5,)), out_sem=DMA((7,)),
+        local_sem=DMA((3,)), out_sem=DMA((7,)),
     )
     names = list(inputs) + list(outputs) + list(scratch)
 

time: 200 us -> 179 us (0.90)
  Pallas kernels: 197 us -> 175 us
    pallas_call x1, Pallas kernels: 194 us -> 172 us  [fused_layer(): pl.pallas_call(kernel, out_shape=[jax.ShapeDtypeStruct(*v) for v in outpu...]
where the time goes in v4:
time: 179 us; the launch traced here: 178 us
  Pallas kernels  175 us (98%)
    pallas_call x1, Pallas kernels, fused_layer(): pl.pallas_call(kernel, out_shape=[jax.ShapeDtypeStruct(*v) for v in outpu...  172 us

profile of v4, /device:TPU:9, one launch (start us, length us, event | category | flops | bytes accessed | tf_op | source)
XLA Modules:
  0.0 177.9 jit_solution(2628278307406395638)
XLA Ops:
  0.6 0.8 slice.3
  1.5 0.1 select_reduce_fusion
  1.6 0.0 copy-start
  1.6 0.0 copy-start.1
  1.6 0.0 copy-start.2
  1.6 0.0 copy-start.3
  1.6 0.6 pad_add_fusion.refs_0_
  2.2 0.0 copy-done
  2.2 0.0 copy-done.1
  2.2 0.0 copy-done.2
  2.3 0.0 copy-done.3
  2.3 0.7 fusion.9.refs_3_
  2.9 171.9 %layer.1 = (bf16[128,1024]{1,0:T(8,128)(2,1)}, f32[128,1024]{1,0:T(8,128)}, bf16[8,32,512]{2,1,0:T(8,128)(2,1)}, bf16[64,1024]{1,0:T(8,128)(2,1)}, bf16[8,32,768...) custom-call(s32[2,16]{1,0:T(2,128)} %pad_add_fusion.refs_0_, bf16[2,64,1024]{2,1,0:T(8,128)(2,1)} %bitcast.15, ...), custom_call_target="tpu_custom_call" | custom-call | tf_op jit(solution)/shard_map/layer/pallas_call | solution.py:1012
  174.8 3.0 %finish.1 = (bf16[128,1024]{1,0:T(8,128)(2,1)}, f32[128,1024]{1,0:T(8,128)}, f32[1,32]{1,0:T(1,128)}, f32[32,2048]{1,0:T(8,128)}, f32[32,1024]{1,0:T(8,128)}, /*...) custom-call(bf16[128,1024]{1,0:T(8,128)(2,1)} %get-tuple-element.33., ...), custom_call_target="tpu_custom_call" | custom-call | tf_op jit(solution)/shard_map/finish/pallas_call | solution.py:1028
  (2 shorter events, 0.0 us)
Async XLA Ops:
  1.6 0.7 copy-start
  1.6 0.7 copy-start.1
  1.6 0.7 copy-start.2
  1.6 0.7 copy-start.3

commit v5 on v4

--- a/solution.py
+++ b/solution.py
@@ -188,6 +188,9 @@
 
         loop(0, CH, go)
 
+    def scatter_pairs(kind, partial):
+        loop(0, CH, lambda i: scatter_pair(kind, i, partial(i)))
+
     def scatter_mid(kind):
         bank = 1 if kind == 1 else 0
         for k in (0, 1):
@@ -224,7 +227,9 @@
             return r.w_gu.at[rows_of(b * PR, PR), pl.ds(0, U)]
         if w == UP:
             return r.w_gu.at[rows_of(b * PR, PR), pl.ds(U, U)]
-        return (r.z_o if w == OUT else r.z_d).at[b]
+        if w == DOWN:
+            return r.w_d.at[rows_of(b * DR, DR)]
+        return r.z_o.at[b]
 
     def weight_start(w, src=None):
         src = plane(w, s) if src is None else src
@@ -237,7 +242,7 @@
         def _():
             remote(src, plane(w, s), r.z_send.at[w, 1, 0], r.z_recv.at[w, s], seq=s - 1).start()
 
-    rows_ref = {OUT: (0, r.w_o, OR), DOWN: (1, r.w_d, DR)}
+    rows_ref = {OUT: (0, r.w_o, OR)}
 
     def deal(w, b, src=None):
         n, ref, size = rows_ref[w]
@@ -280,9 +285,6 @@
                 remote(plane(w, below), plane(w, below), r.z_send.at[w, 0, t + 1],
                        r.z_recv.at[w, below], seq=s + 1).start()
 
-            if w in rows_ref:
-                deal(w, below)
-
         @pl.when(above <= S - 1)
         def _():
             arrived(plane(w, above), r.z_recv.at[w, above])
@@ -292,8 +294,16 @@
                 remote(plane(w, above), plane(w, above), r.z_send.at[w, 1, t + 1],
                        r.z_recv.at[w, above], seq=s - 1).start()
 
-            if w in rows_ref:
-                deal(w, above)
+    def deal_hop(w, t):
+        below, above = s - 1 - t, s + 1 + t
+
+        @pl.when(below >= 0)
+        def _():
+            deal(w, below)
+
+        @pl.when(above <= S - 1)
+        def _():
+            deal(w, above)
 
     def weight_done(w):
         for t in range(S - 1):
@@ -306,7 +316,7 @@
                 arrived(plane(w, s), r.z_send.at[w, 1, t])
 
     GU = GATE
-    sent = {QKV: (r.g_qkv, PR), OUT: (r.h_o, OR), GU: (r.g_gu, PR), DOWN: (r.h_d, DR)}
+    sent = {QKV: (r.g_qkv, PR), OUT: (r.h_o, OR), GU: (r.g_gu, PR), DOWN: (r.g_d, DR)}
     got = {QKV: r.t_qkv, OUT: r.t_o, GU: r.t_gu, DOWN: r.t_d}
     halfway = {QKV: r.c_qkv, OUT: r.c_o, GU: r.c_gu, DOWN: r.c_d}
     summed = {QKV: r.u_qkv, OUT: r.u_o, GU: r.u_gu, DOWN: r.u_d}
@@ -383,7 +393,7 @@
     def columns_done(n, w):
         loop(1, C, lambda i: arrived(final[w].at[0], r.gp_send.at[n, i]))
 
-    undealt = {OUT: (0, r.g_o, r.h_o, OR), DOWN: (1, r.g_d, r.h_d, DR)}
+    undealt = {OUT: (0, r.g_o, r.h_o, OR)}
 
     def undeal(w):
         n, src, dst, size = undealt[w]
@@ -435,10 +445,12 @@
         )
 
     def gu_piece(j):
-        return (
-            (r.wg_in.at[:, rows_of(j * U, U)], slice(0, U)),
-            (r.wu_in.at[:, rows_of(j * U, U)], slice(U, 2 * U)),
-        )
+        return ((r.gu_own.at[j], slice(0, 2 * U)),)
+
+    def gu_order(k, ref):
+        for j in range(C):
+            parts = [ref[:, (C * b + j) * DR : (C * b + j + 1) * DR] for b in range(S)]
+            r.gu_own[j, :, k * U : (k + 1) * U] = jnp.concatenate(parts, axis=1)
 
     columns_of = {QKV: r.w_qkv, GU: r.w_gu}
 
@@ -465,9 +477,13 @@
     spread(0, QKV, qkv_piece)
     local(r.x_in, block(X, c), r.local_sem.at[0]).start()
     local(r.table_in, r.table, r.local_sem.at[1]).start()
+    local(r.wg_in, r.wg_own, r.local_sem.at[4]).start()
+    local(r.wu_in, r.wu_own, r.local_sem.at[5]).start()
     gather_send(X, r.x_in)
-    deal(OUT, s, r.wo_in)
-    spread(1, GU, gu_piece)
+    arrived(r.wg_own, r.local_sem.at[4])
+    gu_order(0, r.wg_own)
+    arrived(r.wu_own, r.local_sem.at[5])
+    gu_order(1, r.wu_own)
     weight_hop(OUT, 0)
     spread_arrive(0, QKV)
     weight_start(QKV)
@@ -492,11 +508,14 @@
 
     loop(0, L // T, tables)
     arrived(block(X, c), r.local_sem.at[0])
-    weight_hop(QKV, 0)
     gather_relay(X, 1)
     gather_relay(X, 2)
+    weight_hop(QKV, 0)
     weight_hop(QKV2, 0)
     gather_relay(X, 3)
+    spread(1, GU, gu_piece)
+    deal(OUT, s, r.wo_in)
+    deal_hop(OUT, 0)
     local(r.g_in, block(G, c), r.local_sem.at[2]).start()
     gather_send(G, r.g_in)
 
@@ -537,9 +556,11 @@
     weight_hop(QKV2, 1)
     weight_hop(OUT, 1)
     weight_start(DOWN, r.wd_in)
-    deal(DOWN, s, r.wd_in)
-    spread_arrive(1, GU)
+    local(r.wd_in, plane(DOWN, s), r.local_sem.at[3]).start()
+    deal_hop(OUT, 1)
     weight_hop(QKV, 2)
+    gather_relay(G, 1)
+    gather_relay(G, 2)
     weight_hop(QKV2, 2)
 
     def rotate(u, rows):
@@ -565,13 +586,14 @@
         r.v_t[:, rows] = v.T.astype(BF)
 
     loop(0, NB, project)
+    weight_hop(OUT, 2)
+    deal_hop(OUT, 2)
+    spread_arrive(1, GU)
 
     def attend(qb):
         @pl.when(qb == NB - 2)
         def _():
-            gather_relay(G, 1)
-            gather_relay(G, 2)
-            weight_hop(OUT, 2)
+            gather_relay(G, 3)
 
         @pl.when(qb == NB - 1)
         def _():
@@ -613,7 +635,6 @@
 
     loop(0, NR, unsort)
 
-    gather_relay(G, 3)
     deal_arrive(OUT)
     scatter(0, lambda i: nn(r.o[rows_of(partner(i) * 2 * T, 2 * T), :], r.w_o[...]))
     weight_hop(DOWN, 1)
@@ -622,7 +643,6 @@
     scatter_mid(0)
     weight_hop(DOWN, 2)
     y1 = own_x() + scatter_sum(0)
-    scatter_done(0)
     r.y1[...] = y1
     h2_own = (y1 * inverse_root(y1) * r.gain2[...]).astype(BF)
     r.h2_all[rows_of(c * T, T), :] = h2_own
@@ -632,7 +652,7 @@
     arrived(block(G, c), r.local_sem.at[2])
     arrived(block(G, sibling), r.ag_recv.at[G, sibling])
     loop(1, CH, lambda i: gather_other(G, i))
-    deal_arrive(DOWN)
+    arrived(plane(DOWN, s), r.local_sem.at[3])
 
     def act_grad(b):
         rows = rows_of(b * BLOCK, BLOCK)
@@ -644,16 +664,23 @@
     gather_relay(H2, 2)
     weight_hop(GATE, 2)
     weight_hop(UP, 1)
-    gather_relay(H2, 3)
     arrived(block(H2, sibling), r.ag_recv.at[H2, sibling])
-    loop(1, CH, lambda i: gather_other(H2, i))
-
-    def feed_gate(b):
-        rows = rows_of(b * BLOCK, BLOCK)
+
+    def feed_gate(i):
+        @pl.when(i == 3)
+        def _():
+            gather_relay(H2, 3)
+
+        @pl.when(i > 0)
+        def _():
+            gather_other(H2, i)
+
+        rows = rows_of(partner(i) * 2 * T, 2 * T)
         r.gate[rows, :] = nn(r.h2_all[rows, :], r.w_gu[:, :U])
 
-    loop(0, NB, feed_gate)
+    loop(0, CH, feed_gate)
     weight_hop(UP, 2)
+    scatter_done(0)
 
     def feed(i):
         rows = rows_of(partner(i) * 2 * T, 2 * T)
@@ -683,8 +710,8 @@
         r.g_d[cols, :] = tn(r.act[:, cols], r.g_all[...]).astype(BF)
 
     loop(0, U // HD, down_grad)
+    loop(0, S, lambda i: grad_out(DOWN, grad_order(i)))
     d_h2 = scatter_sum(2)
-    scatter_done(2)
     y1 = r.y1[...]
     r2 = inverse_root(y1)
     normed = y1 * r2
@@ -693,6 +720,8 @@
     r.d_y1[...] = d_y1
     r.dy_all[rows_of(c * T, T), :] = d_y1.astype(BF)
     gather_send(DY, block(DY, c))
+    scatter_done(2)
+    scatter_pairs(1, lambda i: nn(r.act[rows_of(partner(i) * 2 * T, 2 * T), :], r.w_d[...]))
     WT = D // HD
     for k in range(WT):
         r.terms[WT + k : WT + k + 1, :] = term2[:, k * HD : (k + 1) * HD]
@@ -724,8 +753,9 @@
         r.g_o[cols, :] = tn(r.o[:, cols], r.dy_all[...]).astype(BF)
 
     loop(0, H * HD // HD, out_weight)
-    undeal(DOWN)
     undeal(OUT)
+    for i in (3, 1, 2):
+        scatter_chip(1, i)
     grad_combine(GU, 0)
 
     def sort(k):
@@ -739,9 +769,9 @@
     def attend_back(qb):
         @pl.when(qb == NB - 1)
         def _():
-            undeal_arrive(DOWN)
-            loop(0, S, lambda i: grad_out(DOWN, grad_order(i)))
-            grad_combine(GU, 1)
+            undeal_arrive(OUT)
+            loop(0, S, lambda i: grad_out(OUT, grad_order(i)))
+            scatter_mid(1)
 
         cols = rows_of(qb * BLOCK, BLOCK)
         d_o_t, d_o_low, row, factor = [], [], [], []
@@ -795,8 +825,8 @@
         r.d_qkv[runs_of(b), :, (H + 1) * HD :] = r.d_v[rows, :].astype(BF).reshape(-1, RUN, HD)
 
     loop(0, NB, key_back)
-    undeal_arrive(OUT)
-    loop(0, S, lambda i: grad_out(OUT, grad_order(i)))
+    r.y_out[...] = (r.y1[...] + scatter_sum(1)).astype(BF)
+    local(r.y_out, r.layer_out, r.out_sem.at[0]).start()
 
     def qkv_grad(i):
         p = grad_order(i)
@@ -805,6 +835,8 @@
         grad_out(QKV, p)
 
     loop(0, S, qkv_grad)
+    grad_combine(GU, 1)
+    scatter_done(1)
 
     def in_chip(i):
         j = partner(i) * 2
@@ -837,16 +869,12 @@
     loop(1, S, terms_far)
     scatter_done(3)
     grad_combine(OUT, 0)
-    scatter(1, lambda i: nn(r.act[rows_of(partner(i) * 2 * T, 2 * T), :], r.w_d[...]))
     grad_combine(OUT, 1)
-    scatter_mid(1)
     columns_arrive(1, GU)
     local(r.f_gu, r.gu_out, r.out_sem.at[3]).start()
     grad_sum(DOWN)
     local(r.u_d, r.down_out, r.out_sem.at[2]).start()
     grad_combine(QKV, 0)
-    r.y_out[...] = (r.y1[...] + scatter_sum(1)).astype(BF)
-    local(r.y_out, r.layer_out, r.out_sem.at[0]).start()
     grad_combine(QKV, 1)
     grad_sum(OUT)
     local(r.u_o, r.o_out, r.out_sem.at[4]).start()
@@ -882,16 +910,13 @@
     spread_done(0, QKV)
     spread_done(1, GU)
     deal_done(OUT)
-    deal_done(DOWN)
     undeal_done(OUT)
-    undeal_done(DOWN)
     for w in (QKV, QKV2, GATE, UP, OUT, DOWN):
         weight_done(w)
     for w in (QKV, OUT, GU, DOWN):
         grad_done(w)
     columns_done(0, QKV)
     columns_done(1, GU)
-    scatter_done(1)
     loop(1, S, lambda i: arrived(r.terms, r.t_send.at[i]))
     loop(1, C, lambda i: arrived(r.terms, r.t_send.at[S + i]))
     pairs = (
@@ -912,11 +937,17 @@
     r.delta_down[...] = r.down_out[...].astype(F32)
     r.delta_out[...] = r.o_out[...].astype(F32)
     for j in range(C):
-        r.delta_gate[:, j * U : (j + 1) * U] = r.gu_out[j, :, :U].astype(F32)
-        r.delta_up[:, j * U : (j + 1) * U] = r.gu_out[j, :, U:].astype(F32)
         r.delta_query[:, j * H * HD : (j + 1) * H * HD] = r.qkv_out[j, :, : H * HD].astype(F32)
         r.delta_key[:, j * HD : (j + 1) * HD] = r.qkv_out[j, :, H * HD : (H + 1) * HD].astype(F32)
         r.delta_value[:, j * HD : (j + 1) * HD] = r.qkv_out[j, :, (H + 1) * HD :].astype(F32)
+
+    for k, ref in ((0, r.delta_gate), (1, r.delta_up)):
+        for d in range(0, S * C, 4):
+            parts = []
+            for e in range(d, d + 4):
+                first = k * U + (e // C) * dims.DR
+                parts.append(r.gu_out[e % C, :, first : first + dims.DR].astype(F32))
+            ref[:, d * dims.DR : (d + 4) * dims.DR] = jnp.concatenate(parts, axis=1)
 
     def own(ref, first_row, count):
         start = me * count
@@ -989,17 +1020,18 @@
         g_qkv=V((D, AC), BF), g_o=V((H * HD, D), BF), g_gu=V((D, 2 * U), BF), g_d=V((U, D), BF),
         t_qkv=V((2, PR, AC), BF), t_o=V((2, OR, D), BF), t_gu=V((2, PR, 2 * U), BF), t_d=V((2, DR, D), BF),
         c_qkv=V((2, PR, AC), BF), c_o=V((2, OR, D), BF), c_gu=V((2, PR, 2 * U), BF), c_d=V((2, DR, D), BF),
-        z_o=V((S, OR, D), BF), z_d=V((S, DR, D), BF), y_out=V((T, D), BF), x_grad=V((T, D), F32), terms_all=V(*TR_shape),
+        z_o=V((S, OR, D), BF), y_out=V((T, D), BF), x_grad=V((T, D), F32), terms_all=V(*TR_shape),
         u_qkv=V((PR, AC), BF), u_o=V((OR, D), BF), u_gu=V((PR, 2 * U), BF), u_d=V((DR, D), BF),
-        f_qkv=V((C, RW, AC), BF), h_o=V((S * OR, D), BF), f_gu=V((C, RW, 2 * U), BF), h_d=V((S * DR, D), BF),
+        f_qkv=V((C, RW, AC), BF), h_o=V((S * OR, D), BF), f_gu=V((C, RW, 2 * U), BF), gu_own=V((C, RW, 2 * U), BF),
+        wg_own=V((RW, C * U), BF), wu_own=V((RW, C * U), BF),
         terms=V((TR, HD), F32), terms_z=V((S, TR, HD), F32), terms_sum=V((TR, HD), F32),
         terms_p=V((C, TR, HD), F32),
         ag_send=DMA((4, 2 * CH)), ag_recv=DMA((4, C)), rs_send=DMA((4, CH + 6)), r1_recv=DMA((4, CH)),
         r2_recv=DMA((4, 6)), z_send=DMA((6, 2, S)), z_recv=DMA((6, S)), gz_send=DMA((5, S)),
-        gz_recv=DMA((5, 2)), gc_recv=DMA((5, 2)), gp_send=DMA((2, C)), gp_recv=DMA((2, C)), u_send=DMA((2, S)),
-        u_recv=DMA((2,)), w_send=DMA((2,)), w_recv=DMA((2,)), m_send=DMA((2, S)), m_recv=DMA((2,)),
+        gz_recv=DMA((5, 2)), gc_recv=DMA((5, 2)), gp_send=DMA((2, C)), gp_recv=DMA((2, C)), u_send=DMA((1, S)),
+        u_recv=DMA((1,)), w_send=DMA((2,)), w_recv=DMA((2,)), m_send=DMA((1, S)), m_recv=DMA((1,)),
         gain_send=DMA((C + S,)), gain_recv=DMA((S,)), t_send=DMA((S + C,)), t_recv=DMA((S + C,)),
-        local_sem=DMA((3,)), out_sem=DMA((7,)),
+        local_sem=DMA((6,)), out_sem=DMA((7,)),
     )
     names = list(inputs) + list(outputs) + list(scratch)
 

time: 179 us -> 171 us (0.955)
  Pallas kernels: 175 us -> 168 us
    pallas_call x1, Pallas kernels: 172 us -> 165 us  [fused_layer(): pl.pallas_call(kernel, out_shape=[jax.ShapeDtypeStruct(*v) for v in outpu...]
where the time goes in v5:
time: 171 us
  Pallas kernels  168 us (98%)
    pallas_call x1, Pallas kernels, fused_layer(): pl.pallas_call(kernel, out_shape=[jax.ShapeDtypeStruct(*v) for v in outpu...  165 us

profile of v5, /device:TPU:9, one launch (start us, length us, event | category | flops | bytes accessed | tf_op | source)
XLA Modules:
  0.0 170.7 jit_solution(746669007737852835)
XLA Ops:
  0.6 0.8 slice.3
  1.5 0.1 select_reduce_fusion
  1.6 0.0 copy-start
  1.6 0.0 copy-start.1
  1.6 0.0 copy-start.2
  1.6 0.0 copy-start.3
  1.6 0.6 pad_add_fusion.refs_0_
  2.2 0.0 copy-done
  2.2 0.0 copy-done.1
  2.2 0.0 copy-done.2
  2.3 0.0 copy-done.3
  2.3 0.7 fusion.9.refs_3_
  2.9 164.5 %layer.1 = (bf16[128,1024]{1,0:T(8,128)(2,1)}, f32[128,1024]{1,0:T(8,128)}, bf16[8,32,512]{2,1,0:T(8,128)(2,1)}, bf16[64,1024]{1,0:T(8,128)(2,1)}, bf16[8,32,768...) custom-call(s32[2,16]{1,0:T(2,128)} %pad_add_fusion.refs_0_, bf16[2,64,1024]{2,1,0:T(8,128)(2,1)} %bitcast.15, ...), custom_call_target="tpu_custom_call" | custom-call | tf_op jit(solution)/shard_map/layer/pallas_call | solution.py:1044
  167.5 3.2 %finish.1 = (bf16[128,1024]{1,0:T(8,128)(2,1)}, f32[128,1024]{1,0:T(8,128)}, f32[1,32]{1,0:T(1,128)}, f32[32,2048]{1,0:T(8,128)}, f32[32,1024]{1,0:T(8,128)}, /*...) custom-call(bf16[128,1024]{1,0:T(8,128)(2,1)} %get-tuple-element.33., ...), custom_call_target="tpu_custom_call" | custom-call | tf_op jit(solution)/shard_map/finish/pallas_call | solution.py:1060
  (2 shorter events, 0.0 us)
Async XLA Ops:
  1.6 0.7 copy-start
  1.6 0.7 copy-start.1
  1.6 0.7 copy-start.2
  1.6 0.7 copy-start.3

commit v6 on v5

--- a/solution.py
+++ b/solution.py
@@ -294,6 +294,18 @@
                 remote(plane(w, above), plane(w, above), r.z_send.at[w, 1, t + 1],
                        r.z_recv.at[w, above], seq=s - 1).start()
 
+    inner = jnp.logical_and(s > 0, s < S - 1)
+
+    def hop_inner(w, t):
+        @pl.when(inner)
+        def _():
+            weight_hop(w, t)
+
+    def hop_outer(w, t):
+        @pl.when(jnp.logical_not(inner))
+        def _():
+            weight_hop(w, t)
+
     def deal_hop(w, t):
         below, above = s - 1 - t, s + 1 + t
 
@@ -316,10 +328,10 @@
                 arrived(plane(w, s), r.z_send.at[w, 1, t])
 
     GU = GATE
-    sent = {QKV: (r.g_qkv, PR), OUT: (r.h_o, OR), GU: (r.g_gu, PR), DOWN: (r.g_d, DR)}
-    got = {QKV: r.t_qkv, OUT: r.t_o, GU: r.t_gu, DOWN: r.t_d}
-    halfway = {QKV: r.c_qkv, OUT: r.c_o, GU: r.c_gu, DOWN: r.c_d}
-    summed = {QKV: r.u_qkv, OUT: r.u_o, GU: r.u_gu, DOWN: r.u_d}
+    sent = {QKV: (r.g_q, PR), QKV2: (r.g_kv, PR), OUT: (r.h_o, OR), GU: (r.g_gu, PR), DOWN: (r.g_d, DR)}
+    got = {QKV: r.t_q, QKV2: r.t_kv, OUT: r.t_o, GU: r.t_gu, DOWN: r.t_d}
+    halfway = {QKV: r.c_q, QKV2: r.c_kv, OUT: r.c_o, GU: r.c_gu, DOWN: r.c_d}
+    summed = {QKV: r.u_q, QKV2: r.u_kv, OUT: r.u_o, GU: r.u_gu, DOWN: r.u_d}
     side = jnp.where(s >= 2, 1, 0)
 
     def grad_rows(w, p):
@@ -376,7 +388,7 @@
     def grad_done(w):
         loop(1, S, lambda i: arrived(got[w].at[0], r.gz_send.at[w, lax.rem(s + i, S)]))
 
-    final = {QKV: r.f_qkv, GU: r.f_gu}
+    final = {QKV: r.f_q, QKV2: r.f_kv, GU: r.f_gu}
 
     def columns_send(n, w):
         def go(i):
@@ -555,12 +567,11 @@
     weight_hop(QKV, 1)
     weight_hop(QKV2, 1)
     weight_hop(OUT, 1)
-    weight_start(DOWN, r.wd_in)
+    spread_arrive(1, GU)
+    weight_start(GATE)
     local(r.wd_in, plane(DOWN, s), r.local_sem.at[3]).start()
     deal_hop(OUT, 1)
     weight_hop(QKV, 2)
-    gather_relay(G, 1)
-    gather_relay(G, 2)
     weight_hop(QKV2, 2)
 
     def rotate(u, rows):
@@ -588,17 +599,17 @@
     loop(0, NB, project)
     weight_hop(OUT, 2)
     deal_hop(OUT, 2)
-    spread_arrive(1, GU)
 
     def attend(qb):
         @pl.when(qb == NB - 2)
         def _():
-            gather_relay(G, 3)
+            gather_relay(G, 1)
+            gather_relay(G, 2)
 
         @pl.when(qb == NB - 1)
         def _():
-            weight_hop(DOWN, 0)
-            weight_start(GATE)
+            hop_inner(GATE, 0)
+            weight_start(UP)
 
         cols = rows_of(qb * BLOCK, BLOCK)
 
@@ -637,64 +648,75 @@
 
     deal_arrive(OUT)
     scatter(0, lambda i: nn(r.o[rows_of(partner(i) * 2 * T, 2 * T), :], r.w_o[...]))
-    weight_hop(DOWN, 1)
-    weight_start(UP)
-    weight_hop(GATE, 0)
+    hop_inner(GATE, 1)
+    gather_relay(G, 3)
     scatter_mid(0)
-    weight_hop(DOWN, 2)
+    hop_inner(UP, 0)
     y1 = own_x() + scatter_sum(0)
     r.y1[...] = y1
     h2_own = (y1 * inverse_root(y1) * r.gain2[...]).astype(BF)
     r.h2_all[rows_of(c * T, T), :] = h2_own
     gather_send(H2, block(H2, c))
 
-    weight_hop(GATE, 1)
+    hop_inner(UP, 1)
+    weight_start(DOWN, r.wd_in)
+    hop_inner(GATE, 2)
+    for w in (GATE, UP):
+        for t in range(S - 1):
+            hop_outer(w, t)
+    hop_inner(UP, 2)
+    arrived(block(H2, sibling), r.ag_recv.at[H2, sibling])
+
+    def feed(i):
+        @pl.when(i == 1)
+        def _():
+            gather_relay(H2, 1)
+            gather_relay(H2, 2)
+            hop_inner(DOWN, 0)
+
+        @pl.when(i == 3)
+        def _():
+            gather_relay(H2, 3)
+            hop_inner(DOWN, 1)
+
+        @pl.when(i > 0)
+        def _():
+            gather_other(H2, i)
+
+        rows = rows_of(partner(i) * 2 * T, 2 * T)
+        both = nn(r.h2_all[rows, :], r.w_gu[...])
+        gate, up = both[:, :U], both[:, U:]
+        sig = 1.0 / (1.0 + jnp.exp(-gate))
+        silu = gate * sig
+        r.act[rows, :] = (silu * up).astype(BF)
+        r.slope[rows, :] = up * sig * (1.0 + gate * (1.0 - sig))
+        r.silu[rows, :] = silu
+
+    loop(0, CH, feed)
     arrived(block(G, c), r.local_sem.at[2])
     arrived(block(G, sibling), r.ag_recv.at[G, sibling])
     loop(1, CH, lambda i: gather_other(G, i))
+
+    def down_grad(m):
+        cols = rows_of(m * HD, HD)
+        r.g_d[cols, :] = tn(r.act[:, cols], r.g_all[...]).astype(BF)
+
+    loop(0, U // HD, down_grad)
+    loop(0, S, lambda i: grad_out(DOWN, grad_order(i)))
+    hop_outer(DOWN, 0)
+    hop_outer(DOWN, 1)
+    weight_hop(DOWN, 2)
     arrived(plane(DOWN, s), r.local_sem.at[3])
-
-    def act_grad(b):
-        rows = rows_of(b * BLOCK, BLOCK)
-        r.d_act[rows, :] = nt(r.g_all[rows, :], r.w_d[...])
-
-    loop(0, NB, act_grad)
-    weight_hop(UP, 0)
-    gather_relay(H2, 1)
-    gather_relay(H2, 2)
-    weight_hop(GATE, 2)
-    weight_hop(UP, 1)
-    arrived(block(H2, sibling), r.ag_recv.at[H2, sibling])
-
-    def feed_gate(i):
-        @pl.when(i == 3)
-        def _():
-            gather_relay(H2, 3)
-
-        @pl.when(i > 0)
-        def _():
-            gather_other(H2, i)
-
+    scatter_done(0)
+
+    def feed_back(i):
         rows = rows_of(partner(i) * 2 * T, 2 * T)
-        r.gate[rows, :] = nn(r.h2_all[rows, :], r.w_gu[:, :U])
-
-    loop(0, CH, feed_gate)
-    weight_hop(UP, 2)
-    scatter_done(0)
-
-    def feed(i):
-        rows = rows_of(partner(i) * 2 * T, 2 * T)
-        up = nn(r.h2_all[rows, :], r.w_gu[:, U:])
-        gate = r.gate[rows, :]
-        sig = 1.0 / (1.0 + jnp.exp(-gate))
-        silu = gate * sig
-        r.act[rows, :] = (silu * up).astype(BF)
-        d_act = r.d_act[rows, :]
-        r.d_gu[rows, :U] = (d_act * up * sig * (1.0 + gate * (1.0 - sig))).astype(BF)
-        r.d_gu[rows, U:] = (d_act * silu).astype(BF)
+        d_act = nt(r.g_all[rows, :], r.w_d[...])
+        r.d_gu[rows, :U] = (d_act * r.slope[rows, :]).astype(BF)
+        r.d_gu[rows, U:] = (d_act * r.silu[rows, :]).astype(BF)
         return nt(r.d_gu[rows, :], r.w_gu[...])
 
-    scatter(2, feed)
+    scatter(2, feed_back)
 
     def gu_grad(i):
         p = grad_order(i)
@@ -704,13 +726,7 @@
 
     loop(0, S, gu_grad)
     scatter_mid(2)
-
-    def down_grad(m):
-        cols = rows_of(m * HD, HD)
-        r.g_d[cols, :] = tn(r.act[:, cols], r.g_all[...]).astype(BF)
-
-    loop(0, U // HD, down_grad)
-    loop(0, S, lambda i: grad_out(DOWN, grad_order(i)))
+    grad_combine(DOWN, 0)
     d_h2 = scatter_sum(2)
     y1 = r.y1[...]
     r2 = inverse_root(y1)
@@ -756,6 +772,7 @@
     undeal(OUT)
     for i in (3, 1, 2):
         scatter_chip(1, i)
+    grad_combine(DOWN, 1)
     grad_combine(GU, 0)
 
     def sort(k):
@@ -771,7 +788,6 @@
         def _():
             undeal_arrive(OUT)
             loop(0, S, lambda i: grad_out(OUT, grad_order(i)))
-            scatter_mid(1)
 
         cols = rows_of(qb * BLOCK, BLOCK)
         d_o_t, d_o_low, row, factor = [], [], [], []
@@ -825,17 +841,21 @@
         r.d_qkv[runs_of(b), :, (H + 1) * HD :] = r.d_v[rows, :].astype(BF).reshape(-1, RUN, HD)
 
     loop(0, NB, key_back)
-    r.y_out[...] = (r.y1[...] + scatter_sum(1)).astype(BF)
-    local(r.y_out, r.layer_out, r.out_sem.at[0]).start()
+    scatter_mid(1)
 
     def qkv_grad(i):
         p = grad_order(i)
         cols = rows_of(p * PR, PR)
-        r.g_qkv[cols, :] = tn(r.h1[:, cols], r.d_qkv[...].reshape(L, AC)).astype(BF)
+        both = tn(r.h1[:, cols], r.d_qkv[...].reshape(L, AC)).astype(BF)
+        r.g_q[cols, :] = both[:, : H * HD]
+        r.g_kv[cols, :] = both[:, H * HD :]
         grad_out(QKV, p)
 
     loop(0, S, qkv_grad)
+    loop(0, S, lambda i: grad_out(QKV2, grad_order(i)))
     grad_combine(GU, 1)
+    r.y_out[...] = (r.y1[...] + scatter_sum(1)).astype(BF)
+    local(r.y_out, r.layer_out, r.out_sem.at[0]).start()
     scatter_done(1)
 
     def in_chip(i):
@@ -846,11 +866,11 @@
         return nt(jnp.concatenate(parts, axis=0), r.w_qkv[...])
 
     scatter(3, in_chip)
-    grad_combine(DOWN, 0)
+    grad_combine(OUT, 0)
     scatter_mid(3)
     grad_sum(GU)
     columns_send(1, GU)
-    grad_combine(DOWN, 1)
+    grad_combine(OUT, 1)
     d_h1 = scatter_sum(3)
     x = own_x()
     r1 = inverse_root(x)
@@ -868,18 +888,20 @@
 
     loop(1, S, terms_far)
     scatter_done(3)
-    grad_combine(OUT, 0)
-    grad_combine(OUT, 1)
-    columns_arrive(1, GU)
-    local(r.f_gu, r.gu_out, r.out_sem.at[3]).start()
+    grad_combine(QKV, 0)
     grad_sum(DOWN)
     local(r.u_d, r.down_out, r.out_sem.at[2]).start()
-    grad_combine(QKV, 0)
     grad_combine(QKV, 1)
     grad_sum(OUT)
     local(r.u_o, r.o_out, r.out_sem.at[4]).start()
+    grad_combine(QKV2, 0)
+    columns_arrive(1, GU)
+    local(r.f_gu, r.gu_out, r.out_sem.at[3]).start()
+    grad_combine(QKV2, 1)
     grad_sum(QKV)
     columns_send(0, QKV)
+    grad_sum(QKV2)
+    columns_send(2, QKV2)
     total = r.terms[...]
     for i in range(1, S):
         p = lax.rem(s + i, S)
@@ -894,7 +916,7 @@
     loop(1, C, terms_near)
 
     columns_arrive(0, QKV)
-    local(r.f_qkv, r.qkv_out, r.out_sem.at[5]).start()
+    local(r.f_q, r.q_out, r.out_sem.at[5]).start()
     total = r.terms_sum[...]
     for i in range(1, C):
         j = lax.rem(c + i, C)
@@ -902,6 +924,8 @@
         total = total + r.terms_p[j]
     r.terms_all[...] = total
     local(r.terms_all, r.terms_out, r.out_sem.at[6]).start()
+    columns_arrive(2, QKV2)
+    local(r.f_kv, r.kv_out, r.out_sem.at[7]).start()
 
     loop(1, C, lambda i: arrived(gains_own, r.gain_send.at[i]))
     loop(1, S, lambda i: arrived(r.gains_all.at[pl.ds(0, C)], r.gain_send.at[C + i]))
@@ -913,15 +937,16 @@
     undeal_done(OUT)
     for w in (QKV, QKV2, GATE, UP, OUT, DOWN):
         weight_done(w)
-    for w in (QKV, OUT, GU, DOWN):
+    for w in (QKV, QKV2, OUT, GU, DOWN):
         grad_done(w)
     columns_done(0, QKV)
+    columns_done(2, QKV2)
     columns_done(1, GU)
     loop(1, S, lambda i: arrived(r.terms, r.t_send.at[i]))
     loop(1, C, lambda i: arrived(r.terms, r.t_send.at[S + i]))
     pairs = (
         (r.y_out, r.layer_out), (r.x_grad, r.hidden_grad), (r.u_d, r.down_out), (r.f_gu, r.gu_out),
-        (r.u_o, r.o_out), (r.f_qkv, r.qkv_out), (r.terms_all, r.terms_out),
+        (r.u_o, r.o_out), (r.f_q, r.q_out), (r.terms_all, r.terms_out), (r.f_kv, r.kv_out),
     )
     for k, (src, dst) in enumerate(pairs):
         local(src, dst, r.out_sem.at[k]).wait()
@@ -937,9 +962,9 @@
     r.delta_down[...] = r.down_out[...].astype(F32)
     r.delta_out[...] = r.o_out[...].astype(F32)
     for j in range(C):
-        r.delta_query[:, j * H * HD : (j + 1) * H * HD] = r.qkv_out[j, :, : H * HD].astype(F32)
-        r.delta_key[:, j * HD : (j + 1) * HD] = r.qkv_out[j, :, H * HD : (H + 1) * HD].astype(F32)
-        r.delta_value[:, j * HD : (j + 1) * HD] = r.qkv_out[j, :, (H + 1) * HD :].astype(F32)
+        r.delta_query[:, j * H * HD : (j + 1) * H * HD] = r.q_out[j].astype(F32)
+        r.delta_key[:, j * HD : (j + 1) * HD] = r.kv_out[j, :, :HD].astype(F32)
+        r.delta_value[:, j * HD : (j + 1) * HD] = r.kv_out[j, :, HD:].astype(F32)
 
     for k, ref in ((0, r.delta_gate), (1, r.delta_up)):
         for d in range(0, S * C, 4):
@@ -992,7 +1017,7 @@
     )
     TR_shape = ((TR, HD), F32)
     outputs = dict(
-        layer_out=((T, D), BF), hidden_grad=((T, D), F32), qkv_out=((C, RW, AC), BF), o_out=((OR, D), BF),
+        layer_out=((T, D), BF), hidden_grad=((T, D), F32), q_out=((C, RW, H * HD), BF), kv_out=((C, RW, 2 * HD), BF), o_out=((OR, D), BF),
         gu_out=((C, RW, 2 * U), BF), down_out=((DR, D), BF), terms_out=TR_shape,
     )
     n1, n3 = D // (S * C), HD // (S * C)
@@ -1011,27 +1036,27 @@
         gainq=V((1, HD), F32), gaink=V((1, HD), F32), q_lin=V((H, L, HD), F32), k_lin=V((L, HD), F32),
         q_rot=V((H, L, HD), BF), k_rot=V((L, HD), BF), v=V((L, HD), BF), k_t=V((HD, L), BF),
         v_t=V((HD, L), BF), e=V((H, L, L), BF), l_inv=V((H, 8, L), F32), o_t=V((H, HD, L), F32),
-        o_sorted=V((L // RUN, RUN, H * HD), BF), o=V((L, H * HD), BF), y1=V((T, D), F32), gate=V((L, U), F32), d_act=V((L, U), F32),
+        o_sorted=V((L // RUN, RUN, H * HD), BF), o=V((L, H * HD), BF), y1=V((T, D), F32), slope=V((L, U), F32), silu=V((L, U), F32),
         act=V((L, U), BF), d_gu=V((L, 2 * U), BF), d_y1=V((T, D), F32), d_o=V((L // RUN, RUN, H * HD), BF),
         d_o_sorted=V((L, H * HD), BF), do_t=V((H, HD, BLOCK), BF), do_l=V((H, BLOCK, HD), BF),
         d_k=V((L, HD), F32), d_v=V((L, HD), F32), d_qkv=V((L // RUN, RUN, AC), BF), sums=V((8, HD), F32),
         pair=V((CH, 2 * T, D), F32), s1=V((CH, T, D), BF), r1=V((2, CH, T, D), BF),
         s2=V((CH, T, D), BF), r2=V((2, 3, T, D), BF), s3=V((T, D), BF),
-        g_qkv=V((D, AC), BF), g_o=V((H * HD, D), BF), g_gu=V((D, 2 * U), BF), g_d=V((U, D), BF),
-        t_qkv=V((2, PR, AC), BF), t_o=V((2, OR, D), BF), t_gu=V((2, PR, 2 * U), BF), t_d=V((2, DR, D), BF),
-        c_qkv=V((2, PR, AC), BF), c_o=V((2, OR, D), BF), c_gu=V((2, PR, 2 * U), BF), c_d=V((2, DR, D), BF),
+        g_q=V((D, H * HD), BF), g_kv=V((D, 2 * HD), BF), g_o=V((H * HD, D), BF), g_gu=V((D, 2 * U), BF), g_d=V((U, D), BF),
+        t_q=V((2, PR, H * HD), BF), t_kv=V((2, PR, 2 * HD), BF), t_o=V((2, OR, D), BF), t_gu=V((2, PR, 2 * U), BF), t_d=V((2, DR, D), BF),
+        c_q=V((2, PR, H * HD), BF), c_kv=V((2, PR, 2 * HD), BF), c_o=V((2, OR, D), BF), c_gu=V((2, PR, 2 * U), BF), c_d=V((2, DR, D), BF),
         z_o=V((S, OR, D), BF), y_out=V((T, D), BF), x_grad=V((T, D), F32), terms_all=V(*TR_shape),
-        u_qkv=V((PR, AC), BF), u_o=V((OR, D), BF), u_gu=V((PR, 2 * U), BF), u_d=V((DR, D), BF),
-        f_qkv=V((C, RW, AC), BF), h_o=V((S * OR, D), BF), f_gu=V((C, RW, 2 * U), BF), gu_own=V((C, RW, 2 * U), BF),
+        u_q=V((PR, H * HD), BF), u_kv=V((PR, 2 * HD), BF), u_o=V((OR, D), BF), u_gu=V((PR, 2 * U), BF), u_d=V((DR, D), BF),
+        f_q=V((C, RW, H * HD), BF), f_kv=V((C, RW, 2 * HD), BF), h_o=V((S * OR, D), BF), f_gu=V((C, RW, 2 * U), BF), gu_own=V((C, RW, 2 * U), BF),
         wg_own=V((RW, C * U), BF), wu_own=V((RW, C * U), BF),
         terms=V((TR, HD), F32), terms_z=V((S, TR, HD), F32), terms_sum=V((TR, HD), F32),
         terms_p=V((C, TR, HD), F32),
         ag_send=DMA((4, 2 * CH)), ag_recv=DMA((4, C)), rs_send=DMA((4, CH + 6)), r1_recv=DMA((4, CH)),
-        r2_recv=DMA((4, 6)), z_send=DMA((6, 2, S)), z_recv=DMA((6, S)), gz_send=DMA((5, S)),
-        gz_recv=DMA((5, 2)), gc_recv=DMA((5, 2)), gp_send=DMA((2, C)), gp_recv=DMA((2, C)), u_send=DMA((1, S)),
+        r2_recv=DMA((4, 6)), z_send=DMA((6, 2, S)), z_recv=DMA((6, S)), gz_send=DMA((6, S)),
+        gz_recv=DMA((6, 2)), gc_recv=DMA((6, 2)), gp_send=DMA((3, C)), gp_recv=DMA((3, C)), u_send=DMA((1, S)),
         u_recv=DMA((1,)), w_send=DMA((2,)), w_recv=DMA((2,)), m_send=DMA((1, S)), m_recv=DMA((1,)),
         gain_send=DMA((C + S,)), gain_recv=DMA((S,)), t_send=DMA((S + C,)), t_recv=DMA((S + C,)),
-        local_sem=DMA((6,)), out_sem=DMA((7,)),
+        local_sem=DMA((6,)), out_sem=DMA((8,)),
     )
     names = list(inputs) + list(outputs) + list(scratch)
 

time: 171 us -> 158 us (0.924)
  Pallas kernels: 168 us -> 154 us
    pallas_call x1, Pallas kernels: 165 us -> 151 us  [fused_layer(): pl.pallas_call(kernel, out_shape=[jax.ShapeDtypeStruct(*v) for v in outpu...]
where the time goes in v6:
time: 158 us; the launch traced here: 157 us
  Pallas kernels  154 us (97%)
    pallas_call x1, Pallas kernels, fused_layer(): pl.pallas_call(kernel, out_shape=[jax.ShapeDtypeStruct(*v) for v in outpu...  151 us

profile of v6, /device:TPU:9, one launch (start us, length us, event | category | flops | bytes accessed | tf_op | source)
XLA Modules:
  0.0 157.2 jit_solution(1010127887074567757)
XLA Ops:
  0.6 0.8 slice.3
  1.5 0.1 select_reduce_fusion
  1.6 0.0 copy-start
  1.6 0.0 copy-start.1
  1.6 0.0 copy-start.2
  1.6 0.0 copy-start.3
  1.6 0.6 pad_add_fusion.refs_0_
  2.2 0.0 copy-done
  2.2 0.0 copy-done.1
  2.2 0.0 copy-done.2
  2.3 0.0 copy-done.3
  2.3 0.7 fusion.9.refs_3_
  2.9 151.1 %layer.1 = (bf16[128,1024]{1,0:T(8,128)(2,1)}, f32[128,1024]{1,0:T(8,128)}, bf16[8,32,256]{2,1,0:T(8,128)(2,1)}, bf16[8,32,256]{2,1,0:T(8,128)(2,1)}, bf16[64,10...) custom-call(s32[2,16]{1,0:T(2,128)} %pad_add_fusion.refs_0_, ...), custom_call_target="tpu_custom_call" | custom-call | tf_op jit(solution)/shard_map/layer/pallas_call | solution.py:1069
  154.1 3.2 %finish.1 = (bf16[128,1024]{1,0:T(8,128)(2,1)}, f32[128,1024]{1,0:T(8,128)}, f32[1,32]{1,0:T(1,128)}, f32[32,2048]{1,0:T(8,128)}, f32[32,1024]{1,0:T(8,128)}, /*...) custom-call(bf16[128,1024]{1,0:T(8,128)(2,1)} %get-tuple-element.34., ...), custom_call_target="tpu_custom_call" | custom-call | tf_op jit(solution)/shard_map/finish/pallas_call | solution.py:1085
  (2 shorter events, 0.0 us)
Async XLA Ops:
  1.6 0.7 copy-start
  1.6 0.7 copy-start.1
  1.6 0.7 copy-start.2
  1.6 0.7 copy-start.3

commit v7 on v6

--- a/solution.py
+++ b/solution.py
@@ -70,7 +70,6 @@
     core = lax.rem(c, 2)
     chip_y, chip_x = lax.div(chip, 2), lax.rem(chip, 2)
     sibling = chip * 2 + (1 - core)
-    flat = s * C + c
     def partner(i):
         x = lax.rem(chip_x + lax.rem(i, 2), 2)
         y = lax.rem(chip_y + lax.div(i, 2), 2)
@@ -87,6 +86,9 @@
     def arrived(dst, sem):
         pltpu.make_async_copy(dst, dst, sem).wait()
 
+    def left(elements, sem):
+        arrived(r.h2_all.at[pl.ds(0, elements // D)], sem)
+
     barrier = pltpu.get_barrier_semaphore()
 
     def hello(**where):
@@ -117,9 +119,9 @@
 
     def gather_send(kind, src):
         for i in (1, 2):
-            remote(src, block(kind, c), r.ag_send.at[kind, i], r.ag_recv.at[kind, c],
+            remote(src, block(kind, c), r.ag_send.at[kind], r.ag_recv.at[kind, c],
                    ctx=partner(i) * 2 + core).start()
-        remote(src, block(kind, c), r.ag_send.at[kind, 0], r.ag_recv.at[kind, c], ctx=sibling).start()
+        remote(src, block(kind, c), r.ag_send.at[kind], r.ag_recv.at[kind, c], ctx=sibling).start()
 
     def gather_relay(kind, i):
         j = partner(i) * 2 + core
@@ -128,14 +130,14 @@
         @pl.when(i == 1)
         def _():
             part = half(block(kind, j), 0)
-            remote(part, part, r.ag_send.at[kind, 3], r.ag_recv.at[kind, j], ctx=partner(2) * 2 + core).start()
+            remote(part, part, r.ag_send.at[kind], r.ag_recv.at[kind, j], ctx=partner(2) * 2 + core).start()
 
         @pl.when(i == 2)
         def _():
             part = half(block(kind, j), 1)
-            remote(part, part, r.ag_send.at[kind, 7], r.ag_recv.at[kind, j], ctx=partner(1) * 2 + core).start()
-
-        remote(block(kind, j), block(kind, j), r.ag_send.at[kind, 3 + i], r.ag_recv.at[kind, j],
+            remote(part, part, r.ag_send.at[kind], r.ag_recv.at[kind, j], ctx=partner(1) * 2 + core).start()
+
+        remote(block(kind, j), block(kind, j), r.ag_send.at[kind], r.ag_recv.at[kind, j],
                ctx=sibling).start()
 
     def gather_other(kind, i):
@@ -143,15 +145,12 @@
         arrived(block(kind, j), r.ag_recv.at[kind, j])
 
     def gather_done(kind):
-        for i in (0, 1, 2, 4, 5, 6):
-            arrived(block(kind, c), r.ag_send.at[kind, i])
-        for i in (3, 7):
-            arrived(half(block(kind, c), 0), r.ag_send.at[kind, i])
+        left(7 * T * D, r.ag_send.at[kind])
 
     def scatter_pair(kind, i, partial):
         r.pair[i] = partial
         r.s1[i] = r.pair[i, rows_of((1 - core) * T, T), :].astype(BF)
-        remote(r.s1.at[i], r.r1.at[1 if kind == 1 else 0, i], r.rs_send.at[kind, i],
+        remote(r.s1.at[i], r.r1.at[1 if kind == 1 else 0, i], r.rs_send.at[kind],
                r.r1_recv.at[kind, i], ctx=sibling).start()
 
     def scatter_chip(kind, i):
@@ -161,7 +160,7 @@
         r.s2[i] = mine.astype(BF)
 
         def to(k, slot, send, recv):
-            remote(half(r.s2.at[i], k), half(r.r2.at[bank, slot], k), r.rs_send.at[kind, send],
+            remote(half(r.s2.at[i], k), half(r.r2.at[bank, slot], k), r.rs_send.at[kind],
                    r.r2_recv.at[kind, recv], ctx=partner(1 + k) * 2 + core).start()
 
         @pl.when(i == 1)
@@ -199,7 +198,7 @@
             arrived(half(r.r2.at[bank, 1], k), r.r2_recv.at[kind, 2 + k])
             mine = r.pair[i, rows_of(core * T, T), part] + r.r1[bank, i, :, part].astype(F32)
             r.s3[:, part] = (mine + r.r2[bank, 1, :, part].astype(F32)).astype(BF)
-            remote(half(r.s3, k), half(r.r2.at[bank, 2], k), r.rs_send.at[kind, CH + 4 + k],
+            remote(half(r.s3, k), half(r.r2.at[bank, 2], k), r.rs_send.at[kind],
                    r.r2_recv.at[kind, 4 + k], ctx=partner(i) * 2 + core).start()
 
     def scatter_sum(kind):
@@ -212,8 +211,7 @@
         return total + r.r2[bank, 0].astype(F32) + r.r2[bank, 2].astype(F32)
 
     def scatter_done(kind):
-        loop(0, CH, lambda i: arrived(r.s1.at[0], r.rs_send.at[kind, i]))
-        loop(CH, CH + 6, lambda i: arrived(half(r.s3, 0), r.rs_send.at[kind, i]))
+        left(7 * T * D, r.rs_send.at[kind])
 
     QKV, GATE, UP, OUT, DOWN, QKV2 = 0, 1, 2, 3, 4, 5
     PH = PR // 2
@@ -236,11 +234,11 @@
 
         @pl.when(s < S - 1)
         def _():
-            remote(src, plane(w, s), r.z_send.at[w, 0, 0], r.z_recv.at[w, s], seq=s + 1).start()
+            remote(src, plane(w, s), r.z_send.at[w], r.z_recv.at[w, s], seq=s + 1).start()
 
         @pl.when(s > 0)
         def _():
-            remote(src, plane(w, s), r.z_send.at[w, 1, 0], r.z_recv.at[w, s], seq=s - 1).start()
+            remote(src, plane(w, s), r.z_send.at[w], r.z_recv.at[w, s], seq=s - 1).start()
 
     rows_ref = {OUT: (0, r.w_o, OR)}
 
@@ -282,7 +280,7 @@
 
             @pl.when(s < S - 1)
             def _():
-                remote(plane(w, below), plane(w, below), r.z_send.at[w, 0, t + 1],
+                remote(plane(w, below), plane(w, below), r.z_send.at[w],
                        r.z_recv.at[w, below], seq=s + 1).start()
 
         @pl.when(above <= S - 1)
@@ -291,7 +289,7 @@
 
             @pl.when(s > 0)
             def _():
-                remote(plane(w, above), plane(w, above), r.z_send.at[w, 1, t + 1],
+                remote(plane(w, above), plane(w, above), r.z_send.at[w],
                        r.z_recv.at[w, above], seq=s - 1).start()
 
     inner = jnp.logical_and(s > 0, s < S - 1)
@@ -318,14 +316,15 @@
             deal(w, above)
 
     def weight_done(w):
-        for t in range(S - 1):
-            @pl.when(jnp.logical_and(s - t >= 0, s < S - 1))
-            def _():
-                arrived(plane(w, s), r.z_send.at[w, 0, t])
-
-            @pl.when(jnp.logical_and(s + t <= S - 1, s > 0))
-            def _():
-                arrived(plane(w, s), r.z_send.at[w, 1, t])
+        size = {QKV: PH * AC, QKV2: PH * AC, GATE: PR * U, UP: PR * U, OUT: OR * D, DOWN: DR * D}[w]
+
+        @pl.when(inner)
+        def _():
+            left((S + 1) * size, r.z_send.at[w])
+
+        @pl.when(jnp.logical_not(inner))
+        def _():
+            left(size, r.z_send.at[w])
 
     GU = GATE
     sent = {QKV: (r.g_q, PR), QKV2: (r.g_kv, PR), OUT: (r.h_o, OR), GU: (r.g_gu, PR), DOWN: (r.g_d, DR)}
@@ -342,7 +341,7 @@
         return jnp.where(s < 2, lax.rem(3 - i + s, S), lax.rem(i + (3 - s) * 3, S))
 
     def grad_direct(w, p):
-        remote(grad_rows(w, p), got[w].at[side], r.gz_send.at[w, p], r.gz_recv.at[w, side], seq=p).start()
+        remote(grad_rows(w, p), got[w].at[side], r.gz_send.at[w], r.gz_recv.at[w, side], seq=p).start()
 
     def grad_out(w, p):
         far_up = jnp.logical_and(s == 0, p >= 2)
@@ -353,12 +352,12 @@
 
         @pl.when(far_up)
         def _():
-            remote(grad_rows(w, p), halfway[w].at[p - 2], r.gz_send.at[w, p], r.gc_recv.at[w, p - 2],
+            remote(grad_rows(w, p), halfway[w].at[p - 2], r.gz_send.at[w], r.gc_recv.at[w, p - 2],
                    seq=1).start()
 
         @pl.when(far_down)
         def _():
-            remote(grad_rows(w, p), halfway[w].at[p], r.gz_send.at[w, p], r.gc_recv.at[w, p], seq=2).start()
+            remote(grad_rows(w, p), halfway[w].at[p], r.gz_send.at[w], r.gc_recv.at[w, p], seq=2).start()
 
         others = jnp.logical_or(jnp.logical_or(far_up, far_down), jnp.logical_or(later, p == s))
 
@@ -386,24 +385,25 @@
         summed[w][...] = total.astype(BF)
 
     def grad_done(w):
-        loop(1, S, lambda i: arrived(got[w].at[0], r.gz_send.at[w, lax.rem(s + i, S)]))
+        size = {QKV: PR * H * HD, QKV2: PR * 2 * HD, GU: 2 * PR * U, OUT: OR * D, DOWN: DR * D}[w]
+        left((S - 1) * size, r.gz_send.at[w])
 
     final = {QKV: r.f_q, QKV2: r.f_kv, GU: r.f_gu}
 
     def columns_send(n, w):
         def go(i):
             j = lax.rem(c + i, C)
-            remote(summed[w].at[rows_of(j * RW, RW)], final[w].at[c], r.gp_send.at[n, i],
-                   r.gp_recv.at[n, c], ctx=j).start()
+            remote(summed[w].at[rows_of(j * RW, RW)], final[w].at[c], r.gp_send.at[n],
+                   r.gp_recv.at[n], ctx=j).start()
 
         loop(1, C, go)
         final[w][c] = summed[w][rows_of(c * RW, RW), :]
 
     def columns_arrive(n, w):
-        loop(1, C, lambda i: arrived(final[w].at[lax.rem(c + i, C)], r.gp_recv.at[n, lax.rem(c + i, C)]))
+        arrived(final[w].at[pl.ds(0, C - 1)], r.gp_recv.at[n])
 
     def columns_done(n, w):
-        loop(1, C, lambda i: arrived(final[w].at[0], r.gp_send.at[n, i]))
+        arrived(final[w].at[pl.ds(0, C - 1)], r.gp_send.at[n])
 
     undealt = {OUT: (0, r.g_o, r.h_o, OR)}
 
@@ -439,12 +439,12 @@
 
         loop(0, S, go)
 
-    gains_own = r.gains_all.at[flat]
-    gain_copy = local(r.gains_in, gains_own, r.gain_recv.at[s])
+    gains_own = r.gains_all.at[c]
+    gain_copy = local(r.gains_in, gains_own, r.gain_recv.at[S])
     gain_copy.start()
 
     def gain_go(i):
-        remote(r.gains_in, gains_own, r.gain_send.at[i], r.gain_recv.at[s],
+        remote(r.gains_in, gains_own, r.gain_send.at[0], r.gain_recv.at[S],
                ctx=lax.rem(c + i, C)).start()
 
     loop(1, C, gain_go)
@@ -500,11 +500,12 @@
     spread_arrive(0, QKV)
     weight_start(QKV)
     weight_start(QKV2)
-    arrived(r.gains_all.at[pl.ds(s * C, C)], r.gain_recv.at[s])
+    arrived(r.gains_all, r.gain_recv.at[S])
+    r.gains_z[s] = jnp.sum(r.gains_all[...], axis=1)
 
     def gain_far(i):
-        mine = r.gains_all.at[pl.ds(s * C, C)]
-        remote(mine, mine, r.gain_send.at[C + i], r.gain_recv.at[s], seq=lax.rem(s + i, S)).start()
+        remote(r.gains_z.at[s], r.gains_z.at[s], r.gain_send.at[1], r.gain_recv.at[s],
+               seq=lax.rem(s + i, S)).start()
 
     loop(1, S, gain_far)
 
@@ -533,10 +534,10 @@
 
     def gain_block(i):
         p = lax.rem(s + i, S)
-        arrived(r.gains_all.at[pl.ds(p * C, C)], r.gain_recv.at[p])
+        arrived(r.gains_z.at[p], r.gain_recv.at[p])
 
     loop(1, S, gain_block)
-    gains = jnp.sum(r.gains_all[...], axis=1).astype(BF)
+    gains = r.gains_z[...].reshape(S * C, HD).astype(BF)
 
     def gain_vector(offset, count):
         width = count * S * C
@@ -868,9 +869,11 @@
     scatter(3, in_chip)
     grad_combine(OUT, 0)
     scatter_mid(3)
+    grad_combine(OUT, 1)
+    grad_combine(QKV, 0)
     grad_sum(GU)
     columns_send(1, GU)
-    grad_combine(OUT, 1)
+    grad_combine(QKV, 1)
     d_h1 = scatter_sum(3)
     x = own_x()
     r1 = inverse_root(x)
@@ -883,34 +886,31 @@
     r.terms[2 * WT : 2 * WT + 8, :] = r.sums[...]
 
     def terms_far(i):
-        remote(r.terms, r.terms_z.at[s], r.t_send.at[i], r.t_recv.at[s],
+        remote(r.terms, r.terms_z.at[s], r.t_send.at[0], r.t_recv.at[0],
                seq=lax.rem(s + i, S)).start()
 
     loop(1, S, terms_far)
     scatter_done(3)
-    grad_combine(QKV, 0)
+    grad_combine(QKV2, 0)
     grad_sum(DOWN)
     local(r.u_d, r.down_out, r.out_sem.at[2]).start()
-    grad_combine(QKV, 1)
+    grad_combine(QKV2, 1)
     grad_sum(OUT)
     local(r.u_o, r.o_out, r.out_sem.at[4]).start()
-    grad_combine(QKV2, 0)
     columns_arrive(1, GU)
     local(r.f_gu, r.gu_out, r.out_sem.at[3]).start()
-    grad_combine(QKV2, 1)
     grad_sum(QKV)
     columns_send(0, QKV)
     grad_sum(QKV2)
     columns_send(2, QKV2)
     total = r.terms[...]
+    arrived(r.terms_z.at[pl.ds(0, S - 1)], r.t_recv.at[0])
     for i in range(1, S):
-        p = lax.rem(s + i, S)
-        arrived(r.terms_z.at[p], r.t_recv.at[p])
-        total = total + r.terms_z[p]
+        total = total + r.terms_z[lax.rem(s + i, S)]
     r.terms_sum[...] = total
 
     def terms_near(i):
-        remote(r.terms_sum, r.terms_p.at[c], r.t_send.at[S + i], r.t_recv.at[S + c],
+        remote(r.terms_sum, r.terms_p.at[c], r.t_send.at[1], r.t_recv.at[1],
                ctx=lax.rem(c + i, C)).start()
 
     loop(1, C, terms_near)
@@ -918,17 +918,16 @@
     columns_arrive(0, QKV)
     local(r.f_q, r.q_out, r.out_sem.at[5]).start()
     total = r.terms_sum[...]
+    arrived(r.terms_p.at[pl.ds(0, C - 1)], r.t_recv.at[1])
     for i in range(1, C):
-        j = lax.rem(c + i, C)
-        arrived(r.terms_p.at[j], r.t_recv.at[S + j])
-        total = total + r.terms_p[j]
+        total = total + r.terms_p[lax.rem(c + i, C)]
     r.terms_all[...] = total
     local(r.terms_all, r.terms_out, r.out_sem.at[6]).start()
     columns_arrive(2, QKV2)
     local(r.f_kv, r.kv_out, r.out_sem.at[7]).start()
 
-    loop(1, C, lambda i: arrived(gains_own, r.gain_send.at[i]))
-    loop(1, S, lambda i: arrived(r.gains_all.at[pl.ds(0, C)], r.gain_send.at[C + i]))
+    arrived(r.gains_all.at[pl.ds(0, C - 1)], r.gain_send.at[0])
+    arrived(r.gains_z.at[pl.ds(0, S - 1)], r.gain_send.at[1])
     for kind in (X, G, H2, DY):
         gather_done(kind)
     spread_done(0, QKV)
@@ -942,8 +941,8 @@
     columns_done(0, QKV)
     columns_done(2, QKV2)
     columns_done(1, GU)
-    loop(1, S, lambda i: arrived(r.terms, r.t_send.at[i]))
-    loop(1, C, lambda i: arrived(r.terms, r.t_send.at[S + i]))
+    arrived(r.terms_z.at[pl.ds(0, S - 1)], r.t_send.at[0])
+    arrived(r.terms_p.at[pl.ds(0, C - 1)], r.t_send.at[1])
     pairs = (
         (r.y_out, r.layer_out), (r.x_grad, r.hidden_grad), (r.u_d, r.down_out), (r.f_gu, r.gu_out),
         (r.u_o, r.o_out), (r.f_q, r.q_out), (r.terms_all, r.terms_out), (r.f_kv, r.kv_out),
@@ -952,39 +951,69 @@
         local(src, dst, r.out_sem.at[k]).wait()
 
 
-def finish_kernel(dims, refs):
+def finish_kernel(dims, inputs, outputs, refs):
     S, C, D, H, U = dims.S, dims.C, dims.D, dims.H, dims.U
     HD = HEAD_DIMENSION
     r = refs
     me = lax.axis_index("seq") * C + lax.axis_index("ctx")
-    r.layer_res[...] = r.layer_out[...]
-    r.hidden_res[...] = r.hidden_grad[...]
-    r.delta_down[...] = r.down_out[...].astype(F32)
-    r.delta_out[...] = r.o_out[...].astype(F32)
+
+    def read(k):
+        return pltpu.make_async_copy(r.far_in[k], r.near_in[k], r.in_sem.at[k])
+
+    def write(src, k):
+        return pltpu.make_async_copy(src, r.far_out[k], r.out_sem.at[k])
+
+    source = dict(zip(inputs, r.near_in))
+    target = dict(zip(outputs, r.near_out))
+    i = types.SimpleNamespace(**source)
+    o = types.SimpleNamespace(**target)
+    for k in range(len(inputs)):
+        read(k).start()
+    read(0).wait()
+    write(i.layer_out, 0).start()
+    read(1).wait()
+    write(i.hidden_grad, 1).start()
+    read(2).wait()
     for j in range(C):
-        r.delta_query[:, j * H * HD : (j + 1) * H * HD] = r.q_out[j].astype(F32)
-        r.delta_key[:, j * HD : (j + 1) * HD] = r.kv_out[j, :, :HD].astype(F32)
-        r.delta_value[:, j * HD : (j + 1) * HD] = r.kv_out[j, :, HD:].astype(F32)
-
-    for k, ref in ((0, r.delta_gate), (1, r.delta_up)):
+        o.delta_query[:, j * H * HD : (j + 1) * H * HD] = i.q_out[j].astype(F32)
+    write(o.delta_query, 3).start()
+    read(3).wait()
+    for j in range(C):
+        o.delta_key[:, j * HD : (j + 1) * HD] = i.kv_out[j, :, :HD].astype(F32)
+        o.delta_value[:, j * HD : (j + 1) * HD] = i.kv_out[j, :, HD:].astype(F32)
+    write(o.delta_key, 4).start()
+    write(o.delta_value, 5).start()
+    read(4).wait()
+    o.delta_out[...] = i.o_out[...].astype(F32)
+    write(o.delta_out, 8).start()
+    read(5).wait()
+    for k, ref in ((0, o.delta_gate), (1, o.delta_up)):
         for d in range(0, S * C, 4):
             parts = []
             for e in range(d, d + 4):
                 first = k * U + (e // C) * dims.DR
-                parts.append(r.gu_out[e % C, :, first : first + dims.DR].astype(F32))
+                parts.append(i.gu_out[e % C, :, first : first + dims.DR].astype(F32))
             ref[:, d * dims.DR : (d + 4) * dims.DR] = jnp.concatenate(parts, axis=1)
-
-    def own(ref, first_row, count):
+        write(ref, 10 + k).start()
+    read(6).wait()
+    o.delta_down[...] = i.down_out[...].astype(F32)
+    write(o.delta_down, 12).start()
+    read(7).wait()
+
+    def own(ref, first_row, count, k):
         start = me * count
-        row = r.terms_out[pl.ds(first_row + lax.div(start, HD), 1), :]
+        row = i.terms_out[pl.ds(first_row + lax.div(start, HD), 1), :]
         back = lax.rem(HD - lax.rem(start, HD), HD)
         ref[...] = pltpu.roll(jnp.broadcast_to(row, (8, HD)), back, 1)[0:1, :count]
+        write(ref, k).start()
 
     n1, n3 = D // (S * C), HD // (S * C)
-    own(r.change1, 0, n1)
-    own(r.change2, D // HD, n1)
-    own(r.changeq, 2 * (D // HD), n3)
-    own(r.changek, 2 * (D // HD) + 1, n3)
+    own(o.change1, 0, n1, 2)
+    own(o.change2, D // HD, n1, 9)
+    own(o.changeq, 2 * (D // HD), n3, 6)
+    own(o.changek, 2 * (D // HD) + 1, n3, 7)
+    for k in range(len(outputs)):
+        write(i.layer_out if k == 0 else i.hidden_grad if k == 1 else r.near_out[k], k).wait()
 
 
 def fused_layer(mesh, args):
@@ -1031,7 +1060,7 @@
     scratch = dict(
         x_all=V((L // RUN, RUN, D), BF), g_all=V((L, D), BF), h2_all=V((L, D), BF), dy_all=V((L, D), BF),
         h1=V((L, D), BF), w_qkv=V((D, AC), BF), w_o=V((H * HD, D), BF), w_gu=V((D, 2 * U), BF),
-        w_d=V((U, D), BF), gains_all=V((S * C, 8, HD), F32), table=V((L, HD), F32),
+        w_d=V((U, D), BF), gains_all=V((C, 8, HD), F32), gains_z=V((S, C, HD), F32), table=V((L, HD), F32),
         cosine=V((L, HD), F32), sine=V((L, HD), F32), gain1=V((1, D), F32), gain2=V((1, D), F32),
         gainq=V((1, HD), F32), gaink=V((1, HD), F32), q_lin=V((H, L, HD), F32), k_lin=V((L, HD), F32),
         q_rot=V((H, L, HD), BF), k_rot=V((L, HD), BF), v=V((L, HD), BF), k_t=V((HD, L), BF),
@@ -1051,11 +1080,11 @@
         wg_own=V((RW, C * U), BF), wu_own=V((RW, C * U), BF),
         terms=V((TR, HD), F32), terms_z=V((S, TR, HD), F32), terms_sum=V((TR, HD), F32),
         terms_p=V((C, TR, HD), F32),
-        ag_send=DMA((4, 2 * CH)), ag_recv=DMA((4, C)), rs_send=DMA((4, CH + 6)), r1_recv=DMA((4, CH)),
-        r2_recv=DMA((4, 6)), z_send=DMA((6, 2, S)), z_recv=DMA((6, S)), gz_send=DMA((6, S)),
-        gz_recv=DMA((6, 2)), gc_recv=DMA((6, 2)), gp_send=DMA((3, C)), gp_recv=DMA((3, C)), u_send=DMA((1, S)),
+        ag_send=DMA((4,)), ag_recv=DMA((4, C)), rs_send=DMA((4,)), r1_recv=DMA((4, CH)),
+        r2_recv=DMA((4, 6)), z_send=DMA((6,)), z_recv=DMA((6, S)), gz_send=DMA((6,)),
+        gz_recv=DMA((6, 2)), gc_recv=DMA((6, 2)), gp_send=DMA((3,)), gp_recv=DMA((3,)), u_send=DMA((1, S)),
         u_recv=DMA((1,)), w_send=DMA((2,)), w_recv=DMA((2,)), m_send=DMA((1, S)), m_recv=DMA((1,)),
-        gain_send=DMA((C + S,)), gain_recv=DMA((S,)), t_send=DMA((S + C,)), t_recv=DMA((S + C,)),
+        gain_send=DMA((2,)), gain_recv=DMA((S + 1,)), t_send=DMA((2,)), t_recv=DMA((2,)),
         local_sem=DMA((6,)), out_sem=DMA((8,)),
     )
     names = list(inputs) + list(outputs) + list(scratch)
@@ -1077,16 +1106,24 @@
         ),
         name="layer",
     )(*inputs.values())
-    finish_names = list(outputs) + list(final)
+    n_in, n_out = len(outputs), len(final)
 
     def finish(*refs):
-        finish_kernel(dims, types.SimpleNamespace(**dict(zip(finish_names, refs))))
+        parts = types.SimpleNamespace(
+            far_in=refs[:n_in], far_out=refs[n_in : n_in + n_out],
+            near_in=refs[n_in + n_out : 2 * n_in + n_out], near_out=refs[2 * n_in + n_out : -2],
+            in_sem=refs[-2], out_sem=refs[-1],
+        )
+        finish_kernel(dims, list(outputs), list(final), parts)
 
     out = pl.pallas_call(
         finish,
         out_shape=[jax.ShapeDtypeStruct(*v) for v in final.values()],
-        in_specs=[pl.BlockSpec(memory_space=pltpu.VMEM)] * len(outputs),
-        out_specs=[pl.BlockSpec(memory_space=pltpu.VMEM)] * len(final),
+        in_specs=[pl.BlockSpec(memory_space=pl.ANY)] * n_in,
+        out_specs=[pl.BlockSpec(memory_space=pl.ANY)] * n_out,
+        scratch_shapes=[V(*v) for v in outputs.values()]
+        + [V((8, HD), F32) if k < 2 else V(*v) for k, v in enumerate(final.values())]
+        + [DMA((n_in,)), DMA((n_out,))],
         name="finish",
     )(*results)
     one_axis = [k for k, v in enumerate(final.values()) if v[0][0] == 1]

time: 158 us -> 153 us (0.968)
  Pallas kernels: 154 us -> 149 us
    pallas_call x1, Pallas kernels: 151 us -> 147 us  [fused_layer(): pl.pallas_call(kernel, out_shape=[jax.ShapeDtypeStruct(*v) for v in outpu...]
where the time goes in v7:
time: 153 us; the launch traced here: 152 us
  Pallas kernels  149 us (97%)
    pallas_call x1, Pallas kernels, fused_layer(): pl.pallas_call(kernel, out_shape=[jax.ShapeDtypeStruct(*v) for v in outpu...  147 us

profile of v7, /device:TPU:9, one launch (start us, length us, event | category | flops | bytes accessed | tf_op | source)
XLA Modules:
  0.0 152.4 jit_solution(12047265014233436700)
XLA Ops:
  0.6 0.8 slice.3
  1.5 0.1 select_reduce_fusion
  1.6 0.0 copy-start
  1.6 0.0 copy-start.1
  1.6 0.0 copy-start.2
  1.6 0.0 copy-start.3
  1.6 0.6 pad_add_fusion.refs_0_
  2.2 0.0 copy-done
  2.2 0.0 copy-done.1
  2.2 0.0 copy-done.2
  2.3 0.0 copy-done.3
  2.3 0.7 fusion.9.refs_3_
  2.9 146.7 %layer.1 = (bf16[128,1024]{1,0:T(8,128)(2,1)}, f32[128,1024]{1,0:T(8,128)}, bf16[8,32,256]{2,1,0:T(8,128)(2,1)}, bf16[8,32,256]{2,1,0:T(8,128)(2,1)}, bf16[64,10...) custom-call(s32[2,16]{1,0:T(2,128)} %pad_add_fusion.refs_0_, ...), custom_call_target="tpu_custom_call" | custom-call | tf_op jit(solution)/shard_map/layer/pallas_call | solution.py:1098
  149.7 2.8 %finish.1 = (bf16[128,1024]{1,0:T(8,128)(2,1)}, f32[128,1024]{1,0:T(8,128)}, f32[1,32]{1,0:T(1,128)}, f32[32,2048]{1,0:T(8,128)}, f32[32,1024]{1,0:T(8,128)}, /*...) custom-call(bf16[128,1024]{1,0:T(8,128)(2,1)} %get-tuple-element.34., ...), custom_call_target="tpu_custom_call" | custom-call | tf_op jit(solution)/shard_map/finish/pallas_call | solution.py:1119
  (2 shorter events, 0.0 us)
Async XLA Ops:
  1.6 0.7 copy-start
  1.6 0.7 copy-start.1
  1.6 0.7 copy-start.2
  1.6 0.7 copy-start.3
